TPU v7x, 128 devices: a whole 4x4x4 slice. The times are simulated.
128 devices in a mesh: cuts: 32 (over x_hi, y, z), event: 4 (over x_lo, core).
Axes of the slice: x: 4 (x_hi: 2, x_lo: 2; x = x_hi * 2 + x_lo), y: 4, z: 4, core: 2. Of those that a mesh axis runs over, the one named last changes fastest.
Arguments:
- kernels: float32 [4, 256, 128, 256], P('event', 'cuts'), may hold values from -24 to 24
- steps: float32 [8, 256, 128, 256], P(None, 'cuts', 'event'), may hold values from -11 to 11
- curvature: float32 [8, 256, 128, 256], P(None, 'cuts', 'event'), may hold values from 0.2 to 5
Outputs:
- gradient: float32 [256, 128, 256], P('cuts', 'event')
- direction: float32 [256, 128, 256], P('cuts', 'event')
All inputs are finite; a program needn't handle non-finite values.
Results may differ from a plain program's by a relative error of at most 0.00021.
Values sent between devices are 32-bit elements; how exact they have to be, the bound alone decides.
No kernel may reach another device: no remote copies, remote signals or barrier semaphores. Data moves between devices by JAX's collectives and lax.ppermute only.
A program may use at most 64 MiB of HBM per device.

v0:
```python
import functools
import math

import jax
import jax.numpy as jnp
from jax import lax
from jax.sharding import Mesh
from jax.sharding import PartitionSpec as P

PAIRS = 8
RIM = 4
CUTS = ("cuts_0", "cuts_1", "cuts_2")
EVENT = ("event_0", "event_1")
CUTS_EVENT = ("cuts_0", "cuts_1", "cuts_2", "event_0", "event_1")


def with_halo(cells, sides, width):
    for axis, dim in sides:
        count = lax.axis_size(axis)
        head = lax.slice_in_dim(cells, 0, width, axis=dim)
        tail = lax.slice_in_dim(cells, cells.shape[dim] - width, cells.shape[dim], axis=dim)
        cells = jnp.concatenate(
            [
                lax.ppermute(tail, axis, [(i, (i + 1) % count) for i in range(count)]),
                cells,
                lax.ppermute(head, axis, [((i + 1) % count, i) for i in range(count)]),
            ],
            axis=dim,
        )
    return cells


def split_up(x, dim, length):
    before, after = (x.shape[:dim], x.shape[dim + 1 :])
    return jnp.moveaxis(x.reshape(*before, length, -1, *after), dim, 0)


def sent_and_summed(x, axis, dim):
    blocks = split_up(x, dim, lax.axis_size(axis))
    arrived = lax.all_to_all(blocks, axis, split_axis=0, concat_axis=0, tiled=True)
    return arrived.sum(axis=0)


def one_axis_at_a_time(x, axes):
    return functools.reduce(lax.psum, axes, x)


def gauss_matrix(length, sigma):
    points = jnp.arange(length, dtype=jnp.float32)
    offset = points[:, None] - points[None, :]
    matrix = jnp.exp(-offset * offset / (2.0 * sigma * sigma))
    return matrix / jnp.sum(matrix, axis=1, keepdims=True)


def cycle_weights():
    unscaled = [math.exp(-((column - RIM) ** 2) / 4.5) for column in range(2 * RIM + 1)]
    whole = sum(unscaled)
    return [weight / whole for weight in unscaled]


def smooth_plane(field):
    lat_len = field.shape[2]
    plane = jnp.dot(
        field.reshape(-1, lat_len), gauss_matrix(lat_len, 4.0).T, precision=lax.Precision.HIGHEST
    ).reshape(field.shape)
    padded = with_halo(plane, ((CUTS, 0),), RIM)
    lon_len = plane.shape[0]
    weights = cycle_weights()
    smoothed = jnp.zeros_like(plane)
    for column in range(2 * RIM + 1):
        smoothed = smoothed + weights[column] * padded[column : column + lon_len]
    return smoothed


def shards(kernels, steps, curvature):
    partial_value = kernels[0]
    rad_len = partial_value.shape[1]
    radial = jnp.einsum(
        "ij,ajb->aib", gauss_matrix(rad_len, 3.0), partial_value, precision=lax.Precision.HIGHEST
    )
    summed = sent_and_summed(radial, EVENT, 1)
    gradient = smooth_plane(summed)
    changes = curvature * steps
    vectors = jnp.concatenate(
        [steps.reshape(PAIRS, -1), changes.reshape(PAIRS, -1), gradient.reshape(1, -1)], axis=0
    )
    products = one_axis_at_a_time(
        jnp.dot(vectors, vectors.T, precision=lax.Precision.HIGHEST), CUTS_EVENT
    )
    curvs = jnp.diagonal(products[:PAIRS, PAIRS : 2 * PAIRS])
    inverse = 1.0 / curvs
    scaling = curvs[PAIRS - 1] / products[2 * PAIRS - 1, 2 * PAIRS - 1]
    weights_now = jnp.zeros((2 * PAIRS + 1,), jnp.float32).at[2 * PAIRS].set(1.0)
    alphas = [None] * PAIRS
    for pair in reversed(range(PAIRS)):
        alphas[pair] = inverse[pair] * jnp.dot(
            products[pair], weights_now, precision=lax.Precision.HIGHEST
        )
        weights_now = weights_now.at[PAIRS + pair].add(-alphas[pair])
    weights_now = scaling * weights_now
    for pair in range(PAIRS):
        second = inverse[pair] * jnp.dot(
            products[PAIRS + pair], weights_now, precision=lax.Precision.HIGHEST
        )
        weights_now = weights_now.at[pair].add(alphas[pair] - second)
    direction = -jnp.dot(weights_now[None, :], vectors, precision=lax.Precision.HIGHEST).reshape(
        gradient.shape
    )
    return (gradient, direction)


def solution(mesh):
    torus = Mesh(
        mesh.devices.reshape(2, 4, 4, 2, 2), ("cuts_0", "cuts_1", "cuts_2", "event_0", "event_1")
    )
    in_specs = (P(EVENT, CUTS, None, None), P(None, CUTS, EVENT, None), P(None, CUTS, EVENT, None))
    out_specs = (P(CUTS, EVENT, None), P(CUTS, EVENT, None))
    return jax.shard_map(
        shards, mesh=torus, in_specs=in_specs, out_specs=out_specs, check_vma=False
    )
```

profile of v0, /device:TPU:1, one launch (start us, length us, event | category | flops | bytes accessed | tf_op | source)
XLA Modules:
  0.0 167.0 jit_solution(4872941888128251538)
XLA Ops:
  0.7 0.1 fusion.39
  0.8 1.1 copy-done
  1.9 1.1 fusion.2
  2.9 1.1 copy.49
  4.0 5.6 %all-to-all-start = ((f32[4,8,32,256]{3,2,1,0:T(8,128)}), f32[4,8,32,256]{3,2,1,0:T(8,128)}, u32[]{:S(2)}, u32[]{:S(2)}) async-start(f32[4,8,32,256]{3,2,1,0:T(8,128)} %bitcast.171), calls=%async_computation | async-start | bytes 2097152 | tf_op jit(solution)/shard_map/all_to_all | solution.py:40
  9.6 1.2 copy.42
  10.8 1.5 constant_dynamic-update-slice_fusion.1
  12.3 0.4 mul.109
  12.8 1.2 copy.43
  14.0 0.2 fusion.31
  14.2 9.0 %all-to-all-done = f32[4,8,32,256]{3,2,1,0:T(8,128)} async-done(((f32[4,8,32,256]{3,2,1,0:T(8,128)}), f32[4,8,32,256]{3,2,1,0:T(8,128)}, u32[]{:S(2)}, u32[]{:S(2)}) %all-to-all-start) | async-done | bytes 1048608 | tf_op jit(solution)/shard_map/all_to_all | solution.py:40
  23.2 1.3 reduce_sum.28
  24.5 0.5 fusion.28
  25.0 1.8 %collective-permute-start = (f32[4,32,256]{2,1,0:T(8,128)S(1)}, f32[4,32,256]{2,1,0:T(8,128)S(1)}, u32[]{:S(2)}, u32[]{:S(2)}) collective-permute-start(f32[4,32,256]{2,1,0:T(8,128)S(1)} %bitcast.175), channel_id=1, source_target_pairs={{0,4},{4,8},{8,12},{12,16},{16,20},{20,24},{24,28},{28,32},{32,36}... | collective-permute-start | bytes 393224 | tf_op jit(solution)/shard_map/ppermute | solution.py:24
  26.8 7.1 %collective-permute-start.1 = (f32[4,32,256]{2,1,0:T(8,128)S(1)}, f32[4,32,256]{2,1,0:T(8,128)S(1)}, u32[]{:S(2)}, u32[]{:S(2)}) collective-permute-start(f32[4,32,256]{2,1,0:T(8,128)S(1)} %bitcast.174), channel_id=1, source_target_pairs={{4,0},{8,4},{12,8},{16,12},{20,16},{24,20},{28,24},{32,28},{36,32}... | collective-permute-start | bytes 393224 | tf_op jit(solution)/shard_map/ppermute | solution.py:26
  34.0 1.4 constant_dynamic-update-slice_fusion
  35.4 1.4 collective-permute-done
  36.8 0.1 fusion.9
  36.9 0.3 reshape.416
  37.2 6.0 %dynamic-update-slice.38 = f32[17,65536]{1,0:T(8,128)} dynamic-update-slice(f32[17,65536]{1,0:T(8,128)} %constant_dynamic-update-slice_fusion, f32[1,65536]{1,0:T(1,128)S(1)} %reshape.416, s32[]{} %constant.458, s32[]{} %constant.456) | dynamic-update-slice | bytes 524292 | tf_op jit(solution)/shard_map/concatenate | solution.py:84
  43.2 8.9 %fusion.79 = f32[17,17]{1,0:T(8,128)S(1)} fusion(f32[17,65536]{1,0:T(8,128)} %dynamic-update-slice.38), kind=kOutput, calls=%fused_computation.133 | convolution fusion | flops 227278848 | bytes 4457604 | tf_op jit(solution)/shard_map/dot_general | solution.py:88
  52.1 7.5 %psum.35 = f32[17,17]{1,0:T(8,128)S(1)} all-reduce(f32[17,17]{1,0:T(8,128)S(1)} %fusion.79), channel_id=1, replica_groups=mesh['cuts_0'=2,'cuts_1'=4,'cuts_2'=4,'event_0'=2,'event_1'=2] {'cuts_0'}, use_global_device_ids=true, to_apply=%region_3.0 | all-reduce | flops 289 | bytes 2312 | tf_op jit(solution)/shard_map/psum | solution.py:45
  59.6 10.8 %psum.36 = f32[17,17]{1,0:T(8,128)S(1)} all-reduce(f32[17,17]{1,0:T(8,128)S(1)} %psum.35), channel_id=1, replica_groups=mesh['cuts_0'=2,'cuts_1'=4,'cuts_2'=4,'event_0'=2,'event_1'=2] {'cuts_1'}, use_global_device_ids=true, to_apply=%region_4.0 | all-reduce | flops 289 | bytes 2312 | tf_op jit(solution)/shard_map/psum | solution.py:45
  70.5 16.5 %psum.37 = f32[17,17]{1,0:T(8,128)S(1)} all-reduce(f32[17,17]{1,0:T(8,128)S(1)} %psum.36), channel_id=1, replica_groups=mesh['cuts_0'=2,'cuts_1'=4,'cuts_2'=4,'event_0'=2,'event_1'=2] {'cuts_2'}, use_global_device_ids=true, to_apply=%region_5.0 | all-reduce | flops 289 | bytes 2312 | tf_op jit(solution)/shard_map/psum | solution.py:45
  86.9 5.9 %psum.38 = f32[17,17]{1,0:T(8,128)S(1)} all-reduce(f32[17,17]{1,0:T(8,128)S(1)} %psum.37), channel_id=1, replica_groups=mesh['cuts_0'=2,'cuts_1'=4,'cuts_2'=4,'event_0'=2,'event_1'=2] {'event_0'}, use_global_device_ids=true, to_apply=%region_6.0 | all-reduce | flops 289 | bytes 2312 | tf_op jit(solution)/shard_map/psum | solution.py:45
  92.8 16.1 %psum.39 = f32[17,17]{1,0:T(8,128)S(1)} all-reduce(f32[17,17]{1,0:T(8,128)S(1)} %psum.38), channel_id=1, replica_groups=mesh['cuts_0'=2,'cuts_1'=4,'cuts_2'=4,'event_0'=2,'event_1'=2] {'event_1'}, use_global_device_ids=true, to_apply=%region_7.0 | all-reduce | flops 289 | bytes 2312 | tf_op jit(solution)/shard_map/psum | solution.py:45
  108.9 0.6 gather_fusion
  109.6 0.6 slice.344
  110.1 0.6 slice.402
  110.7 0.7 fusion.78
  111.4 0.6 fusion.73
  113.3 1.3 fusion.71
  115.9 0.2 constant_dynamic-update-slice_fusion.13
  116.0 1.3 fusion.69
  118.6 0.2 constant_dynamic-update-slice_fusion.12
  118.8 1.3 fusion.67
  121.4 0.2 constant_dynamic-update-slice_fusion.11
  121.5 1.3 fusion.65
  124.0 0.2 constant_dynamic-update-slice_fusion.10
  124.2 1.3 fusion.63
  126.8 0.2 constant_dynamic-update-slice_fusion.9
  127.0 1.3 fusion.61
  129.6 0.2 constant_dynamic-update-slice_fusion.8
  129.7 1.3 fusion.59
  132.3 0.2 constant_dynamic-update-slice_fusion.7
  133.7 1.3 fusion.57
  136.2 1.3 fusion.55
  138.7 0.2 constant_dynamic-update-slice_fusion.6
  138.9 1.4 fusion.53
  141.6 0.2 constant_dynamic-update-slice_fusion.5
  141.7 1.4 fusion.51
  144.3 0.2 add_dynamic-update-slice_fusion.1
  144.5 1.3 fusion.49
  147.0 0.2 constant_dynamic-update-slice_fusion.4
  147.1 1.3 fusion.47
  149.7 0.2 constant_dynamic-update-slice_fusion.3
  149.9 1.4 fusion.45
  152.5 0.2 constant_dynamic-update-slice_fusion.2
  152.7 1.3 fusion.43
  155.2 0.2 add_dynamic-update-slice_fusion
  155.4 4.8 %copy.44 = f32[3,8,256,256]{3,2,1,0:T(8,128)S(1)} copy(f32[3,8,256,256]{3,1,2,0:T(8,128)} %bitcast.163) | data formatting | bytes 12582912
  160.2 0.4 slice.419
  160.6 5.6 %fusion = f32[1,8,32,256]{3,0,2,1:T(1,128)S(1)} fusion(f32[8,32,256,17]{2,1,0,3:T(8,128)S(1)} %bitcast.164, f32[17]{0:T(128)S(1)} %add_dynamic-update-slice_fusion), kind=kOutput, calls=%fused_computation.1 | convolution fusion | flops 13369344 | bytes 4718660 | tf_op jit(solution)/shard_map/dot_general | solution.py:106
  166.2 0.7 bitcast_negate_fusion
  (19 shorter events, 0.2 us)
Async XLA Ops:
  0.6 1.2 copy-start
  0.6 9.0 %copy-start.1 = (f32[8,8,32,256]{3,2,1,0:T(8,128)S(1)}, f32[8,8,32,256]{3,2,1,0:T(8,128)}, u32[]{:S(2)}) copy-start(f32[8,8,32,256]{3,2,1,0:T(8,128)} %param.38) | copy-start | bytes 6291460
  4.0 19.2 %all-to-all-start = ((f32[4,8,32,256]{3,2,1,0:T(8,128)}), f32[4,8,32,256]{3,2,1,0:T(8,128)}, u32[]{:S(2)}, u32[]{:S(2)}) async-start(f32[4,8,32,256]{3,2,1,0:T(8,128)} %bitcast.171), calls=%async_computation | async-start | bytes 2097152 | tf_op jit(solution)/shard_map/all_to_all | solution.py:40
  9.6 2.7 %copy-start.2 = (f32[8,8,32,256]{3,2,1,0:T(8,128)S(1)}, f32[8,8,32,256]{3,2,1,0:T(8,128)}, u32[]{:S(2)}) copy-start(f32[8,8,32,256]{3,2,1,0:T(8,128)} %param.39) | copy-start | bytes 6291460
  12.7 22.6 %copy-start.5 = (f32[17]{0:T(128)S(1)}, f32[17]{0:T(128)}, u32[]{:S(2)}) copy-start(f32[17]{0:T(128)} %constant.406.clone.1) | copy-start | bytes 208
  25.0 11.8 %collective-permute-start = (f32[4,32,256]{2,1,0:T(8,128)S(1)}, f32[4,32,256]{2,1,0:T(8,128)S(1)}, u32[]{:S(2)}, u32[]{:S(2)}) collective-permute-start(f32[4,32,256]{2,1,0:T(8,128)S(1)} %bitcast.175), channel_id=1, source_target_pairs={{0,4},{4,8},{8,12},{12,16},{16,20},{20,24},{24,28},{28,32},{32,36}... | collective-permute-start | bytes 393224 | tf_op jit(solution)/shard_map/ppermute | solution.py:24
  26.8 9.9 %collective-permute-start.1 = (f32[4,32,256]{2,1,0:T(8,128)S(1)}, f32[4,32,256]{2,1,0:T(8,128)S(1)}, u32[]{:S(2)}, u32[]{:S(2)}) collective-permute-start(f32[4,32,256]{2,1,0:T(8,128)S(1)} %bitcast.174), channel_id=1, source_target_pairs={{4,0},{8,4},{12,8},{16,12},{20,16},{24,20},{28,24},{32,28},{36,32}... | collective-permute-start | bytes 393224 | tf_op jit(solution)/shard_map/ppermute | solution.py:26
  36.9 15.2 %copy-start.3 = (f32[8,32,256]{2,1,0:T(8,128)}, f32[8,32,256]{2,1,0:T(8,128)S(1)}, u32[]{:S(2)}) copy-start(f32[8,32,256]{2,1,0:T(8,128)S(1)} %fusion.9) | copy-start | bytes 786436
  108.9 4.4 %copy-start.4 = (f32[17,17]{1,0:T(8,128)}, f32[17,17]{1,0:T(8,128)S(1)}, u32[]{:S(2)}) copy-start(f32[17,17]{1,0:T(8,128)S(1)} %psum.39) | copy-start | bytes 3472
where the time goes:
time: 168 us; the launch traced here: 167 us
  blocking collectives  56.8 us (34%)
  other arithmetic  25.5 us (15%)
  between operations  22.1 us (13%)
  local copies, waits for them, and re-layouts  21.7 us (13%)
  matrix products  16 us (10%)
  starting transfers between devices  14.5 us (9%)
  waiting for transfers between devices  10.4 us (6%)
    psum x5, blocking collectives, one_axis_at_a_time(): return functools.reduce(lax.psum, axes, x)  56.8 us
    unnamed x19, local copies, waits for them, and re-layouts  11.7 us
    dot_general x8, other arithmetic, shards(): jnp.dot(products[PAIRS + pair], weights_now, precision=lax.Precision.HIGH...  10.6 us
    dot_general x8, other arithmetic, shards(): jnp.dot(products[pair], weights_now, precision=lax.Precision.HIGHEST)  9.84 us
    all_to_all x1, waiting for transfers between devices, sent_and_summed(): lax.all_to_all(blocks, axis, split_axis=0, concat_axis=0, tiled=True)  9.01 us
    dot_general x1, matrix products, shards(): jnp.dot(vectors, vectors.T, precision=lax.Precision.HIGHEST)  8.85 us
    ppermute x1, starting transfers between devices, with_halo(): lax.ppermute(head, axis, [((i + 1) % count, i) for i in range(count)])  7.11 us
    concatenate x1, local copies, waits for them, and re-layouts, shards(): jnp.concatenate([steps.reshape(PAIRS, -1), changes.reshape(PAIRS, -1), gr...  6.03 us
  transfers between devices with their start and end apart: 3, of which 2 were waited for; matrix products, arithmetic and copies ran while one was open for 4% of the time, Pallas kernels for 0%

commit v1 on v0

v1 whole, which is shorter than its diff:
```python
import functools
import math

import jax
import jax.numpy as jnp
import numpy as np
from jax import lax
from jax.experimental import pallas as pl
from jax.experimental.pallas import tpu as pltpu
from jax.sharding import Mesh
from jax.sharding import PartitionSpec as P

PAIRS = 8
RIM = 4
CUTS = ("cuts_0", "cuts_1", "cuts_2")
EVENT = ("event_0", "event_1")
CUTS_EVENT = ("cuts_0", "cuts_1", "cuts_2", "event_0", "event_1")
LANES = 128
SQUARES, STEPS_GRADIENT, CHANGES_GRADIENT = 64, 100, 108


def square_lane(i, j):
    low, high = min(i, j), max(i, j)
    return SQUARES + low * PAIRS - low * (low - 1) // 2 + high - low


def gauss_matrix(length, sigma):
    points = np.arange(length, dtype=np.float64)
    offset = points[:, None] - points[None, :]
    matrix = np.exp(-offset * offset / (2.0 * sigma * sigma))
    return (matrix / matrix.sum(axis=1, keepdims=True)).astype(np.float32)


def halves(matrix):
    high = matrix.astype(jnp.bfloat16)
    low = (matrix - high.astype(np.float32)).astype(jnp.bfloat16)
    return high, low


def cycle_weights():
    unscaled = [math.exp(-((column - RIM) ** 2) / 4.5) for column in range(2 * RIM + 1)]
    whole = sum(unscaled)
    return [weight / whole for weight in unscaled]


def split(x):
    high = x.astype(jnp.bfloat16)
    low = (x - high.astype(jnp.float32)).astype(jnp.bfloat16)
    return high, low


def dot(a, b):
    return jnp.dot(a, b, preferred_element_type=jnp.float32)


def call(kernel, outs, flops, moved, limit=16):
    return pl.pallas_call(
        kernel,
        out_shape=[jax.ShapeDtypeStruct(shape, jnp.float32) for shape in outs],
        compiler_params=pltpu.CompilerParams(vmem_limit_bytes=limit << 20),
        cost_estimate=pl.CostEstimate(flops=flops, bytes_accessed=moved, transcendentals=0),
    )


def radial_kernel(kernels_ref, high_ref, low_ref, keep_ref, pass_ref, send_ref):
    part = 2 * lax.axis_index("event_0") + lax.axis_index("event_1")
    rows = kernels_ref.shape[2] // 4
    order = [part, part ^ 2, part ^ 1, part ^ 3]
    starts = [pl.multiple_of(block * rows, rows) for block in order]
    weights = jnp.concatenate(
        [ref[pl.ds(start, rows), :] for ref in (high_ref, low_ref) for start in starts], axis=0
    )
    for a in range(kernels_ref.shape[1]):
        both = dot(weights, jnp.concatenate(split(kernels_ref[0, a]), axis=0))
        out = both[: 4 * rows] + both[4 * rows :]
        keep_ref[a] = out[:rows]
        pass_ref[a] = out[rows : 2 * rows]
        send_ref[0, a] = out[2 * rows : 3 * rows]
        send_ref[1, a] = out[3 * rows :]


def latitude_kernel(keep_ref, near_ref, far_ref, high_ref, low_ref, head_ref, tail_ref):
    lons, rows, lats = keep_ref.shape
    summed = (keep_ref[...] + near_ref[0] + far_ref[...]).reshape(lons * rows, lats)
    both = jnp.concatenate(split(summed), axis=0)
    out = dot(both, high_ref[...]) + dot(both, low_ref[...])
    plane = (out[: lons * rows] + out[lons * rows :]).reshape(lons, rows, lats)
    head_ref[...] = plane[:RIM]
    tail_ref[...] = plane[lons - RIM :]


def lane_numbers():
    return lax.broadcasted_iota(jnp.int32, (8, LANES), 1)


def tiles(shape):
    return [
        (a, slice(8 * r, 8 * r + 8), slice(LANES * b, LANES * (b + 1)))
        for r in range(shape[1] // 8)
        for b in range(shape[2] // LANES)
        for a in range(shape[0])
    ]


def placed(sums):
    lanes = lane_numbers()
    row = jnp.zeros((8, LANES), jnp.float32)
    for lane, value in sums:
        row = row + jnp.where(lanes == lane, jnp.sum(value, axis=1, keepdims=True), 0.0)
    return row


def gram_kernel(steps_ref, curvature_ref, changes_ref, row_ref):
    lons, rows, lats = steps_ref.shape[1:]
    zero = jnp.zeros((8, LANES), jnp.float32)

    def tile(ref, pair, t):
        r = t // (lats // LANES) % (rows // 8)
        b = t % (lats // LANES)
        a = t // (lats // LANES * (rows // 8))
        return (pair, a, pl.ds(pl.multiple_of(r * 8, 8), 8), pl.ds(pl.multiple_of(b * LANES, LANES), LANES))

    count = lons * (rows // 8) * (lats // LANES)

    def first(t, sums):
        steps = [steps_ref[tile(None, i, t)] for i in range(PAIRS)]
        changes = [curvature_ref[tile(None, i, t)] * steps[i] for i in range(PAIRS)]
        for i in range(PAIRS):
            changes_ref[tile(None, i, t)] = changes[i]
        return [sums[i * PAIRS + j] + steps[i] * changes[j] for i in range(4) for j in range(PAIRS)]

    def second(t, sums):
        steps = [steps_ref[tile(None, i, t)] for i in range(4, PAIRS)]
        changes = [changes_ref[tile(None, i, t)] for i in range(PAIRS)]
        return [sums[i * PAIRS + j] + steps[i] * changes[j] for i in range(4) for j in range(PAIRS)]

    upper = [(i, j) for i in range(PAIRS) for j in range(i, PAIRS)]

    def third(t, sums):
        changes = [changes_ref[tile(None, i, t)] for i in range(PAIRS)]
        return [value + changes[i] * changes[j] for value, (i, j) in zip(sums, upper)]

    row = zero
    for number, step, size in ((0, first, 32), (1, second, 32), (2, third, len(upper))):
        sums = lax.fori_loop(0, count, step, [zero] * size)
        row = row + placed([(32 * number + k, value) for k, value in enumerate(sums)])
    row_ref[...] = row


def product_kernel(head_ref, tail_ref, left_ref, right_ref, steps_ref, changes_ref, gram_ref, gradient_ref, rows_ref):
    lons, rows, lats = gradient_ref.shape
    weights = cycle_weights()
    sums = [jnp.zeros((8, LANES), jnp.float32) for _ in range(2 * PAIRS)]
    for r in range(rows // 8):
        for b in range(lats // LANES):
            at = (slice(8 * r, 8 * r + 8), slice(LANES * b, LANES * (b + 1)))
            padded = [ref[(a, *at)] for ref in (left_ref, head_ref, tail_ref, right_ref) for a in range(RIM)]
            for a in range(lons):
                value = weights[RIM] * padded[a + RIM]
                for k in range(RIM):
                    value = value + weights[k] * (padded[a + k] + padded[a + 2 * RIM - k])
                gradient_ref[(a, *at)] = value
                for pair in range(PAIRS):
                    sums[pair] = sums[pair] + steps_ref[(pair, a, *at)] * value
                    sums[PAIRS + pair] = sums[PAIRS + pair] + changes_ref[(pair, a, *at)] * value
    row = gram_ref[...] + placed([(STEPS_GRADIENT + k, value) for k, value in enumerate(sums)])
    row = jnp.sum(row, axis=0, keepdims=True)
    rows_ref[...] = jnp.broadcast_to(row[None], rows_ref.shape)


def direction_kernel(rows_ref, gradient_ref, steps_ref, changes_ref, direction_ref):
    row = jnp.broadcast_to(jnp.sum(rows_ref[...], axis=0), (8, LANES))
    lanes = lane_numbers()
    pairs = lax.broadcasted_iota(jnp.int32, (8, LANES), 0)

    def column(lane_of):
        picked = jnp.where(lanes == lane_of, row, 0.0)
        return jnp.broadcast_to(jnp.sum(picked, axis=1, keepdims=True), (8, LANES))

    def element(vector, i):
        return jnp.broadcast_to(vector[i : i + 1], (8, LANES))

    def square_lanes(j):
        low, high = jnp.minimum(pairs, j), jnp.maximum(pairs, j)
        return SQUARES + low * PAIRS - ((low * (low - 1)) >> 1) + high - low

    by_change = [column(pairs * PAIRS + i) for i in range(PAIRS)]
    by_step = [column(pairs + PAIRS * i) for i in range(PAIRS)]
    squares = [column(square_lanes(i)) for i in range(PAIRS)]
    curvs = column(pairs * (PAIRS + 1))
    steps_part = column(pairs + STEPS_GRADIENT)
    changes_part = column(pairs + CHANGES_GRADIENT)
    inverse = 1.0 / curvs
    scaling = element(curvs, PAIRS - 1) / element(squares[PAIRS - 1], PAIRS - 1)
    alphas = [None] * PAIRS
    for i in reversed(range(PAIRS)):
        alphas[i] = element(inverse * steps_part, i)
        steps_part = steps_part - alphas[i] * by_change[i]
        changes_part = changes_part - alphas[i] * squares[i]
    changes_part = scaling * changes_part
    weights = [None] * PAIRS
    for i in range(PAIRS):
        weights[i] = alphas[i] - element(inverse * changes_part, i)
        changes_part = changes_part + weights[i] * by_step[i]
    change_weights = [scaling * alpha for alpha in alphas]
    for a, r, b in tiles(gradient_ref.shape):
        value = -(scaling * gradient_ref[a, r, b])
        for i in range(PAIRS):
            value = value + change_weights[i] * changes_ref[i, a, r, b]
            value = value - weights[i] * steps_ref[i, a, r, b]
        direction_ref[a, r, b] = value


def shifted(x, axis, shift):
    count = lax.axis_size(axis)
    return lax.ppermute(x, axis, [(i, (i + shift) % count) for i in range(count)])


def shards(kernels, steps, curvature):
    _, lons, rad_len, lats = kernels.shape
    rows = rad_len // 4
    block = (lons, rows, lats)
    size = lons * rows * lats
    high, low = (np.concatenate([m, m], axis=1) for m in halves(gauss_matrix(rad_len, 3.0)))
    keep, pass_on, send = call(
        radial_kernel, [block, block, (2, *block)], 2 * 4 * rad_len * kernels.size, 8 * kernels.size
    )(kernels, jnp.asarray(high), jnp.asarray(low))
    near = shifted(send, "event_1", 1)
    far = shifted(pass_on + near[1], "event_0", 1)
    changes, gram = call(
        gram_kernel, [steps.shape, (8, LANES)], 2 * 100 * size, 12 * steps.size
    )(steps, curvature)
    high, low = halves(gauss_matrix(lats, 4.0).T)
    side = (RIM, rows, lats)
    head, tail = call(latitude_kernel, [side, side], 2 * 4 * lats * size, 16 * size)(
        keep, near, far, jnp.asarray(high), jnp.asarray(low)
    )
    left = shifted(tail, CUTS, 1)
    right = shifted(head, CUTS, -1)
    devices = lax.axis_size(CUTS_EVENT)
    gradient, outgoing = call(
        product_kernel, [block, (devices, 1, LANES)], 2 * 30 * size, 4 * 20 * size
    )(head, tail, left, right, steps, changes, gram)
    arrived = lax.all_to_all(outgoing, CUTS_EVENT, 0, 0, tiled=True)
    (direction,) = call(direction_kernel, [block], 2 * 17 * size, 4 * 18 * size)(
        arrived, gradient, steps, changes
    )
    return (gradient, direction)


def solution(mesh):
    torus = Mesh(
        mesh.devices.reshape(2, 4, 4, 2, 2), ("cuts_0", "cuts_1", "cuts_2", "event_0", "event_1")
    )
    in_specs = (P(EVENT, CUTS, None, None), P(None, CUTS, EVENT, None), P(None, CUTS, EVENT, None))
    out_specs = (P(CUTS, EVENT, None), P(CUTS, EVENT, None))
    return jax.shard_map(
        shards, mesh=torus, in_specs=in_specs, out_specs=out_specs, check_vma=False
    )
```

time: 168 us -> 57 us (0.34)
  blocking collectives: 56.8 us -> 18.2 us
  other arithmetic: 25.5 us -> 0.04 us
  between operations: 22.1 us -> 0.69 us
  matrix products: 16 us -> 0 us
  local copies, waits for them, and re-layouts: 21.7 us -> 7.4 us
  Pallas kernels: 0 us -> 9.6 us
  starting transfers between devices: 14.5 us -> 11.7 us
    psum x5 -> x0, blocking collectives: 56.8 us -> none  [one_axis_at_a_time(): return functools.reduce(lax.psum, axes, x)]
    dot_general x16 -> x0, other arithmetic: 20.4 us -> none  [the longest x8 10.6 us: shards(): jnp.dot(products[PAIRS + pair], weights_now, precision=lax.Precision.HIGH...]
    all_to_all x0 -> x1, blocking collectives: none -> 18.2 us  [shards(): arrived = lax.all_to_all(outgoing, CUTS_EVENT, 0, 0, tiled=True)]
    dot_general x4 -> x0, matrix products: 16 us -> none  [the longest x1 8.85 us: shards(): jnp.dot(vectors, vectors.T, precision=lax.Precision.HIGHEST)]
    pallas_call x0 -> x5, Pallas kernels: none -> 9.6 us  [the longest x1 6.63 us: shards(): call(gram_kernel, [steps.shape, (8, LANES)], 2 * 100 * size, 12 * steps.s...]
    all_to_all x1 -> x0, waiting for transfers between devices: 9.01 us -> none  [sent_and_summed(): lax.all_to_all(blocks, axis, split_axis=0, concat_axis=0, tiled=True)]
    ppermute x2 -> x4, waiting for transfers between devices: 1.38 us -> 9.01 us  [shifted(): lax.ppermute(x, axis, [(i, (i + shift) % count) for i in range(count)])]
    concatenate x1 -> x0, local copies, waits for them, and re-layouts: 6.03 us -> none  [shards(): jnp.concatenate([steps.reshape(PAIRS, -1), changes.reshape(PAIRS, -1), gr...]
  transfers between devices with their start and end apart: 3 -> 4, of which waited for: 2 -> 3; matrix products, arithmetic and copies ran while one was open for 4% -> 0% of each run, Pallas kernels for 0% -> 12%
where the time goes in v1:
time: 57 us; the launch traced here: 56.7 us
  blocking collectives  18.2 us (32%)
  starting transfers between devices  11.7 us (21%)
  Pallas kernels  9.6 us (17%)
  waiting for transfers between devices  9.01 us (16%)
  local copies, waits for them, and re-layouts  7.4 us (13%)
  between operations  0.69 us (1%)
    all_to_all x1, blocking collectives, shards(): arrived = lax.all_to_all(outgoing, CUTS_EVENT, 0, 0, tiled=True)  18.2 us
    ppermute x4, starting transfers between devices, shifted(): lax.ppermute(x, axis, [(i, (i + shift) % count) for i in range(count)])  11.7 us
    ppermute x4, waiting for transfers between devices, shifted(): lax.ppermute(x, axis, [(i, (i + shift) % count) for i in range(count)])  9.01 us
    unnamed x16, local copies, waits for them, and re-layouts  7.4 us
    pallas_call x1, Pallas kernels, shards(): call(gram_kernel, [steps.shape, (8, LANES)], 2 * 100 * size, 12 * steps.s...  6.63 us
    pallas_call x1, Pallas kernels, shards(): call(direction_kernel, [block], 2 * 17 * size, 4 * 18 * size)  1.4 us
  transfers between devices with their start and end apart: 4, of which 3 were waited for; matrix products, arithmetic and copies ran while one was open for 0% of the time, Pallas kernels for 12%

profile of v1, /device:TPU:1, one launch (start us, length us, event | category | flops | bytes accessed | tf_op | source)
XLA Modules:
  0.0 56.7 jit_solution(16922226622182177736)
XLA Ops:
  0.6 0.0 copy-start
  0.6 0.0 copy-start.2
  0.6 1.4 %copy-done.2 = f32[1,8,128,256]{3,2,1,0:T(8,128)S(1)} copy-done((f32[1,8,128,256]{3,2,1,0:T(8,128)S(1)}, f32[1,8,128,256]{3,2,1,0:T(8,128)}, u32[]{:S(2)}) %copy-start.2) | copy-done | bytes 1048600
  2.0 0.0 copy-start.6
  2.0 0.8 %copy-done.6 = bf16[128,256]{1,0:T(8,128)(2,1)S(1)} copy-done((bf16[128,256]{1,0:T(8,128)(2,1)S(1)}, bf16[128,256]{1,0:T(8,128)(2,1)}, u32[]{:S(2)}) %copy-start.6) | copy-done | bytes 65560
  2.9 0.0 copy-start.7
  2.9 0.8 %copy-done.7 = bf16[128,256]{1,0:T(8,128)(2,1)S(1)} copy-done((bf16[128,256]{1,0:T(8,128)(2,1)S(1)}, bf16[128,256]{1,0:T(8,128)(2,1)}, u32[]{:S(2)}) %copy-start.7) | copy-done | bytes 65560
  3.7 0.4 shard_map.86
  4.1 1.5 %collective-permute-start = (f32[2,8,32,256]{3,2,1,0:T(8,128)S(1)}, f32[2,8,32,256]{3,2,1,0:T(8,128)S(1)}, u32[]{:S(2)}, u32[]{:S(2)}) collective-permute-start(f32[2,8,32,256]{3,2,1,0:T(8,128)S(1)} %get-tuple-element.12), channel_id=1, source_target_pairs={{0,1},{1,0},{2,3},{3,2},{4,5},{5,4},{6,7},{7,6},{8,9},{9,8},{10,11... | collective-permute-start | bytes 1572872 | tf_op jit(solution)/shard_map/ppermute | solution.py:216
  5.6 1.5 %collective-permute-done.near_ref = f32[2,8,32,256]{3,2,1,0:T(8,128)S(1)} collective-permute-done((f32[2,8,32,256]{3,2,1,0:T(8,128)S(1)}, f32[2,8,32,256]{3,2,1,0:T(8,128)S(1)}, u32[]{:S(2)}, u32[]{:S(2)}) %collective-permute-start) | collective-permute-done | bytes 524320 | tf_op jit(solution)/shard_map/ppermute | solution.py:216
  7.2 1.4 %collective-permute-start.1 = (f32[8,32,256]{2,1,0:T(8,128)S(1)}, f32[8,32,256]{2,1,0:T(8,128)S(1)}, u32[]{:S(2)}, u32[]{:S(2)}) collective-permute-start(f32[8,32,256]{2,1,0:T(8,128)S(1)} %fusion), channel_id=1, source_target_pairs={{0,2},{2,0},{1,3},{3,1},{4,6},{6,4},{5,7},{7,5},{8,10},{10,8},{9,1... | collective-permute-start | bytes 786440 | tf_op jit(solution)/shard_map/ppermute | solution.py:216
  8.6 6.2 %collective-permute-done.1.far_ref = f32[8,32,256]{2,1,0:T(8,128)S(1)} collective-permute-done((f32[8,32,256]{2,1,0:T(8,128)S(1)}, f32[8,32,256]{2,1,0:T(8,128)S(1)}, u32[]{:S(2)}, u32[]{:S(2)}) %collective-permute-start.1) | collective-permute-done | bytes 262176 | tf_op jit(solution)/shard_map/ppermute | solution.py:216
  14.7 0.0 copy-start.4
  14.8 0.9 %copy-done.4 = bf16[256,256]{1,0:T(8,128)(2,1)S(1)} copy-done((bf16[256,256]{1,0:T(8,128)(2,1)S(1)}, bf16[256,256]{1,0:T(8,128)(2,1)}, u32[]{:S(2)}) %copy-start.4) | copy-done | bytes 131096
  15.7 0.0 copy-start.5
  15.7 0.9 %copy-done.5 = bf16[256,256]{1,0:T(8,128)(2,1)S(1)} copy-done((bf16[256,256]{1,0:T(8,128)(2,1)S(1)}, bf16[256,256]{1,0:T(8,128)(2,1)}, u32[]{:S(2)}) %copy-start.5) | copy-done | bytes 131096
  16.6 0.3 shard_map.87
  16.9 8.8 %collective-permute-start.3 = (f32[4,32,256]{2,1,0:T(8,128)S(1)}, f32[4,32,256]{2,1,0:T(8,128)S(1)}, u32[]{:S(2)}, u32[]{:S(2)}) collective-permute-start(f32[4,32,256]{2,1,0:T(8,128)S(1)} %get-tuple-element.14.head_ref), channel_id=1, source_target_pairs={{0,124},{4,0},{8,4},{12,8},{16,12},{20,16},{24,20},{28,24},{32,28}... | collective-permute-start | bytes 393224 | tf_op jit(solution)/shard_map/ppermute | solution.py:216
  25.7 0.0 collective-permute-start.2
  25.7 0.0 copy-done
  25.7 0.0 copy-start.1
  25.7 1.6 %copy-done.1 = f32[8,8,32,256]{3,2,1,0:T(8,128)S(1)} copy-done((f32[8,8,32,256]{3,2,1,0:T(8,128)S(1)}, f32[8,8,32,256]{3,2,1,0:T(8,128)}, u32[]{:S(2)}) %copy-start.1) | copy-done | bytes 2097176
  27.3 6.6 %shard_map.88 = (f32[8,8,32,256]{3,2,1,0:T(8,128)S(1)}, f32[8,128]{1,0:T(8,128)S(1)}) custom-call(f32[8,8,32,256]{3,2,1,0:T(8,128)S(1)} %copy-done, f32[8,8,32,256]{3,2,1,0:T(8,128)S(1)} %copy-done.1), custom_call_target="tpu_custom_call" | custom-call | flops 13107200 | bytes 6291456 | tf_op jit(solution)/shard_map/pallas_call | solution.py:230
  33.9 0.0 collective-permute-done.3.right_ref
  34.0 1.3 %collective-permute-done.2.left_ref = f32[4,32,256]{2,1,0:T(8,128)S(1)} collective-permute-done((f32[4,32,256]{2,1,0:T(8,128)S(1)}, f32[4,32,256]{2,1,0:T(8,128)S(1)}, u32[]{:S(2)}, u32[]{:S(2)}) %collective-permute-start.2) | collective-permute-done | bytes 131104 | tf_op jit(solution)/shard_map/ppermute | solution.py:216
  35.3 0.8 %shard_map.89 = (f32[8,32,256]{2,1,0:T(8,128)}, f32[128,1,128]{2,1,0:T(1,128)S(1)}) custom-call(f32[4,32,256]{2,1,0:T(8,128)S(1)} %get-tuple-element.14.head_ref, f32[4,32,256]{2,1,0:T(8,128)S(1)} %get-tuple-element.15.tail_ref, f32[4,32,256]{2,1,0:T(8,128)S(1)} %collective-permute-done.2.left_ref, f32[4,32,256]{2,1,0:T(8,128)S(1)} %collective-permute-done.3.right_ref, ...), custom_call_target="tpu_custom_call" | custom-call | flops 3932160 | bytes 5242880 | tf_op jit(solution)/shard_map/pallas_call | solution.py:241
  36.1 18.2 %all_to_all.5.rows_ref = f32[128,1,128]{2,1,0:T(1,128)S(1)} all-to-all(f32[128,1,128]{2,1,0:T(1,128)S(1)} %get-tuple-element.19), channel_id=1, replica_groups=mesh['cuts_0'=2,'cuts_1'=4,'cuts_2'=4,'event_0'=2,'event_1'=2] {'cuts_0'..., dimensions={0} | all-to-all | bytes 131072 | tf_op jit(solution)/shard_map/all_to_all | solution.py:244
  54.3 0.0 copy-start.3
  54.3 0.9 %copy-done.3 = f32[8,32,256]{2,1,0:T(8,128)S(1)} copy-done((f32[8,32,256]{2,1,0:T(8,128)S(1)}, f32[8,32,256]{2,1,0:T(8,128)}, u32[]{:S(2)}) %copy-start.3) | copy-done | bytes 262168
  55.3 1.4 %shard_map.90 = f32[8,32,256]{2,1,0:T(8,128)} custom-call(f32[128,1,128]{2,1,0:T(1,128)S(1)} %all_to_all.5.rows_ref, f32[8,32,256]{2,1,0:T(8,128)S(1)} %copy-done.3, f32[8,8,32,256]{3,2,1,0:T(8,128)S(1)} %copy-done, f32[8,8,32,256]{3,2,1,0:T(8,128)S(1)} %get-tuple-element.16.changes_ref), custom_call_target="tpu_custom_call" | custom-call | flops 2228224 | bytes 4718592 | tf_op jit(solution)/shard_map/pallas_call | solution.py:245
  (1 shorter events, 0.0 us)
Async XLA Ops:
  0.6 25.1 %copy-start = (f32[8,8,32,256]{3,2,1,0:T(8,128)S(1)}, f32[8,8,32,256]{3,2,1,0:T(8,128)}, u32[]{:S(2)}) copy-start(f32[8,8,32,256]{3,2,1,0:T(8,128)} %steps_ref.5) | copy-start | bytes 6291460
  0.6 1.4 %copy-start.2 = (f32[1,8,128,256]{3,2,1,0:T(8,128)S(1)}, f32[1,8,128,256]{3,2,1,0:T(8,128)}, u32[]{:S(2)}) copy-start(f32[1,8,128,256]{3,2,1,0:T(8,128)} %kernels_ref.1) | copy-start | bytes 3145732
  2.0 0.8 %copy-start.6 = (bf16[128,256]{1,0:T(8,128)(2,1)S(1)}, bf16[128,256]{1,0:T(8,128)(2,1)}, u32[]{:S(2)}) copy-start(bf16[128,256]{1,0:T(8,128)(2,1)} %constant.9.clone.low_ref) | copy-start | bytes 196612
  2.9 0.8 %copy-start.7 = (bf16[128,256]{1,0:T(8,128)(2,1)S(1)}, bf16[128,256]{1,0:T(8,128)(2,1)}, u32[]{:S(2)}) copy-start(bf16[128,256]{1,0:T(8,128)(2,1)} %constant.8.clone.high_ref) | copy-start | bytes 196612
  4.1 3.0 %collective-permute-start = (f32[2,8,32,256]{3,2,1,0:T(8,128)S(1)}, f32[2,8,32,256]{3,2,1,0:T(8,128)S(1)}, u32[]{:S(2)}, u32[]{:S(2)}) collective-permute-start(f32[2,8,32,256]{3,2,1,0:T(8,128)S(1)} %get-tuple-element.12), channel_id=1, source_target_pairs={{0,1},{1,0},{2,3},{3,2},{4,5},{5,4},{6,7},{7,6},{8,9},{9,8},{10,11... | collective-permute-start | bytes 1572872 | tf_op jit(solution)/shard_map/ppermute | solution.py:216
  7.2 7.6 %collective-permute-start.1 = (f32[8,32,256]{2,1,0:T(8,128)S(1)}, f32[8,32,256]{2,1,0:T(8,128)S(1)}, u32[]{:S(2)}, u32[]{:S(2)}) collective-permute-start(f32[8,32,256]{2,1,0:T(8,128)S(1)} %fusion), channel_id=1, source_target_pairs={{0,2},{2,0},{1,3},{3,1},{4,6},{6,4},{5,7},{7,5},{8,10},{10,8},{9,1... | collective-permute-start | bytes 786440 | tf_op jit(solution)/shard_map/ppermute | solution.py:216
  14.7 0.9 %copy-start.4 = (bf16[256,256]{1,0:T(8,128)(2,1)S(1)}, bf16[256,256]{1,0:T(8,128)(2,1)}, u32[]{:S(2)}) copy-start(bf16[256,256]{1,0:T(8,128)(2,1)} %constant.11.clone.low_ref) | copy-start | bytes 393220
  15.7 0.9 %copy-start.5 = (bf16[256,256]{1,0:T(8,128)(2,1)S(1)}, bf16[256,256]{1,0:T(8,128)(2,1)}, u32[]{:S(2)}) copy-start(bf16[256,256]{1,0:T(8,128)(2,1)} %constant.10.clone.high_ref) | copy-start | bytes 393220
  16.9 17.1 %collective-permute-start.3 = (f32[4,32,256]{2,1,0:T(8,128)S(1)}, f32[4,32,256]{2,1,0:T(8,128)S(1)}, u32[]{:S(2)}, u32[]{:S(2)}) collective-permute-start(f32[4,32,256]{2,1,0:T(8,128)S(1)} %get-tuple-element.14.head_ref), channel_id=1, source_target_pairs={{0,124},{4,0},{8,4},{12,8},{16,12},{20,16},{24,20},{28,24},{32,28}... | collective-permute-start | bytes 393224 | tf_op jit(solution)/shard_map/ppermute | solution.py:216
  25.7 9.5 %collective-permute-start.2 = (f32[4,32,256]{2,1,0:T(8,128)S(1)}, f32[4,32,256]{2,1,0:T(8,128)S(1)}, u32[]{:S(2)}, u32[]{:S(2)}) collective-permute-start(f32[4,32,256]{2,1,0:T(8,128)S(1)} %get-tuple-element.15.tail_ref), channel_id=1, source_target_pairs={{0,4},{4,8},{8,12},{12,16},{16,20},{20,24},{24,28},{28,32},{32,36}... | collective-permute-start | bytes 393224 | tf_op jit(solution)/shard_map/ppermute | solution.py:216
  25.7 1.6 %copy-start.1 = (f32[8,8,32,256]{3,2,1,0:T(8,128)S(1)}, f32[8,8,32,256]{3,2,1,0:T(8,128)}, u32[]{:S(2)}) copy-start(f32[8,8,32,256]{3,2,1,0:T(8,128)} %curvature_ref.1) | copy-start | bytes 6291460
  54.3 1.0 %copy-start.3 = (f32[8,32,256]{2,1,0:T(8,128)S(1)}, f32[8,32,256]{2,1,0:T(8,128)}, u32[]{:S(2)}) copy-start(f32[8,32,256]{2,1,0:T(8,128)} %get-tuple-element.9.gradient_ref) | copy-start | bytes 786436

commit v2 on v1

--- a/solution.py
+++ b/solution.py
@@ -3,7 +3,6 @@
 
 import jax
 import jax.numpy as jnp
-import numpy as np
 from jax import lax
 from jax.experimental import pallas as pl
 from jax.experimental.pallas import tpu as pltpu
@@ -24,19 +23,6 @@
     return SQUARES + low * PAIRS - low * (low - 1) // 2 + high - low
 
 
-def gauss_matrix(length, sigma):
-    points = np.arange(length, dtype=np.float64)
-    offset = points[:, None] - points[None, :]
-    matrix = np.exp(-offset * offset / (2.0 * sigma * sigma))
-    return (matrix / matrix.sum(axis=1, keepdims=True)).astype(np.float32)
-
-
-def halves(matrix):
-    high = matrix.astype(jnp.bfloat16)
-    low = (matrix - high.astype(np.float32)).astype(jnp.bfloat16)
-    return high, low
-
-
 def cycle_weights():
     unscaled = [math.exp(-((column - RIM) ** 2) / 4.5) for column in range(2 * RIM + 1)]
     whole = sum(unscaled)
@@ -53,26 +39,42 @@
     return jnp.dot(a, b, preferred_element_type=jnp.float32)
 
 
-def call(kernel, outs, flops, moved, limit=16):
+def call(kernel, outs, flops, moved, limit=16, **options):
     return pl.pallas_call(
         kernel,
-        out_shape=[jax.ShapeDtypeStruct(shape, jnp.float32) for shape in outs],
+        out_shape=[jax.ShapeDtypeStruct(*out) for out in outs],
         compiler_params=pltpu.CompilerParams(vmem_limit_bytes=limit << 20),
         cost_estimate=pl.CostEstimate(flops=flops, bytes_accessed=moved, transcendentals=0),
-    )
-
-
-def radial_kernel(kernels_ref, high_ref, low_ref, keep_ref, pass_ref, send_ref):
+        **options,
+    )
+
+
+def gauss_rows(length, sigma, rows, axis):
+    offset = (rows - lax.broadcasted_iota(jnp.int32, rows.shape, axis)).astype(jnp.float32)
+    matrix = jnp.exp(-offset * offset / (2.0 * sigma * sigma))
+    return matrix / jnp.sum(matrix, axis=axis, keepdims=True)
+
+
+def radial_kernel(kernels_ref, keep_ref, pass_ref, send_ref, held_ref, semaphores):
+    _, lons, length, lats = kernels_ref.shape
+    copies = [
+        pltpu.make_async_copy(kernels_ref.at[0, a], held_ref.at[a], semaphores.at[a])
+        for a in range(lons)
+    ]
+    for copy in copies:
+        copy.start()
     part = 2 * lax.axis_index("event_0") + lax.axis_index("event_1")
-    rows = kernels_ref.shape[2] // 4
+    rows = length // 4
+    local = lax.broadcasted_iota(jnp.int32, (rows, length), 0)
     order = [part, part ^ 2, part ^ 1, part ^ 3]
-    starts = [pl.multiple_of(block * rows, rows) for block in order]
-    weights = jnp.concatenate(
-        [ref[pl.ds(start, rows), :] for ref in (high_ref, low_ref) for start in starts], axis=0
-    )
-    for a in range(kernels_ref.shape[1]):
-        both = dot(weights, jnp.concatenate(split(kernels_ref[0, a]), axis=0))
-        out = both[: 4 * rows] + both[4 * rows :]
+    matrix = jnp.concatenate(
+        [gauss_rows(length, 3.0, local + rows * block, 1) for block in order], axis=0
+    )
+    weights = jnp.concatenate([jnp.concatenate([m, m], axis=1) for m in split(matrix)], axis=0)
+    for a in range(lons):
+        copies[a].wait()
+        both = dot(weights, jnp.concatenate(split(held_ref[a]), axis=0))
+        out = both[:length] + both[length:]
         keep_ref[a] = out[:rows]
         pass_ref[a] = out[rows : 2 * rows]
         send_ref[0, a] = out[2 * rows : 3 * rows]
@@ -110,44 +112,51 @@
     return row
 
 
-def gram_kernel(steps_ref, curvature_ref, changes_ref, row_ref):
+def gram_kernel(steps_ref, curvature_ref, changes_ref, row_ref, high_ref, low_ref):
     lons, rows, lats = steps_ref.shape[1:]
+    column = lax.broadcasted_iota(jnp.int32, (lats, lats), 1)
+    high_ref[...], low_ref[...] = split(gauss_rows(lats, 4.0, column, 0))
+    spots = [
+        (slice(8 * r, 8 * r + 8), slice(LANES * b, LANES * (b + 1)))
+        for r in range(rows // 8)
+        for b in range(lats // LANES)
+    ]
+    half = PAIRS // 2
+    upper = [(i, j) for i in range(PAIRS) for j in range(i, PAIRS)]
+
+    def first(a, sums):
+        for at in spots:
+            steps = [steps_ref[(i, a, *at)] for i in range(half)]
+            changes = [None] * PAIRS
+            for i in range(PAIRS):
+                step = steps[i] if i < half else steps_ref[(i, a, *at)]
+                changes[i] = curvature_ref[(i, a, *at)] * step
+                changes_ref[(i, a, *at)] = changes[i]
+            sums = [sums[k] + steps[k // PAIRS] * changes[k % PAIRS] for k in range(half * PAIRS)]
+        return sums
+
+    def second(a, sums):
+        for at in spots:
+            steps = [steps_ref[(i, a, *at)] for i in range(half, PAIRS)]
+            changes = [changes_ref[(i, a, *at)] for i in range(PAIRS)]
+            sums = [sums[k] + steps[k // PAIRS] * changes[k % PAIRS] for k in range(half * PAIRS)]
+        return sums
+
+    def third(a, sums):
+        for at in spots:
+            changes = [changes_ref[(i, a, *at)] for i in range(PAIRS)]
+            sums = [value + changes[i] * changes[j] for value, (i, j) in zip(sums, upper)]
+        return sums
+
     zero = jnp.zeros((8, LANES), jnp.float32)
-
-    def tile(ref, pair, t):
-        r = t // (lats // LANES) % (rows // 8)
-        b = t % (lats // LANES)
-        a = t // (lats // LANES * (rows // 8))
-        return (pair, a, pl.ds(pl.multiple_of(r * 8, 8), 8), pl.ds(pl.multiple_of(b * LANES, LANES), LANES))
-
-    count = lons * (rows // 8) * (lats // LANES)
-
-    def first(t, sums):
-        steps = [steps_ref[tile(None, i, t)] for i in range(PAIRS)]
-        changes = [curvature_ref[tile(None, i, t)] * steps[i] for i in range(PAIRS)]
-        for i in range(PAIRS):
-            changes_ref[tile(None, i, t)] = changes[i]
-        return [sums[i * PAIRS + j] + steps[i] * changes[j] for i in range(4) for j in range(PAIRS)]
-
-    def second(t, sums):
-        steps = [steps_ref[tile(None, i, t)] for i in range(4, PAIRS)]
-        changes = [changes_ref[tile(None, i, t)] for i in range(PAIRS)]
-        return [sums[i * PAIRS + j] + steps[i] * changes[j] for i in range(4) for j in range(PAIRS)]
-
-    upper = [(i, j) for i in range(PAIRS) for j in range(i, PAIRS)]
-
-    def third(t, sums):
-        changes = [changes_ref[tile(None, i, t)] for i in range(PAIRS)]
-        return [value + changes[i] * changes[j] for value, (i, j) in zip(sums, upper)]
-
     row = zero
-    for number, step, size in ((0, first, 32), (1, second, 32), (2, third, len(upper))):
-        sums = lax.fori_loop(0, count, step, [zero] * size)
-        row = row + placed([(32 * number + k, value) for k, value in enumerate(sums)])
+    for start, step, size in ((0, first, 32), (32, second, 32), (SQUARES, third, len(upper))):
+        sums = lax.fori_loop(0, lons, step, [zero] * size)
+        row = row + placed([(start + k, value) for k, value in enumerate(sums)])
     row_ref[...] = row
 
 
-def product_kernel(head_ref, tail_ref, left_ref, right_ref, steps_ref, changes_ref, gram_ref, gradient_ref, rows_ref):
+def product_kernel(head_ref, tail_ref, left_ref, right_ref, steps_ref, changes_ref, gram_ref, gradient_ref, kept_ref, rows_ref):
     lons, rows, lats = gradient_ref.shape
     weights = cycle_weights()
     sums = [jnp.zeros((8, LANES), jnp.float32) for _ in range(2 * PAIRS)]
@@ -160,6 +169,7 @@
                 for k in range(RIM):
                     value = value + weights[k] * (padded[a + k] + padded[a + 2 * RIM - k])
                 gradient_ref[(a, *at)] = value
+                kept_ref[(a, *at)] = value
                 for pair in range(PAIRS):
                     sums[pair] = sums[pair] + steps_ref[(pair, a, *at)] * value
                     sums[PAIRS + pair] = sums[PAIRS + pair] + changes_ref[(pair, a, *at)] * value
@@ -219,31 +229,44 @@
 def shards(kernels, steps, curvature):
     _, lons, rad_len, lats = kernels.shape
     rows = rad_len // 4
-    block = (lons, rows, lats)
+    block = ((lons, rows, lats), jnp.float32)
     size = lons * rows * lats
-    high, low = (np.concatenate([m, m], axis=1) for m in halves(gauss_matrix(rad_len, 3.0)))
     keep, pass_on, send = call(
-        radial_kernel, [block, block, (2, *block)], 2 * 4 * rad_len * kernels.size, 8 * kernels.size
-    )(kernels, jnp.asarray(high), jnp.asarray(low))
+        radial_kernel,
+        [block, block, ((2, lons, rows, lats), jnp.float32)],
+        2 * 4 * rad_len * kernels.size,
+        8 * kernels.size,
+        in_specs=[pl.BlockSpec(memory_space=pltpu.HBM)],
+        scratch_shapes=[
+            pltpu.VMEM(kernels.shape[1:], jnp.float32),
+            pltpu.SemaphoreType.DMA((lons,)),
+        ],
+    )(pltpu.with_memory_space_constraint(kernels, pltpu.HBM))
     near = shifted(send, "event_1", 1)
     far = shifted(pass_on + near[1], "event_0", 1)
-    changes, gram = call(
-        gram_kernel, [steps.shape, (8, LANES)], 2 * 100 * size, 12 * steps.size
+    square = ((lats, lats), jnp.bfloat16)
+    changes, gram, high, low = call(
+        gram_kernel,
+        [(steps.shape, jnp.float32), ((8, LANES), jnp.float32), square, square],
+        2 * 100 * size,
+        12 * steps.size,
     )(steps, curvature)
-    high, low = halves(gauss_matrix(lats, 4.0).T)
-    side = (RIM, rows, lats)
+    side = ((RIM, rows, lats), jnp.float32)
     head, tail = call(latitude_kernel, [side, side], 2 * 4 * lats * size, 16 * size)(
-        keep, near, far, jnp.asarray(high), jnp.asarray(low)
+        keep, near, far, high, low
     )
     left = shifted(tail, CUTS, 1)
     right = shifted(head, CUTS, -1)
     devices = lax.axis_size(CUTS_EVENT)
-    gradient, outgoing = call(
-        product_kernel, [block, (devices, 1, LANES)], 2 * 30 * size, 4 * 20 * size
+    gradient, kept, outgoing = call(
+        product_kernel,
+        [block, block, ((devices, 1, LANES), jnp.float32)],
+        2 * 30 * size,
+        4 * 20 * size,
     )(head, tail, left, right, steps, changes, gram)
     arrived = lax.all_to_all(outgoing, CUTS_EVENT, 0, 0, tiled=True)
     (direction,) = call(direction_kernel, [block], 2 * 17 * size, 4 * 18 * size)(
-        arrived, gradient, steps, changes
+        arrived, kept, steps, changes
     )
     return (gradient, direction)
 

time: 57 us -> 50.3 us (0.88)
  local copies, waits for them, and re-layouts: 7.4 us -> 3.18 us
  blocking collectives: 18.2 us -> 15.1 us
  waiting for transfers between devices: 9.01 us -> 11.5 us
  Pallas kernels: 9.6 us -> 7.8 us
    unnamed x16 -> x6, local copies, waits for them, and re-layouts: 7.4 us -> 3.18 us
    all_to_all x1, blocking collectives: 18.2 us -> 15.1 us  [shards(): arrived = lax.all_to_all(outgoing, CUTS_EVENT, 0, 0, tiled=True)]
    ppermute x4, waiting for transfers between devices: 9.01 us -> 11.5 us  [shifted(): lax.ppermute(x, axis, [(i, (i + shift) % count) for i in range(count)])]
    pallas_call x3, Pallas kernels: 7.9 us -> 6.1 us  [the longest x1 2.71 us: shards(): call(radial_kernel, [block, block, ((2, lons, rows, lats), jnp.float32)],...]
  transfers between devices with their start and end apart: 4 -> 4, of which waited for: 3 -> 4; matrix products, arithmetic and copies ran while one was open for 0% -> 0% of each run, Pallas kernels for 12% -> 5%
where the time goes in v2:
time: 50.3 us; the launch traced here: 50.1 us
  blocking collectives  15.1 us (30%)
  starting transfers between devices  11.7 us (23%)
  waiting for transfers between devices  11.5 us (23%)
  Pallas kernels  7.8 us (16%)
  local copies, waits for them, and re-layouts  3.18 us (6%)
  between operations  0.66 us (1%)
    all_to_all x1, blocking collectives, shards(): arrived = lax.all_to_all(outgoing, CUTS_EVENT, 0, 0, tiled=True)  15.1 us
    ppermute x4, starting transfers between devices, shifted(): lax.ppermute(x, axis, [(i, (i + shift) % count) for i in range(count)])  11.7 us
    ppermute x4, waiting for transfers between devices, shifted(): lax.ppermute(x, axis, [(i, (i + shift) % count) for i in range(count)])  11.5 us
    unnamed x6, local copies, waits for them, and re-layouts  3.18 us
    pallas_call x1, Pallas kernels, shards(): call(radial_kernel, [block, block, ((2, lons, rows, lats), jnp.float32)],...  2.71 us
    pallas_call x1, Pallas kernels, shards(): call(gram_kernel, [(steps.shape, jnp.float32), ((8, LANES), jnp.float32),...  2.54 us
    pallas_call x1, Pallas kernels, shards(): call(direction_kernel, [block], 2 * 17 * size, 4 * 18 * size)  1.39 us
  transfers between devices with their start and end apart: 4, of which 4 were waited for; matrix products, arithmetic and copies ran while one was open for 0% of the time, Pallas kernels for 5%

profile of v2, /device:TPU:1, one launch (start us, length us, event | category | flops | bytes accessed | tf_op | source)
XLA Modules:
  0.0 50.1 jit_solution(2881965829928124954)
XLA Ops:
  0.6 2.7 %shard_map.50 = (f32[8,32,256]{2,1,0:T(8,128)S(1)}, f32[8,32,256]{2,1,0:T(8,128)S(1)}, f32[2,8,32,256]{3,2,1,0:T(8,128)S(1)}) custom-call(f32[1,8,128,256]{3,2,1,0:T(8,128)} %kernels_ref.1), custom_call_target="tpu_custom_call" | custom-call | flops 268435456 | bytes 2097152 | tf_op jit(solution)/shard_map/pallas_call | solution.py:234
  3.3 1.5 %collective-permute-start = (f32[2,8,32,256]{3,2,1,0:T(8,128)S(1)}, f32[2,8,32,256]{3,2,1,0:T(8,128)S(1)}, u32[]{:S(2)}, u32[]{:S(2)}) collective-permute-start(f32[2,8,32,256]{3,2,1,0:T(8,128)S(1)} %get-tuple-element.15), channel_id=1, source_target_pairs={{0,1},{1,0},{2,3},{3,2},{4,5},{5,4},{6,7},{7,6},{8,9},{9,8},{10,11... | collective-permute-start | bytes 1572872 | tf_op jit(solution)/shard_map/ppermute | solution.py:226
  4.8 1.5 %collective-permute-done.near_ref = f32[2,8,32,256]{3,2,1,0:T(8,128)S(1)} collective-permute-done((f32[2,8,32,256]{3,2,1,0:T(8,128)S(1)}, f32[2,8,32,256]{3,2,1,0:T(8,128)S(1)}, u32[]{:S(2)}, u32[]{:S(2)}) %collective-permute-start) | collective-permute-done | bytes 524320 | tf_op jit(solution)/shard_map/ppermute | solution.py:226
  6.4 1.4 %collective-permute-start.1 = (f32[8,32,256]{2,1,0:T(8,128)S(1)}, f32[8,32,256]{2,1,0:T(8,128)S(1)}, u32[]{:S(2)}, u32[]{:S(2)}) collective-permute-start(f32[8,32,256]{2,1,0:T(8,128)S(1)} %fusion), channel_id=1, source_target_pairs={{0,2},{2,0},{1,3},{3,1},{4,6},{6,4},{5,7},{7,5},{8,10},{10,8},{9,1... | collective-permute-start | bytes 786440 | tf_op jit(solution)/shard_map/ppermute | solution.py:226
  7.8 0.0 copy-start
  7.8 1.6 %copy-done = f32[8,8,32,256]{3,2,1,0:T(8,128)S(1)} copy-done((f32[8,8,32,256]{3,2,1,0:T(8,128)S(1)}, f32[8,8,32,256]{3,2,1,0:T(8,128)}, u32[]{:S(2)}) %copy-start) | copy-done | bytes 2097176
  9.4 0.0 copy-start.2
  9.4 1.6 %copy-done.2 = f32[8,8,32,256]{3,2,1,0:T(8,128)S(1)} copy-done((f32[8,8,32,256]{3,2,1,0:T(8,128)S(1)}, f32[8,8,32,256]{3,2,1,0:T(8,128)}, u32[]{:S(2)}) %copy-start.2) | copy-done | bytes 2097176
  11.0 0.0 copy-start.1
  11.0 2.5 %shard_map.51 = (f32[8,8,32,256]{3,2,1,0:T(8,128)S(1)}, f32[8,128]{1,0:T(8,128)S(1)}, bf16[256,256]{1,0:T(8,128)(2,1)S(1)}, bf16[256,256]{1,0:T(8,128)(2,1)S(1)}) custom-call(f32[8,8,32,256]{3,2,1,0:T(8,128)S(1)} %copy-done, f32[8,8,32,256]{3,2,1,0:T(8,128)S(1)} %copy-done.2), custom_call_target="tpu_custom_call" | custom-call | flops 13107200 | bytes 6291456 | tf_op jit(solution)/shard_map/pallas_call | solution.py:248
  13.5 0.4 collective-permute-done.1.far_ref
  14.0 0.3 shard_map.52
  14.3 8.8 %collective-permute-start.3 = (f32[4,32,256]{2,1,0:T(8,128)S(1)}, f32[4,32,256]{2,1,0:T(8,128)S(1)}, u32[]{:S(2)}, u32[]{:S(2)}) collective-permute-start(f32[4,32,256]{2,1,0:T(8,128)S(1)} %get-tuple-element.19.head_ref), channel_id=1, source_target_pairs={{0,124},{4,0},{8,4},{12,8},{16,12},{20,16},{24,20},{28,24},{32,28}... | collective-permute-start | bytes 393224 | tf_op jit(solution)/shard_map/ppermute | solution.py:226
  23.1 0.0 collective-permute-start.2
  23.1 1.9 %collective-permute-done.3.right_ref = f32[4,32,256]{2,1,0:T(8,128)S(1)} collective-permute-done((f32[4,32,256]{2,1,0:T(8,128)S(1)}, f32[4,32,256]{2,1,0:T(8,128)S(1)}, u32[]{:S(2)}, u32[]{:S(2)}) %collective-permute-start.3) | collective-permute-done | bytes 131104 | tf_op jit(solution)/shard_map/ppermute | solution.py:226
  25.1 7.6 %collective-permute-done.2.left_ref = f32[4,32,256]{2,1,0:T(8,128)S(1)} collective-permute-done((f32[4,32,256]{2,1,0:T(8,128)S(1)}, f32[4,32,256]{2,1,0:T(8,128)S(1)}, u32[]{:S(2)}, u32[]{:S(2)}) %collective-permute-start.2) | collective-permute-done | bytes 131104 | tf_op jit(solution)/shard_map/ppermute | solution.py:226
  32.7 0.0 copy-done.1
  32.7 0.9 %shard_map.53 = (f32[8,32,256]{2,1,0:T(8,128)}, f32[8,32,256]{2,1,0:T(8,128)S(1)}, f32[128,1,128]{2,1,0:T(1,128)S(1)}) custom-call(f32[4,32,256]{2,1,0:T(8,128)S(1)} %get-tuple-element.19.head_ref, f32[4,32,256]{2,1,0:T(8,128)S(1)} %get-tuple-element.20.tail_ref, f32[4,32,256]{2,1,0:T(8,128)S(1)} %collective-permute-done.2.left_ref, ...), custom_call_target="tpu_custom_call" | custom-call | flops 3932160 | bytes 5242880 | tf_op jit(solution)/shard_map/pallas_call | solution.py:261
  33.5 15.1 %all_to_all.5.rows_ref = f32[128,1,128]{2,1,0:T(1,128)S(1)} all-to-all(f32[128,1,128]{2,1,0:T(1,128)S(1)} %get-tuple-element.24), channel_id=1, replica_groups=mesh['cuts_0'=2,'cuts_1'=4,'cuts_2'=4,'event_0'=2,'event_1'=2] {'cuts_0'..., dimensions={0} | all-to-all | bytes 131072 | tf_op jit(solution)/shard_map/all_to_all | solution.py:267
  48.7 1.4 %shard_map.54 = f32[8,32,256]{2,1,0:T(8,128)} custom-call(f32[128,1,128]{2,1,0:T(1,128)S(1)} %all_to_all.5.rows_ref, f32[8,32,256]{2,1,0:T(8,128)S(1)} %get-tuple-element.25.gradient_ref, f32[8,8,32,256]{3,2,1,0:T(8,128)S(1)} %copy-done.1, f32[8,8,32,256]{3,2,1,0:T(8,128)S(1)} %get-tuple-element.21.changes_ref), custom_call_target="tpu_custom_call" | custom-call | flops 2228224 | bytes 4718592 | tf_op jit(solution)/shard_map/pallas_call | solution.py:268
  (1 shorter events, 0.0 us)
Async XLA Ops:
  3.3 3.0 %collective-permute-start = (f32[2,8,32,256]{3,2,1,0:T(8,128)S(1)}, f32[2,8,32,256]{3,2,1,0:T(8,128)S(1)}, u32[]{:S(2)}, u32[]{:S(2)}) collective-permute-start(f32[2,8,32,256]{3,2,1,0:T(8,128)S(1)} %get-tuple-element.15), channel_id=1, source_target_pairs={{0,1},{1,0},{2,3},{3,2},{4,5},{5,4},{6,7},{7,6},{8,9},{9,8},{10,11... | collective-permute-start | bytes 1572872 | tf_op jit(solution)/shard_map/ppermute | solution.py:226
  6.4 7.6 %collective-permute-start.1 = (f32[8,32,256]{2,1,0:T(8,128)S(1)}, f32[8,32,256]{2,1,0:T(8,128)S(1)}, u32[]{:S(2)}, u32[]{:S(2)}) collective-permute-start(f32[8,32,256]{2,1,0:T(8,128)S(1)} %fusion), channel_id=1, source_target_pairs={{0,2},{2,0},{1,3},{3,1},{4,6},{6,4},{5,7},{7,5},{8,10},{10,8},{9,1... | collective-permute-start | bytes 786440 | tf_op jit(solution)/shard_map/ppermute | solution.py:226
  7.8 1.6 %copy-start = (f32[8,8,32,256]{3,2,1,0:T(8,128)S(1)}, f32[8,8,32,256]{3,2,1,0:T(8,128)}, u32[]{:S(2)}) copy-start(f32[8,8,32,256]{3,2,1,0:T(8,128)} %steps_ref.5) | copy-start | bytes 6291460
  9.4 1.6 %copy-start.2 = (f32[8,8,32,256]{3,2,1,0:T(8,128)S(1)}, f32[8,8,32,256]{3,2,1,0:T(8,128)}, u32[]{:S(2)}) copy-start(f32[8,8,32,256]{3,2,1,0:T(8,128)} %curvature_ref.1) | copy-start | bytes 6291460
  11.0 21.7 %copy-start.1 = (f32[8,8,32,256]{3,2,1,0:T(8,128)S(1)}, f32[8,8,32,256]{3,2,1,0:T(8,128)}, u32[]{:S(2)}) copy-start(f32[8,8,32,256]{3,2,1,0:T(8,128)} %steps_ref.5) | copy-start | bytes 6291460
  14.3 10.8 %collective-permute-start.3 = (f32[4,32,256]{2,1,0:T(8,128)S(1)}, f32[4,32,256]{2,1,0:T(8,128)S(1)}, u32[]{:S(2)}, u32[]{:S(2)}) collective-permute-start(f32[4,32,256]{2,1,0:T(8,128)S(1)} %get-tuple-element.19.head_ref), channel_id=1, source_target_pairs={{0,124},{4,0},{8,4},{12,8},{16,12},{20,16},{24,20},{28,24},{32,28}... | collective-permute-start | bytes 393224 | tf_op jit(solution)/shard_map/ppermute | solution.py:226
  23.1 9.5 %collective-permute-start.2 = (f32[4,32,256]{2,1,0:T(8,128)S(1)}, f32[4,32,256]{2,1,0:T(8,128)S(1)}, u32[]{:S(2)}, u32[]{:S(2)}) collective-permute-start(f32[4,32,256]{2,1,0:T(8,128)S(1)} %get-tuple-element.20.tail_ref), channel_id=1, source_target_pairs={{0,4},{4,8},{8,12},{12,16},{16,20},{20,24},{24,28},{28,32},{32,36}... | collective-permute-start | bytes 393224 | tf_op jit(solution)/shard_map/ppermute | solution.py:226

commit v3 on v2

--- a/solution.py
+++ b/solution.py
@@ -3,6 +3,7 @@
 
 import jax
 import jax.numpy as jnp
+import numpy as np
 from jax import lax
 from jax.experimental import pallas as pl
 from jax.experimental.pallas import tpu as pltpu
@@ -23,6 +24,20 @@
     return SQUARES + low * PAIRS - low * (low - 1) // 2 + high - low
 
 
+def gauss_matrix(length, sigma):
+    points = np.arange(length, dtype=np.float64)
+    offset = points[:, None] - points[None, :]
+    matrix = np.exp(-offset * offset / (2.0 * sigma * sigma))
+    return (matrix / matrix.sum(axis=1, keepdims=True)).astype(np.float32)
+
+
+def radial_table(length):
+    matrix = gauss_matrix(length, 3.0)
+    high = matrix.astype(jnp.bfloat16)
+    low = (matrix - high.astype(np.float32)).astype(jnp.bfloat16)
+    return np.stack([np.concatenate([m, m], axis=1) for m in (high, low)])
+
+
 def cycle_weights():
     unscaled = [math.exp(-((column - RIM) ** 2) / 4.5) for column in range(2 * RIM + 1)]
     whole = sum(unscaled)
@@ -55,24 +70,32 @@
     return matrix / jnp.sum(matrix, axis=axis, keepdims=True)
 
 
-def radial_kernel(kernels_ref, keep_ref, pass_ref, send_ref, held_ref, semaphores):
+def radial_kernel(kernels_ref, table_ref, keep_ref, pass_ref, send_ref, held_ref, weights_ref, semaphores):
     _, lons, length, lats = kernels_ref.shape
-    copies = [
-        pltpu.make_async_copy(kernels_ref.at[0, a], held_ref.at[a], semaphores.at[a])
-        for a in range(lons)
-    ]
+    part = 2 * lax.axis_index("event_0") + lax.axis_index("event_1")
+    rows = length // 4
+    copies = []
+    for half in range(2):
+        for k, block in enumerate((part, part ^ 2, part ^ 1, part ^ 3)):
+            at = pl.ds(pl.multiple_of(block * rows, rows), rows)
+            copies.append(
+                pltpu.make_async_copy(
+                    table_ref.at[half, at],
+                    weights_ref.at[pl.ds(half * length + k * rows, rows)],
+                    semaphores.at[len(copies)],
+                )
+            )
+    for a in range(lons):
+        copies.append(
+            pltpu.make_async_copy(kernels_ref.at[0, a], held_ref.at[a], semaphores.at[len(copies)])
+        )
     for copy in copies:
         copy.start()
-    part = 2 * lax.axis_index("event_0") + lax.axis_index("event_1")
-    rows = length // 4
-    local = lax.broadcasted_iota(jnp.int32, (rows, length), 0)
-    order = [part, part ^ 2, part ^ 1, part ^ 3]
-    matrix = jnp.concatenate(
-        [gauss_rows(length, 3.0, local + rows * block, 1) for block in order], axis=0
-    )
-    weights = jnp.concatenate([jnp.concatenate([m, m], axis=1) for m in split(matrix)], axis=0)
+    for copy in copies[:8]:
+        copy.wait()
+    weights = weights_ref[...]
     for a in range(lons):
-        copies[a].wait()
+        copies[8 + a].wait()
         both = dot(weights, jnp.concatenate(split(held_ref[a]), axis=0))
         out = both[:length] + both[length:]
         keep_ref[a] = out[:rows]
@@ -81,7 +104,7 @@
         send_ref[1, a] = out[3 * rows :]
 
 
-def latitude_kernel(keep_ref, near_ref, far_ref, high_ref, low_ref, head_ref, tail_ref):
+def latitude_kernel(keep_ref, near_ref, far_ref, high_ref, low_ref, tail_ref, head_ref):
     lons, rows, lats = keep_ref.shape
     summed = (keep_ref[...] + near_ref[0] + far_ref[...]).reshape(lons * rows, lats)
     both = jnp.concatenate(split(summed), axis=0)
@@ -156,7 +179,7 @@
     row_ref[...] = row
 
 
-def product_kernel(head_ref, tail_ref, left_ref, right_ref, steps_ref, changes_ref, gram_ref, gradient_ref, kept_ref, rows_ref):
+def product_kernel(head_ref, tail_ref, right_ref, left_ref, steps_ref, changes_ref, gram_ref, gradient_ref, kept_ref, rows_ref):
     lons, rows, lats = gradient_ref.shape
     weights = cycle_weights()
     sums = [jnp.zeros((8, LANES), jnp.float32) for _ in range(2 * PAIRS)]
@@ -221,6 +244,10 @@
         direction_ref[a, r, b] = value
 
 
+def in_hbm(x):
+    return pltpu.with_memory_space_constraint(x, pltpu.HBM)
+
+
 def shifted(x, axis, shift):
     count = lax.axis_size(axis)
     return lax.ppermute(x, axis, [(i, (i + shift) % count) for i in range(count)])
@@ -236,12 +263,13 @@
         [block, block, ((2, lons, rows, lats), jnp.float32)],
         2 * 4 * rad_len * kernels.size,
         8 * kernels.size,
-        in_specs=[pl.BlockSpec(memory_space=pltpu.HBM)],
+        in_specs=[pl.BlockSpec(memory_space=pltpu.HBM)] * 2,
         scratch_shapes=[
             pltpu.VMEM(kernels.shape[1:], jnp.float32),
-            pltpu.SemaphoreType.DMA((lons,)),
+            pltpu.VMEM((2 * rad_len, 2 * rad_len), jnp.bfloat16),
+            pltpu.SemaphoreType.DMA((8 + lons,)),
         ],
-    )(pltpu.with_memory_space_constraint(kernels, pltpu.HBM))
+    )(in_hbm(kernels), in_hbm(jnp.asarray(radial_table(rad_len))))
     near = shifted(send, "event_1", 1)
     far = shifted(pass_on + near[1], "event_0", 1)
     square = ((lats, lats), jnp.bfloat16)
@@ -252,7 +280,7 @@
         12 * steps.size,
     )(steps, curvature)
     side = ((RIM, rows, lats), jnp.float32)
-    head, tail = call(latitude_kernel, [side, side], 2 * 4 * lats * size, 16 * size)(
+    tail, head = call(latitude_kernel, [side, side], 2 * 4 * lats * size, 16 * size)(
         keep, near, far, high, low
     )
     left = shifted(tail, CUTS, 1)
@@ -263,7 +291,7 @@
         [block, block, ((devices, 1, LANES), jnp.float32)],
         2 * 30 * size,
         4 * 20 * size,
-    )(head, tail, left, right, steps, changes, gram)
+    )(head, tail, right, left, steps, changes, gram)
     arrived = lax.all_to_all(outgoing, CUTS_EVENT, 0, 0, tiled=True)
     (direction,) = call(direction_kernel, [block], 2 * 17 * size, 4 * 18 * size)(
         arrived, kept, steps, changes

time: 50.3 us -> 50.5 us (level)
  no operation moved by 1% of the time
where the time goes in v3:
time: 50.5 us; the launch traced here: 50.3 us
  blocking collectives  15.1 us (30%)
  starting transfers between devices  11.7 us (23%)
  waiting for transfers between devices  11.5 us (23%)
  Pallas kernels  8.03 us (16%)
  local copies, waits for them, and re-layouts  3.18 us (6%)
  between operations  0.66 us (1%)
    all_to_all x1, blocking collectives, shards(): arrived = lax.all_to_all(outgoing, CUTS_EVENT, 0, 0, tiled=True)  15.1 us
    ppermute x4, starting transfers between devices, shifted(): lax.ppermute(x, axis, [(i, (i + shift) % count) for i in range(count)])  11.7 us
    ppermute x4, waiting for transfers between devices, shifted(): lax.ppermute(x, axis, [(i, (i + shift) % count) for i in range(count)])  11.5 us
    unnamed x6, local copies, waits for them, and re-layouts  3.18 us
    pallas_call x1, Pallas kernels, shards(): call(radial_kernel, [block, block, ((2, lons, rows, lats), jnp.float32)],...  2.94 us
    pallas_call x1, Pallas kernels, shards(): call(gram_kernel, [(steps.shape, jnp.float32), ((8, LANES), jnp.float32),...  2.54 us
    pallas_call x1, Pallas kernels, shards(): call(direction_kernel, [block], 2 * 17 * size, 4 * 18 * size)  1.39 us
  transfers between devices with their start and end apart: 4, of which 4 were waited for; matrix products, arithmetic and copies ran while one was open for 0% of the time, Pallas kernels for 5%

profile of v3, /device:TPU:1, one launch (start us, length us, event | category | flops | bytes accessed | tf_op | source)
XLA Modules:
  0.0 50.3 jit_solution(2435754423170525926)
XLA Ops:
  0.6 2.9 %shard_map.59 = (f32[8,32,256]{2,1,0:T(8,128)S(1)}, f32[8,32,256]{2,1,0:T(8,128)S(1)}, f32[2,8,32,256]{3,2,1,0:T(8,128)S(1)}) custom-call(f32[1,8,128,256]{3,2,1,0:T(8,128)} %kernels_ref.1, bf16[2,128,256]{2,1,0:T(8,128)(2,1)} %constant.2.clone.table_ref), custom_call_target="tpu_custom_call" | custom-call | flops 268435456 | bytes 2097152 | tf_op jit(solution)/shard_map/pallas_call | solution.py:261
  3.6 1.5 %collective-permute-start = (f32[2,8,32,256]{3,2,1,0:T(8,128)S(1)}, f32[2,8,32,256]{3,2,1,0:T(8,128)S(1)}, u32[]{:S(2)}, u32[]{:S(2)}) collective-permute-start(f32[2,8,32,256]{3,2,1,0:T(8,128)S(1)} %get-tuple-element.15), channel_id=1, source_target_pairs={{0,1},{1,0},{2,3},{3,2},{4,5},{5,4},{6,7},{7,6},{8,9},{9,8},{10,11... | collective-permute-start | bytes 1572872 | tf_op jit(solution)/shard_map/ppermute | solution.py:253
  5.0 1.5 %collective-permute-done.near_ref = f32[2,8,32,256]{3,2,1,0:T(8,128)S(1)} collective-permute-done((f32[2,8,32,256]{3,2,1,0:T(8,128)S(1)}, f32[2,8,32,256]{3,2,1,0:T(8,128)S(1)}, u32[]{:S(2)}, u32[]{:S(2)}) %collective-permute-start) | collective-permute-done | bytes 524320 | tf_op jit(solution)/shard_map/ppermute | solution.py:253
  6.6 1.4 %collective-permute-start.1 = (f32[8,32,256]{2,1,0:T(8,128)S(1)}, f32[8,32,256]{2,1,0:T(8,128)S(1)}, u32[]{:S(2)}, u32[]{:S(2)}) collective-permute-start(f32[8,32,256]{2,1,0:T(8,128)S(1)} %fusion), channel_id=1, source_target_pairs={{0,2},{2,0},{1,3},{3,1},{4,6},{6,4},{5,7},{7,5},{8,10},{10,8},{9,1... | collective-permute-start | bytes 786440 | tf_op jit(solution)/shard_map/ppermute | solution.py:253
  8.0 0.0 copy-start
  8.0 1.6 %copy-done = f32[8,8,32,256]{3,2,1,0:T(8,128)S(1)} copy-done((f32[8,8,32,256]{3,2,1,0:T(8,128)S(1)}, f32[8,8,32,256]{3,2,1,0:T(8,128)}, u32[]{:S(2)}) %copy-start) | copy-done | bytes 2097176
  9.6 0.0 copy-start.2
  9.6 1.6 %copy-done.2 = f32[8,8,32,256]{3,2,1,0:T(8,128)S(1)} copy-done((f32[8,8,32,256]{3,2,1,0:T(8,128)S(1)}, f32[8,8,32,256]{3,2,1,0:T(8,128)}, u32[]{:S(2)}) %copy-start.2) | copy-done | bytes 2097176
  11.2 0.0 copy-start.1
  11.2 2.5 %shard_map.60 = (f32[8,8,32,256]{3,2,1,0:T(8,128)S(1)}, f32[8,128]{1,0:T(8,128)S(1)}, bf16[256,256]{1,0:T(8,128)(2,1)S(1)}, bf16[256,256]{1,0:T(8,128)(2,1)S(1)}) custom-call(f32[8,8,32,256]{3,2,1,0:T(8,128)S(1)} %copy-done, f32[8,8,32,256]{3,2,1,0:T(8,128)S(1)} %copy-done.2), custom_call_target="tpu_custom_call" | custom-call | flops 13107200 | bytes 6291456 | tf_op jit(solution)/shard_map/pallas_call | solution.py:276
  13.7 0.4 collective-permute-done.1.far_ref
  14.2 0.3 shard_map.61
  14.5 8.8 %collective-permute-start.2 = (f32[4,32,256]{2,1,0:T(8,128)S(1)}, f32[4,32,256]{2,1,0:T(8,128)S(1)}, u32[]{:S(2)}, u32[]{:S(2)}) collective-permute-start(f32[4,32,256]{2,1,0:T(8,128)S(1)} %get-tuple-element.19.head_ref), channel_id=1, source_target_pairs={{0,124},{4,0},{8,4},{12,8},{16,12},{20,16},{24,20},{28,24},{32,28}... | collective-permute-start | bytes 393224 | tf_op jit(solution)/shard_map/ppermute | solution.py:253
  23.3 0.0 collective-permute-start.3
  23.3 1.9 %collective-permute-done.2.right_ref = f32[4,32,256]{2,1,0:T(8,128)S(1)} collective-permute-done((f32[4,32,256]{2,1,0:T(8,128)S(1)}, f32[4,32,256]{2,1,0:T(8,128)S(1)}, u32[]{:S(2)}, u32[]{:S(2)}) %collective-permute-start.2) | collective-permute-done | bytes 131104 | tf_op jit(solution)/shard_map/ppermute | solution.py:253
  25.3 7.6 %collective-permute-done.3.left_ref = f32[4,32,256]{2,1,0:T(8,128)S(1)} collective-permute-done((f32[4,32,256]{2,1,0:T(8,128)S(1)}, f32[4,32,256]{2,1,0:T(8,128)S(1)}, u32[]{:S(2)}, u32[]{:S(2)}) %collective-permute-start.3) | collective-permute-done | bytes 131104 | tf_op jit(solution)/shard_map/ppermute | solution.py:253
  32.9 0.0 copy-done.1
  32.9 0.9 %shard_map.62 = (f32[8,32,256]{2,1,0:T(8,128)}, f32[8,32,256]{2,1,0:T(8,128)S(1)}, f32[128,1,128]{2,1,0:T(1,128)S(1)}) custom-call(f32[4,32,256]{2,1,0:T(8,128)S(1)} %get-tuple-element.19.head_ref, f32[4,32,256]{2,1,0:T(8,128)S(1)} %get-tuple-element.20.tail_ref, f32[4,32,256]{2,1,0:T(8,128)S(1)} %collective-permute-done.2.right_ref, ...), custom_call_target="tpu_custom_call" | custom-call | flops 3932160 | bytes 5242880 | tf_op jit(solution)/shard_map/pallas_call | solution.py:289
  33.7 15.1 %all_to_all.5.rows_ref = f32[128,1,128]{2,1,0:T(1,128)S(1)} all-to-all(f32[128,1,128]{2,1,0:T(1,128)S(1)} %get-tuple-element.24), channel_id=1, replica_groups=mesh['cuts_0'=2,'cuts_1'=4,'cuts_2'=4,'event_0'=2,'event_1'=2] {'cuts_0'..., dimensions={0} | all-to-all | bytes 131072 | tf_op jit(solution)/shard_map/all_to_all | solution.py:295
  48.9 1.4 %shard_map.63 = f32[8,32,256]{2,1,0:T(8,128)} custom-call(f32[128,1,128]{2,1,0:T(1,128)S(1)} %all_to_all.5.rows_ref, f32[8,32,256]{2,1,0:T(8,128)S(1)} %get-tuple-element.25.gradient_ref, f32[8,8,32,256]{3,2,1,0:T(8,128)S(1)} %copy-done.1, f32[8,8,32,256]{3,2,1,0:T(8,128)S(1)} %get-tuple-element.21.changes_ref), custom_call_target="tpu_custom_call" | custom-call | flops 2228224 | bytes 4718592 | tf_op jit(solution)/shard_map/pallas_call | solution.py:296
  (1 shorter events, 0.0 us)
Async XLA Ops:
  3.6 3.0 %collective-permute-start = (f32[2,8,32,256]{3,2,1,0:T(8,128)S(1)}, f32[2,8,32,256]{3,2,1,0:T(8,128)S(1)}, u32[]{:S(2)}, u32[]{:S(2)}) collective-permute-start(f32[2,8,32,256]{3,2,1,0:T(8,128)S(1)} %get-tuple-element.15), channel_id=1, source_target_pairs={{0,1},{1,0},{2,3},{3,2},{4,5},{5,4},{6,7},{7,6},{8,9},{9,8},{10,11... | collective-permute-start | bytes 1572872 | tf_op jit(solution)/shard_map/ppermute | solution.py:253
  6.6 7.6 %collective-permute-start.1 = (f32[8,32,256]{2,1,0:T(8,128)S(1)}, f32[8,32,256]{2,1,0:T(8,128)S(1)}, u32[]{:S(2)}, u32[]{:S(2)}) collective-permute-start(f32[8,32,256]{2,1,0:T(8,128)S(1)} %fusion), channel_id=1, source_target_pairs={{0,2},{2,0},{1,3},{3,1},{4,6},{6,4},{5,7},{7,5},{8,10},{10,8},{9,1... | collective-permute-start | bytes 786440 | tf_op jit(solution)/shard_map/ppermute | solution.py:253
  8.0 1.6 %copy-start = (f32[8,8,32,256]{3,2,1,0:T(8,128)S(1)}, f32[8,8,32,256]{3,2,1,0:T(8,128)}, u32[]{:S(2)}) copy-start(f32[8,8,32,256]{3,2,1,0:T(8,128)} %steps_ref.5) | copy-start | bytes 6291460
  9.6 1.6 %copy-start.2 = (f32[8,8,32,256]{3,2,1,0:T(8,128)S(1)}, f32[8,8,32,256]{3,2,1,0:T(8,128)}, u32[]{:S(2)}) copy-start(f32[8,8,32,256]{3,2,1,0:T(8,128)} %curvature_ref.1) | copy-start | bytes 6291460
  11.2 21.7 %copy-start.1 = (f32[8,8,32,256]{3,2,1,0:T(8,128)S(1)}, f32[8,8,32,256]{3,2,1,0:T(8,128)}, u32[]{:S(2)}) copy-start(f32[8,8,32,256]{3,2,1,0:T(8,128)} %steps_ref.5) | copy-start | bytes 6291460
  14.5 10.8 %collective-permute-start.2 = (f32[4,32,256]{2,1,0:T(8,128)S(1)}, f32[4,32,256]{2,1,0:T(8,128)S(1)}, u32[]{:S(2)}, u32[]{:S(2)}) collective-permute-start(f32[4,32,256]{2,1,0:T(8,128)S(1)} %get-tuple-element.19.head_ref), channel_id=1, source_target_pairs={{0,124},{4,0},{8,4},{12,8},{16,12},{20,16},{24,20},{28,24},{32,28}... | collective-permute-start | bytes 393224 | tf_op jit(solution)/shard_map/ppermute | solution.py:253
  23.3 9.5 %collective-permute-start.3 = (f32[4,32,256]{2,1,0:T(8,128)S(1)}, f32[4,32,256]{2,1,0:T(8,128)S(1)}, u32[]{:S(2)}, u32[]{:S(2)}) collective-permute-start(f32[4,32,256]{2,1,0:T(8,128)S(1)} %get-tuple-element.20.tail_ref), channel_id=1, source_target_pairs={{0,4},{4,8},{8,12},{12,16},{16,20},{20,24},{24,28},{28,32},{32,36}... | collective-permute-start | bytes 393224 | tf_op jit(solution)/shard_map/ppermute | solution.py:253

commit v4 on v3

--- a/solution.py
+++ b/solution.py
@@ -1,4 +1,3 @@
-import functools
 import math
 
 import jax
@@ -19,11 +18,6 @@
 SQUARES, STEPS_GRADIENT, CHANGES_GRADIENT = 64, 100, 108
 
 
-def square_lane(i, j):
-    low, high = min(i, j), max(i, j)
-    return SQUARES + low * PAIRS - low * (low - 1) // 2 + high - low
-
-
 def gauss_matrix(length, sigma):
     points = np.arange(length, dtype=np.float64)
     offset = points[:, None] - points[None, :]
@@ -64,14 +58,14 @@
     )
 
 
-def gauss_rows(length, sigma, rows, axis):
+def gauss_rows(sigma, rows, axis):
     offset = (rows - lax.broadcasted_iota(jnp.int32, rows.shape, axis)).astype(jnp.float32)
     matrix = jnp.exp(-offset * offset / (2.0 * sigma * sigma))
     return matrix / jnp.sum(matrix, axis=axis, keepdims=True)
 
 
 def radial_kernel(kernels_ref, table_ref, keep_ref, pass_ref, send_ref, held_ref, weights_ref, semaphores):
-    _, lons, length, lats = kernels_ref.shape
+    _, lons, length, _ = kernels_ref.shape
     part = 2 * lax.axis_index("event_0") + lax.axis_index("event_1")
     rows = length // 4
     copies = []
@@ -85,23 +79,26 @@
                     semaphores.at[len(copies)],
                 )
             )
-    for a in range(lons):
+    half = lons // 2
+    for part in range(2):
+        at = slice(part * half, part * half + half)
         copies.append(
-            pltpu.make_async_copy(kernels_ref.at[0, a], held_ref.at[a], semaphores.at[len(copies)])
+            pltpu.make_async_copy(kernels_ref.at[0, at], held_ref.at[at], semaphores.at[len(copies)])
         )
     for copy in copies:
         copy.start()
     for copy in copies[:8]:
         copy.wait()
-    weights = weights_ref[...]
-    for a in range(lons):
-        copies[8 + a].wait()
-        both = dot(weights, jnp.concatenate(split(held_ref[a]), axis=0))
-        out = both[:length] + both[length:]
-        keep_ref[a] = out[:rows]
-        pass_ref[a] = out[rows : 2 * rows]
-        send_ref[0, a] = out[2 * rows : 3 * rows]
-        send_ref[1, a] = out[3 * rows :]
+    for part in range(2):
+        copies[8 + part].wait()
+        weights = weights_ref[...]
+        for a in range(part * half, part * half + half):
+            both = dot(weights, jnp.concatenate(split(held_ref[a]), axis=0))
+            out = both[:length] + both[length:]
+            keep_ref[a] = out[:rows]
+            pass_ref[a] = out[rows : 2 * rows]
+            send_ref[0, a] = out[2 * rows : 3 * rows]
+            send_ref[1, a] = out[3 * rows :]
 
 
 def latitude_kernel(keep_ref, near_ref, far_ref, high_ref, low_ref, tail_ref, head_ref):
@@ -138,7 +135,7 @@
 def gram_kernel(steps_ref, curvature_ref, changes_ref, row_ref, high_ref, low_ref):
     lons, rows, lats = steps_ref.shape[1:]
     column = lax.broadcasted_iota(jnp.int32, (lats, lats), 1)
-    high_ref[...], low_ref[...] = split(gauss_rows(lats, 4.0, column, 0))
+    high_ref[...], low_ref[...] = split(gauss_rows(4.0, column, 0))
     spots = [
         (slice(8 * r, 8 * r + 8), slice(LANES * b, LANES * (b + 1)))
         for r in range(rows // 8)
@@ -267,7 +264,7 @@
         scratch_shapes=[
             pltpu.VMEM(kernels.shape[1:], jnp.float32),
             pltpu.VMEM((2 * rad_len, 2 * rad_len), jnp.bfloat16),
-            pltpu.SemaphoreType.DMA((8 + lons,)),
+            pltpu.SemaphoreType.DMA((10,)),
         ],
     )(in_hbm(kernels), in_hbm(jnp.asarray(radial_table(rad_len))))
     near = shifted(send, "event_1", 1)

time: 50.5 us -> 49.5 us (0.980)
  Pallas kernels: 8.03 us -> 6.98 us
    pallas_call x1, Pallas kernels: 2.94 us -> 1.89 us  [shards(): call(radial_kernel, [block, block, ((2, lons, rows, lats), jnp.float32)],...]
where the time goes in v4:
time: 49.5 us; the launch traced here: 49.2 us
  blocking collectives  15.1 us (31%)
  starting transfers between devices  11.7 us (24%)
  waiting for transfers between devices  11.5 us (23%)
  Pallas kernels  6.98 us (14%)
  local copies, waits for them, and re-layouts  3.18 us (6%)
  between operations  0.66 us (1%)
    all_to_all x1, blocking collectives, shards(): arrived = lax.all_to_all(outgoing, CUTS_EVENT, 0, 0, tiled=True)  15.1 us
    ppermute x4, starting transfers between devices, shifted(): lax.ppermute(x, axis, [(i, (i + shift) % count) for i in range(count)])  11.7 us
    ppermute x4, waiting for transfers between devices, shifted(): lax.ppermute(x, axis, [(i, (i + shift) % count) for i in range(count)])  11.5 us
    unnamed x6, local copies, waits for them, and re-layouts  3.18 us
    pallas_call x1, Pallas kernels, shards(): call(gram_kernel, [(steps.shape, jnp.float32), ((8, LANES), jnp.float32),...  2.54 us
    pallas_call x1, Pallas kernels, shards(): call(radial_kernel, [block, block, ((2, lons, rows, lats), jnp.float32)],...  1.89 us
    pallas_call x1, Pallas kernels, shards(): call(direction_kernel, [block], 2 * 17 * size, 4 * 18 * size)  1.39 us
  transfers between devices with their start and end apart: 4, of which 4 were waited for; matrix products, arithmetic and copies ran while one was open for 0% of the time, Pallas kernels for 5%

profile of v4, /device:TPU:1, one launch (start us, length us, event | category | flops | bytes accessed | tf_op | source)
XLA Modules:
  0.0 49.2 jit_solution(11325379462833326208)
XLA Ops:
  0.6 1.9 %shard_map.59 = (f32[8,32,256]{2,1,0:T(8,128)S(1)}, f32[8,32,256]{2,1,0:T(8,128)S(1)}, f32[2,8,32,256]{3,2,1,0:T(8,128)S(1)}) custom-call(f32[1,8,128,256]{3,2,1,0:T(8,128)} %kernels_ref.1, bf16[2,128,256]{2,1,0:T(8,128)(2,1)} %constant.2.clone.table_ref), custom_call_target="tpu_custom_call" | custom-call | flops 268435456 | bytes 2097152 | tf_op jit(solution)/shard_map/pallas_call | solution.py:258
  2.5 1.5 %collective-permute-start = (f32[2,8,32,256]{3,2,1,0:T(8,128)S(1)}, f32[2,8,32,256]{3,2,1,0:T(8,128)S(1)}, u32[]{:S(2)}, u32[]{:S(2)}) collective-permute-start(f32[2,8,32,256]{3,2,1,0:T(8,128)S(1)} %get-tuple-element.15), channel_id=1, source_target_pairs={{0,1},{1,0},{2,3},{3,2},{4,5},{5,4},{6,7},{7,6},{8,9},{9,8},{10,11... | collective-permute-start | bytes 1572872 | tf_op jit(solution)/shard_map/ppermute | solution.py:250
  4.0 1.5 %collective-permute-done.near_ref = f32[2,8,32,256]{3,2,1,0:T(8,128)S(1)} collective-permute-done((f32[2,8,32,256]{3,2,1,0:T(8,128)S(1)}, f32[2,8,32,256]{3,2,1,0:T(8,128)S(1)}, u32[]{:S(2)}, u32[]{:S(2)}) %collective-permute-start) | collective-permute-done | bytes 524320 | tf_op jit(solution)/shard_map/ppermute | solution.py:250
  5.6 1.4 %collective-permute-start.1 = (f32[8,32,256]{2,1,0:T(8,128)S(1)}, f32[8,32,256]{2,1,0:T(8,128)S(1)}, u32[]{:S(2)}, u32[]{:S(2)}) collective-permute-start(f32[8,32,256]{2,1,0:T(8,128)S(1)} %fusion), channel_id=1, source_target_pairs={{0,2},{2,0},{1,3},{3,1},{4,6},{6,4},{5,7},{7,5},{8,10},{10,8},{9,1... | collective-permute-start | bytes 786440 | tf_op jit(solution)/shard_map/ppermute | solution.py:250
  7.0 0.0 copy-start
  7.0 1.6 %copy-done = f32[8,8,32,256]{3,2,1,0:T(8,128)S(1)} copy-done((f32[8,8,32,256]{3,2,1,0:T(8,128)S(1)}, f32[8,8,32,256]{3,2,1,0:T(8,128)}, u32[]{:S(2)}) %copy-start) | copy-done | bytes 2097176
  8.6 0.0 copy-start.2
  8.6 1.6 %copy-done.2 = f32[8,8,32,256]{3,2,1,0:T(8,128)S(1)} copy-done((f32[8,8,32,256]{3,2,1,0:T(8,128)S(1)}, f32[8,8,32,256]{3,2,1,0:T(8,128)}, u32[]{:S(2)}) %copy-start.2) | copy-done | bytes 2097176
  10.2 0.0 copy-start.1
  10.2 2.5 %shard_map.60 = (f32[8,8,32,256]{3,2,1,0:T(8,128)S(1)}, f32[8,128]{1,0:T(8,128)S(1)}, bf16[256,256]{1,0:T(8,128)(2,1)S(1)}, bf16[256,256]{1,0:T(8,128)(2,1)S(1)}) custom-call(f32[8,8,32,256]{3,2,1,0:T(8,128)S(1)} %copy-done, f32[8,8,32,256]{3,2,1,0:T(8,128)S(1)} %copy-done.2), custom_call_target="tpu_custom_call" | custom-call | flops 13107200 | bytes 6291456 | tf_op jit(solution)/shard_map/pallas_call | solution.py:273
  12.7 0.4 collective-permute-done.1.far_ref
  13.1 0.3 shard_map.61
  13.5 8.8 %collective-permute-start.2 = (f32[4,32,256]{2,1,0:T(8,128)S(1)}, f32[4,32,256]{2,1,0:T(8,128)S(1)}, u32[]{:S(2)}, u32[]{:S(2)}) collective-permute-start(f32[4,32,256]{2,1,0:T(8,128)S(1)} %get-tuple-element.19.head_ref), channel_id=1, source_target_pairs={{0,124},{4,0},{8,4},{12,8},{16,12},{20,16},{24,20},{28,24},{32,28}... | collective-permute-start | bytes 393224 | tf_op jit(solution)/shard_map/ppermute | solution.py:250
  22.3 0.0 collective-permute-start.3
  22.3 1.9 %collective-permute-done.2.right_ref = f32[4,32,256]{2,1,0:T(8,128)S(1)} collective-permute-done((f32[4,32,256]{2,1,0:T(8,128)S(1)}, f32[4,32,256]{2,1,0:T(8,128)S(1)}, u32[]{:S(2)}, u32[]{:S(2)}) %collective-permute-start.2) | collective-permute-done | bytes 131104 | tf_op jit(solution)/shard_map/ppermute | solution.py:250
  24.2 7.6 %collective-permute-done.3.left_ref = f32[4,32,256]{2,1,0:T(8,128)S(1)} collective-permute-done((f32[4,32,256]{2,1,0:T(8,128)S(1)}, f32[4,32,256]{2,1,0:T(8,128)S(1)}, u32[]{:S(2)}, u32[]{:S(2)}) %collective-permute-start.3) | collective-permute-done | bytes 131104 | tf_op jit(solution)/shard_map/ppermute | solution.py:250
  31.8 0.0 copy-done.1
  31.8 0.9 %shard_map.62 = (f32[8,32,256]{2,1,0:T(8,128)}, f32[8,32,256]{2,1,0:T(8,128)S(1)}, f32[128,1,128]{2,1,0:T(1,128)S(1)}) custom-call(f32[4,32,256]{2,1,0:T(8,128)S(1)} %get-tuple-element.19.head_ref, f32[4,32,256]{2,1,0:T(8,128)S(1)} %get-tuple-element.20.tail_ref, f32[4,32,256]{2,1,0:T(8,128)S(1)} %collective-permute-done.2.right_ref, ...), custom_call_target="tpu_custom_call" | custom-call | flops 3932160 | bytes 5242880 | tf_op jit(solution)/shard_map/pallas_call | solution.py:286
  32.7 15.1 %all_to_all.5.rows_ref = f32[128,1,128]{2,1,0:T(1,128)S(1)} all-to-all(f32[128,1,128]{2,1,0:T(1,128)S(1)} %get-tuple-element.24), channel_id=1, replica_groups=mesh['cuts_0'=2,'cuts_1'=4,'cuts_2'=4,'event_0'=2,'event_1'=2] {'cuts_0'..., dimensions={0} | all-to-all | bytes 131072 | tf_op jit(solution)/shard_map/all_to_all | solution.py:292
  47.8 1.4 %shard_map.63 = f32[8,32,256]{2,1,0:T(8,128)} custom-call(f32[128,1,128]{2,1,0:T(1,128)S(1)} %all_to_all.5.rows_ref, f32[8,32,256]{2,1,0:T(8,128)S(1)} %get-tuple-element.25.gradient_ref, f32[8,8,32,256]{3,2,1,0:T(8,128)S(1)} %copy-done.1, f32[8,8,32,256]{3,2,1,0:T(8,128)S(1)} %get-tuple-element.21.changes_ref), custom_call_target="tpu_custom_call" | custom-call | flops 2228224 | bytes 4718592 | tf_op jit(solution)/shard_map/pallas_call | solution.py:293
  (1 shorter events, 0.0 us)
Async XLA Ops:
  2.5 3.0 %collective-permute-start = (f32[2,8,32,256]{3,2,1,0:T(8,128)S(1)}, f32[2,8,32,256]{3,2,1,0:T(8,128)S(1)}, u32[]{:S(2)}, u32[]{:S(2)}) collective-permute-start(f32[2,8,32,256]{3,2,1,0:T(8,128)S(1)} %get-tuple-element.15), channel_id=1, source_target_pairs={{0,1},{1,0},{2,3},{3,2},{4,5},{5,4},{6,7},{7,6},{8,9},{9,8},{10,11... | collective-permute-start | bytes 1572872 | tf_op jit(solution)/shard_map/ppermute | solution.py:250
  5.6 7.6 %collective-permute-start.1 = (f32[8,32,256]{2,1,0:T(8,128)S(1)}, f32[8,32,256]{2,1,0:T(8,128)S(1)}, u32[]{:S(2)}, u32[]{:S(2)}) collective-permute-start(f32[8,32,256]{2,1,0:T(8,128)S(1)} %fusion), channel_id=1, source_target_pairs={{0,2},{2,0},{1,3},{3,1},{4,6},{6,4},{5,7},{7,5},{8,10},{10,8},{9,1... | collective-permute-start | bytes 786440 | tf_op jit(solution)/shard_map/ppermute | solution.py:250
  7.0 1.6 %copy-start = (f32[8,8,32,256]{3,2,1,0:T(8,128)S(1)}, f32[8,8,32,256]{3,2,1,0:T(8,128)}, u32[]{:S(2)}) copy-start(f32[8,8,32,256]{3,2,1,0:T(8,128)} %steps_ref.5) | copy-start | bytes 6291460
  8.6 1.6 %copy-start.2 = (f32[8,8,32,256]{3,2,1,0:T(8,128)S(1)}, f32[8,8,32,256]{3,2,1,0:T(8,128)}, u32[]{:S(2)}) copy-start(f32[8,8,32,256]{3,2,1,0:T(8,128)} %curvature_ref.1) | copy-start | bytes 6291460
  10.2 21.7 %copy-start.1 = (f32[8,8,32,256]{3,2,1,0:T(8,128)S(1)}, f32[8,8,32,256]{3,2,1,0:T(8,128)}, u32[]{:S(2)}) copy-start(f32[8,8,32,256]{3,2,1,0:T(8,128)} %steps_ref.5) | copy-start | bytes 6291460
  13.5 10.8 %collective-permute-start.2 = (f32[4,32,256]{2,1,0:T(8,128)S(1)}, f32[4,32,256]{2,1,0:T(8,128)S(1)}, u32[]{:S(2)}, u32[]{:S(2)}) collective-permute-start(f32[4,32,256]{2,1,0:T(8,128)S(1)} %get-tuple-element.19.head_ref), channel_id=1, source_target_pairs={{0,124},{4,0},{8,4},{12,8},{16,12},{20,16},{24,20},{28,24},{32,28}... | collective-permute-start | bytes 393224 | tf_op jit(solution)/shard_map/ppermute | solution.py:250
  22.3 9.5 %collective-permute-start.3 = (f32[4,32,256]{2,1,0:T(8,128)S(1)}, f32[4,32,256]{2,1,0:T(8,128)S(1)}, u32[]{:S(2)}, u32[]{:S(2)}) collective-permute-start(f32[4,32,256]{2,1,0:T(8,128)S(1)} %get-tuple-element.20.tail_ref), channel_id=1, source_target_pairs={{0,4},{4,8},{8,12},{12,16},{16,20},{20,24},{24,28},{28,32},{32,36}... | collective-permute-start | bytes 393224 | tf_op jit(solution)/shard_map/ppermute | solution.py:250

commit v5 on v2

--- a/solution.py
+++ b/solution.py
@@ -1,4 +1,3 @@
-import functools
 import math
 
 import jax
@@ -18,11 +17,6 @@
 SQUARES, STEPS_GRADIENT, CHANGES_GRADIENT = 64, 100, 108
 
 
-def square_lane(i, j):
-    low, high = min(i, j), max(i, j)
-    return SQUARES + low * PAIRS - low * (low - 1) // 2 + high - low
-
-
 def cycle_weights():
     unscaled = [math.exp(-((column - RIM) ** 2) / 4.5) for column in range(2 * RIM + 1)]
     whole = sum(unscaled)
@@ -55,14 +49,22 @@
     return matrix / jnp.sum(matrix, axis=axis, keepdims=True)
 
 
-def radial_kernel(kernels_ref, keep_ref, pass_ref, send_ref, held_ref, semaphores):
-    _, lons, length, lats = kernels_ref.shape
-    copies = [
-        pltpu.make_async_copy(kernels_ref.at[0, a], held_ref.at[a], semaphores.at[a])
-        for a in range(lons)
-    ]
-    for copy in copies:
-        copy.start()
+def gauss_rows(length, sigma, rows, axis):
+    offset = (rows - lax.broadcasted_iota(jnp.int32, rows.shape, axis)).astype(jnp.float32)
+    matrix = jnp.exp(-offset * offset / (2.0 * sigma * sigma))
+    return matrix / jnp.sum(matrix, axis=axis, keepdims=True)
+
+
+def radial_kernel(kernels_ref, keep_ref, pass_ref, send_keep_ref, send_pass_ref, held_ref, semaphores):
+    _, lons, length, _ = kernels_ref.shape
+    half = lons // 2
+    copies = []
+    for piece in range(2):
+        at = slice(piece * half, piece * half + half)
+        copies.append(
+            pltpu.make_async_copy(kernels_ref.at[0, at], held_ref.at[at], semaphores.at[piece])
+        )
+        copies[piece].start()
     part = 2 * lax.axis_index("event_0") + lax.axis_index("event_1")
     rows = length // 4
     local = lax.broadcasted_iota(jnp.int32, (rows, length), 0)
@@ -71,22 +73,36 @@
         [gauss_rows(length, 3.0, local + rows * block, 1) for block in order], axis=0
     )
     weights = jnp.concatenate([jnp.concatenate([m, m], axis=1) for m in split(matrix)], axis=0)
-    for a in range(lons):
-        copies[a].wait()
-        both = dot(weights, jnp.concatenate(split(held_ref[a]), axis=0))
-        out = both[:length] + both[length:]
-        keep_ref[a] = out[:rows]
-        pass_ref[a] = out[rows : 2 * rows]
-        send_ref[0, a] = out[2 * rows : 3 * rows]
-        send_ref[1, a] = out[3 * rows :]
-
-
-def latitude_kernel(keep_ref, near_ref, far_ref, high_ref, low_ref, head_ref, tail_ref):
+    outs = (keep_ref, pass_ref, send_keep_ref, send_pass_ref)
+    for piece in range(2):
+        copies[piece].wait()
+        for a in range(piece * half, piece * half + half):
+            both = dot(weights, jnp.concatenate(split(held_ref[a]), axis=0))
+            out = both[:length] + both[length:]
+            for k, ref in enumerate(outs):
+                ref[a] = out[k * rows : (k + 1) * rows]
+
+
+def smoothed(field, high, low):
+    count = field.shape[0]
+    both = jnp.concatenate(split(field), axis=0)
+    out = dot(both, high) + dot(both, low)
+    return out[:count] + out[count:]
+
+
+def fetch_kernel(curvature_ref, held_ref, high_ref, low_ref, semaphore):
+    copy = pltpu.make_async_copy(curvature_ref, held_ref, semaphore)
+    copy.start()
+    lats = high_ref.shape[0]
+    column = lax.broadcasted_iota(jnp.int32, (lats, lats), 1)
+    high_ref[...], low_ref[...] = split(gauss_rows(lats, 4.0, column, 0))
+    copy.wait()
+
+
+def latitude_kernel(keep_ref, near_ref, far_ref, high_ref, low_ref, tail_ref, head_ref):
     lons, rows, lats = keep_ref.shape
-    summed = (keep_ref[...] + near_ref[0] + far_ref[...]).reshape(lons * rows, lats)
-    both = jnp.concatenate(split(summed), axis=0)
-    out = dot(both, high_ref[...]) + dot(both, low_ref[...])
-    plane = (out[: lons * rows] + out[lons * rows :]).reshape(lons, rows, lats)
+    summed = (keep_ref[...] + near_ref[...] + far_ref[...]).reshape(lons * rows, lats)
+    plane = smoothed(summed, high_ref[...], low_ref[...]).reshape(lons, rows, lats)
     head_ref[...] = plane[:RIM]
     tail_ref[...] = plane[lons - RIM :]
 
@@ -112,10 +128,8 @@
     return row
 
 
-def gram_kernel(steps_ref, curvature_ref, changes_ref, row_ref, high_ref, low_ref):
+def gram_kernel(steps_ref, curvature_ref, changes_ref, row_ref):
     lons, rows, lats = steps_ref.shape[1:]
-    column = lax.broadcasted_iota(jnp.int32, (lats, lats), 1)
-    high_ref[...], low_ref[...] = split(gauss_rows(lats, 4.0, column, 0))
     spots = [
         (slice(8 * r, 8 * r + 8), slice(LANES * b, LANES * (b + 1)))
         for r in range(rows // 8)
@@ -156,20 +170,36 @@
     row_ref[...] = row
 
 
-def product_kernel(head_ref, tail_ref, left_ref, right_ref, steps_ref, changes_ref, gram_ref, gradient_ref, kept_ref, rows_ref):
+def product_kernel(
+    head_ref, tail_ref, left_ref, wrap_left_ref, right_ref, wrap_own_ref, wrap_other_ref,
+    high_ref, low_ref, steps_ref, changes_ref, gram_ref, gradient_ref, rows_ref, right_scratch,
+):
     lons, rows, lats = gradient_ref.shape
     weights = cycle_weights()
+    cut = cut_number()
+    last = lax.axis_size(CUTS) - 1
+
+    @pl.when(cut == last)
+    def _():
+        summed = (wrap_own_ref[...] + wrap_other_ref[...]).reshape(RIM * rows, lats)
+        plane = smoothed(summed, high_ref[...], low_ref[...])
+        right_scratch[...] = plane.reshape(RIM, rows, lats)
+
+    @pl.when(cut != last)
+    def _():
+        right_scratch[...] = right_ref[...]
+
     sums = [jnp.zeros((8, LANES), jnp.float32) for _ in range(2 * PAIRS)]
     for r in range(rows // 8):
         for b in range(lats // LANES):
             at = (slice(8 * r, 8 * r + 8), slice(LANES * b, LANES * (b + 1)))
-            padded = [ref[(a, *at)] for ref in (left_ref, head_ref, tail_ref, right_ref) for a in range(RIM)]
+            padded = [left_ref[(a, *at)] + wrap_left_ref[(a, *at)] for a in range(RIM)]
+            padded += [ref[(a, *at)] for ref in (head_ref, tail_ref, right_scratch) for a in range(RIM)]
             for a in range(lons):
                 value = weights[RIM] * padded[a + RIM]
                 for k in range(RIM):
                     value = value + weights[k] * (padded[a + k] + padded[a + 2 * RIM - k])
                 gradient_ref[(a, *at)] = value
-                kept_ref[(a, *at)] = value
                 for pair in range(PAIRS):
                     sums[pair] = sums[pair] + steps_ref[(pair, a, *at)] * value
                     sums[PAIRS + pair] = sums[PAIRS + pair] + changes_ref[(pair, a, *at)] * value
@@ -178,7 +208,11 @@
     rows_ref[...] = jnp.broadcast_to(row[None], rows_ref.shape)
 
 
-def direction_kernel(rows_ref, gradient_ref, steps_ref, changes_ref, direction_ref):
+def direction_kernel(
+    rows_ref, gradient_ref, steps_ref, changes_ref, gradient_out, direction_out, direction_ref, semaphores
+):
+    written = pltpu.make_async_copy(gradient_ref, gradient_out, semaphores.at[0])
+    written.start()
     row = jnp.broadcast_to(jnp.sum(rows_ref[...], axis=0), (8, LANES))
     lanes = lane_numbers()
     pairs = lax.broadcasted_iota(jnp.int32, (8, LANES), 0)
@@ -213,17 +247,48 @@
         weights[i] = alphas[i] - element(inverse * changes_part, i)
         changes_part = changes_part + weights[i] * by_step[i]
     change_weights = [scaling * alpha for alpha in alphas]
-    for a, r, b in tiles(gradient_ref.shape):
-        value = -(scaling * gradient_ref[a, r, b])
-        for i in range(PAIRS):
-            value = value + change_weights[i] * changes_ref[i, a, r, b]
-            value = value - weights[i] * steps_ref[i, a, r, b]
-        direction_ref[a, r, b] = value
+    copies = []
+    lons, pieces = gradient_ref.shape[0], 4
+    for piece in range(pieces):
+        at = slice(piece * lons // pieces, (piece + 1) * lons // pieces)
+        for a, r, b in tiles(gradient_ref.shape):
+            if at.start <= a < at.stop:
+                value = -(scaling * gradient_ref[a, r, b])
+                for i in range(PAIRS):
+                    value = value + change_weights[i] * changes_ref[i, a, r, b]
+                    value = value - weights[i] * steps_ref[i, a, r, b]
+                direction_ref[a, r, b] = value
+        if copies:
+            copies[-1].start()
+        copies.append(
+            pltpu.make_async_copy(
+                direction_ref.at[at], direction_out.at[at], semaphores.at[1 + piece]
+            )
+        )
+    copies[-1].start()
+    for copy in copies:
+        copy.wait()
+    written.wait()
+
+
+def in_hbm(x):
+    return pltpu.with_memory_space_constraint(x, pltpu.HBM)
 
 
 def shifted(x, axis, shift):
     count = lax.axis_size(axis)
-    return lax.ppermute(x, axis, [(i, (i + shift) % count) for i in range(count)])
+    return lax.ppermute(x, axis, [(i, i + shift) for i in range(count) if 0 <= i + shift < count])
+
+
+def swapped(x, axis):
+    return lax.ppermute(x, axis, [(0, 1), (1, 0)])
+
+
+def cut_number():
+    number = 0
+    for axis in CUTS:
+        number = number * lax.axis_size(axis) + lax.axis_index(axis)
+    return number
 
 
 def shards(kernels, steps, curvature):
@@ -231,44 +296,62 @@
     rows = rad_len // 4
     block = ((lons, rows, lats), jnp.float32)
     size = lons * rows * lats
-    keep, pass_on, send = call(
+    keep, pass_on, send_keep, send_pass = call(
         radial_kernel,
-        [block, block, ((2, lons, rows, lats), jnp.float32)],
+        [block] * 4,
         2 * 4 * rad_len * kernels.size,
         8 * kernels.size,
         in_specs=[pl.BlockSpec(memory_space=pltpu.HBM)],
-        scratch_shapes=[
-            pltpu.VMEM(kernels.shape[1:], jnp.float32),
-            pltpu.SemaphoreType.DMA((lons,)),
-        ],
-    )(pltpu.with_memory_space_constraint(kernels, pltpu.HBM))
-    near = shifted(send, "event_1", 1)
-    far = shifted(pass_on + near[1], "event_0", 1)
+        scratch_shapes=[pltpu.VMEM(kernels.shape[1:], jnp.float32), pltpu.SemaphoreType.DMA((2,))],
+    )(in_hbm(kernels))
+    near_pass = swapped(send_pass, "event_1")
+    passed = pass_on + near_pass
+    far = swapped(passed, "event_0")
+    near_keep = swapped(send_keep, "event_1")
     square = ((lats, lats), jnp.bfloat16)
-    changes, gram, high, low = call(
+    held_curvature, high, low = call(
+        fetch_kernel,
+        [(curvature.shape, jnp.float32), square, square],
+        10 * lats * lats,
+        8 * curvature.size,
+        in_specs=[pl.BlockSpec(memory_space=pltpu.HBM)],
+        scratch_shapes=[pltpu.SemaphoreType.DMA],
+    )(in_hbm(curvature))
+    cuts, last = lax.axis_size(CUTS), lax.axis_size(CUTS) - 1
+    events = lax.axis_size(EVENT)
+    wrap_other = lax.ppermute(
+        passed[:RIM], CUTS_EVENT, [(e, last * events + (e ^ 2)) for e in range(events)]
+    )
+    wrap_own = lax.ppermute(keep[:RIM] + near_keep[:RIM], CUTS, [(0, last)])
+    side = ((RIM, rows, lats), jnp.float32)
+    tail, head = call(latitude_kernel, [side, side], 2 * 4 * lats * size, 16 * size)(
+        keep, near_keep, far, high, low
+    )
+    left = shifted(tail, CUTS, 1)
+    right = shifted(head, CUTS, -1)
+    wrap_left = lax.ppermute(tail, CUTS, [(last, 0)])
+    changes, gram = call(
         gram_kernel,
-        [(steps.shape, jnp.float32), ((8, LANES), jnp.float32), square, square],
+        [(steps.shape, jnp.float32), ((8, LANES), jnp.float32)],
         2 * 100 * size,
         12 * steps.size,
-    )(steps, curvature)
-    side = ((RIM, rows, lats), jnp.float32)
-    head, tail = call(latitude_kernel, [side, side], 2 * 4 * lats * size, 16 * size)(
-        keep, near, far, high, low
-    )
-    left = shifted(tail, CUTS, 1)
-    right = shifted(head, CUTS, -1)
-    devices = lax.axis_size(CUTS_EVENT)
-    gradient, kept, outgoing = call(
+    )(steps, held_curvature)
+    gradient, outgoing = call(
         product_kernel,
-        [block, block, ((devices, 1, LANES), jnp.float32)],
+        [block, ((cuts * events, 1, LANES), jnp.float32)],
         2 * 30 * size,
         4 * 20 * size,
-    )(head, tail, left, right, steps, changes, gram)
+        scratch_shapes=[pltpu.VMEM((RIM, rows, lats), jnp.float32)],
+    )(head, tail, left, wrap_left, right, wrap_own, wrap_other, high, low, steps, changes, gram)
     arrived = lax.all_to_all(outgoing, CUTS_EVENT, 0, 0, tiled=True)
-    (direction,) = call(direction_kernel, [block], 2 * 17 * size, 4 * 18 * size)(
-        arrived, kept, steps, changes
-    )
-    return (gradient, direction)
+    return call(
+        direction_kernel,
+        [block] * 2,
+        2 * 17 * size,
+        4 * 18 * size,
+        out_specs=[pl.BlockSpec(memory_space=pltpu.HBM)] * 2,
+        scratch_shapes=[pltpu.VMEM((lons, rows, lats), jnp.float32), pltpu.SemaphoreType.DMA((5,))],
+    )(arrived, gradient, steps, changes)
 
 
 def solution(mesh):

time: 50.3 us -> 52 us (1.034)
  starting transfers between devices: 11.7 us -> 20.5 us
  waiting for transfers between devices: 11.5 us -> 5.69 us
  local copies, waits for them, and re-layouts: 3.18 us -> 0.02 us
  blocking collectives: 15.1 us -> 16.7 us
    ppermute x4 -> x8, starting transfers between devices: 11.7 us -> 20.5 us  [the longest x1 10.3 us: shards(): wrap_own = lax.ppermute(keep[:RIM] + near_keep[:RIM], CUTS, [(0, last)])]
    ppermute x4 -> x8, waiting for transfers between devices: 11.5 us -> 5.69 us  [the longest x1 4.6 us: shards(): wrap_left = lax.ppermute(tail, CUTS, [(last, 0)])]
    unnamed x6 -> x2, local copies, waits for them, and re-layouts: 3.18 us -> 0.01 us
    all_to_all x1, blocking collectives: 15.1 us -> 16.7 us  [shards(): arrived = lax.all_to_all(outgoing, CUTS_EVENT, 0, 0, tiled=True)]
    pallas_call x4 -> x5, Pallas kernels: 7.5 us -> 7.66 us  [the longest x1 2.41 us: shards(): call(gram_kernel, [(steps.shape, jnp.float32), ((8, LANES), jnp.float32)]...]
  transfers between devices with their start and end apart: 4 -> 8, of which waited for: 4 -> 2; matrix products, arithmetic and copies ran while one was open for 0% -> 0% of each run, Pallas kernels for 5% -> 8%
where the time goes in v5:
time: 52 us; the launch traced here: 51.7 us
  starting transfers between devices  20.5 us (39%)
  blocking collectives  16.7 us (32%)
  Pallas kernels  7.96 us (15%)
  waiting for transfers between devices  5.69 us (11%)
  between operations  0.78 us (2%)
    all_to_all x1, blocking collectives, shards(): arrived = lax.all_to_all(outgoing, CUTS_EVENT, 0, 0, tiled=True)  16.7 us
    ppermute x1, starting transfers between devices, shards(): wrap_own = lax.ppermute(keep[:RIM] + near_keep[:RIM], CUTS, [(0, last)])  10.3 us
    ppermute x2, starting transfers between devices, shifted(): lax.ppermute(x, axis, [(i, i + shift) for i in range(count) if 0 <= i + s...  4.66 us
    ppermute x1, waiting for transfers between devices, shards(): wrap_left = lax.ppermute(tail, CUTS, [(last, 0)])  4.6 us
    ppermute x3, starting transfers between devices, swapped(): return lax.ppermute(x, axis, [(0, 1), (1, 0)])  2.96 us
    pallas_call x1, Pallas kernels, shards(): call(gram_kernel, [(steps.shape, jnp.float32), ((8, LANES), jnp.float32)]...  2.41 us
    pallas_call x1, Pallas kernels, shards(): call(radial_kernel, [block] * 4, 2 * 4 * rad_len * kernels.size, 8 * kern...  1.67 us
    pallas_call x1, Pallas kernels, shards(): call(fetch_kernel, [(curvature.shape, jnp.float32), square, square], 10 *...  1.6 us
  transfers between devices with their start and end apart: 8, of which 2 were waited for; matrix products, arithmetic and copies ran while one was open for 0% of the time, Pallas kernels for 8%

profile of v5, /device:TPU:1, one launch (start us, length us, event | category | flops | bytes accessed | tf_op | source)
XLA Modules:
  0.0 51.7 jit_solution(17983157742521193604)
XLA Ops:
  0.6 1.7 %shard_map.50 = (f32[8,32,256]{2,1,0:T(8,128)S(1)}, f32[8,32,256]{2,1,0:T(8,128)S(1)}, f32[8,32,256]{2,1,0:T(8,128)S(1)}, f32[8,32,256]{2,1,0:T(8,128)S(1)}) custom-call(f32[1,8,128,256]{3,2,1,0:T(8,128)} %kernels_ref.1), custom_call_target="tpu_custom_call" | custom-call | flops 268435456 | bytes 2097152 | tf_op jit(solution)/shard_map/pallas_call | solution.py:299
  2.3 1.5 %collective-permute-start.1 = (f32[8,32,256]{2,1,0:T(8,128)S(1)}, f32[8,32,256]{2,1,0:T(8,128)S(1)}, u32[]{:S(2)}, u32[]{:S(2)}) collective-permute-start(f32[8,32,256]{2,1,0:T(8,128)S(1)} %get-tuple-element.18), channel_id=1, source_target_pairs={{0,1},{1,0},{2,3},{3,2},{4,5},{5,4},{6,7},{7,6},{8,9},{9,8},{10,11... | collective-permute-start | bytes 786440 | tf_op jit(solution)/shard_map/ppermute | solution.py:284
  3.8 0.1 collective-permute-start
  3.9 1.1 %collective-permute-done.1 = f32[8,32,256]{2,1,0:T(8,128)S(1)} collective-permute-done((f32[8,32,256]{2,1,0:T(8,128)S(1)}, f32[8,32,256]{2,1,0:T(8,128)S(1)}, u32[]{:S(2)}, u32[]{:S(2)}) %collective-permute-start.1) | collective-permute-done | bytes 262176 | tf_op jit(solution)/shard_map/ppermute | solution.py:284
  5.0 0.0 copy-start
  5.0 1.4 %collective-permute-start.2 = (f32[8,32,256]{2,1,0:T(8,128)S(1)}, f32[8,32,256]{2,1,0:T(8,128)S(1)}, u32[]{:S(2)}, u32[]{:S(2)}) collective-permute-start(f32[8,32,256]{2,1,0:T(8,128)S(1)} %add.6), channel_id=1, source_target_pairs={{0,2},{2,0},{1,3},{3,1},{4,6},{6,4},{5,7},{7,5},{8,10},{10,8},{9,1... | collective-permute-start | bytes 786440 | tf_op jit(solution)/shard_map/ppermute | solution.py:284
  6.4 1.6 %shard_map.51 = (f32[8,8,32,256]{3,2,1,0:T(8,128)S(1)}, bf16[256,256]{1,0:T(8,128)(2,1)S(1)}, bf16[256,256]{1,0:T(8,128)(2,1)S(1)}) custom-call(f32[8,8,32,256]{3,2,1,0:T(8,128)} %curvature_ref.1), custom_call_target="tpu_custom_call" | custom-call | flops 655360 | bytes 4194304 | tf_op jit(solution)/shard_map/pallas_call | solution.py:312
  8.0 0.0 collective-permute-done.near_ref
  8.0 10.3 %collective-permute-start.6 = (f32[4,32,256]{2,1,0:T(8,128)S(1)}, f32[4,32,256]{2,1,0:T(8,128)S(1)}, u32[]{:S(2)}, u32[]{:S(2)}) collective-permute-start(f32[4,32,256]{2,1,0:T(8,128)S(1)} %slice_add_fusion), channel_id=1, source_target_pairs={{0,124},{1,125},{2,126},{3,127}} | collective-permute-start | bytes 393224 | tf_op jit(solution)/shard_map/ppermute | solution.py:325
  18.3 1.3 %collective-permute-start.7 = (f32[4,32,256]{2,1,0:T(8,128)S(1)}, f32[4,32,256]{2,1,0:T(8,128)S(1)}, u32[]{:S(2)}, u32[]{:S(2)}) collective-permute-start(f32[4,32,256]{2,1,0:T(8,128)S(1)} %slice.13), channel_id=1, source_target_pairs={{0,126},{1,127},{2,124},{3,125}} | collective-permute-start | bytes 393224 | tf_op jit(solution)/shard_map/ppermute | solution.py:322
  19.6 0.0 collective-permute-done.2.far_ref
  19.7 0.3 shard_map.52
  20.0 1.3 %collective-permute-start.5 = (f32[4,32,256]{2,1,0:T(8,128)S(1)}, f32[4,32,256]{2,1,0:T(8,128)S(1)}, u32[]{:S(2)}, u32[]{:S(2)}) collective-permute-start(f32[4,32,256]{2,1,0:T(8,128)S(1)} %get-tuple-element.21.head_ref), channel_id=1, source_target_pairs={{4,0},{8,4},{12,8},{16,12},{20,16},{24,20},{28,24},{32,28},{36,32}... | collective-permute-start | bytes 393224 | tf_op jit(solution)/shard_map/ppermute | solution.py:280
  21.3 1.3 %collective-permute-start.4 = (f32[4,32,256]{2,1,0:T(8,128)S(1)}, f32[4,32,256]{2,1,0:T(8,128)S(1)}, u32[]{:S(2)}, u32[]{:S(2)}) collective-permute-start(f32[4,32,256]{2,1,0:T(8,128)S(1)} %get-tuple-element.22.tail_ref), channel_id=1, source_target_pairs={{124,0},{125,1},{126,2},{127,3}} | collective-permute-start | bytes 393224 | tf_op jit(solution)/shard_map/ppermute | solution.py:332
  22.6 3.4 %collective-permute-start.3 = (f32[4,32,256]{2,1,0:T(8,128)S(1)}, f32[4,32,256]{2,1,0:T(8,128)S(1)}, u32[]{:S(2)}, u32[]{:S(2)}) collective-permute-start(f32[4,32,256]{2,1,0:T(8,128)S(1)} %get-tuple-element.22.tail_ref), channel_id=1, source_target_pairs={{0,4},{4,8},{8,12},{12,16},{16,20},{20,24},{24,28},{28,32},{32,36}... | collective-permute-start | bytes 393224 | tf_op jit(solution)/shard_map/ppermute | solution.py:280
  25.9 0.0 copy-done
  26.0 2.4 %shard_map.53 = (f32[8,8,32,256]{3,2,1,0:T(8,128)S(1)}, f32[8,128]{1,0:T(8,128)S(1)}) custom-call(f32[8,8,32,256]{3,2,1,0:T(8,128)S(1)} %copy-done, f32[8,8,32,256]{3,2,1,0:T(8,128)S(1)} %get-tuple-element.23.curvature_ref), custom_call_target="tpu_custom_call" | custom-call | flops 13107200 | bytes 6291456 | tf_op jit(solution)/shard_map/pallas_call | solution.py:333
  28.4 0.0 collective-permute-done.6.wrap_own_ref
  28.4 0.0 collective-permute-done.7.wrap_other_ref
  28.4 0.0 collective-permute-done.5.right_ref
  28.4 4.6 %collective-permute-done.4.wrap_left_ref = f32[4,32,256]{2,1,0:T(8,128)S(1)} collective-permute-done((f32[4,32,256]{2,1,0:T(8,128)S(1)}, f32[4,32,256]{2,1,0:T(8,128)S(1)}, u32[]{:S(2)}, u32[]{:S(2)}) %collective-permute-start.4) | collective-permute-done | bytes 131104 | tf_op jit(solution)/shard_map/ppermute | solution.py:332
  33.0 0.0 collective-permute-done.3.left_ref
  33.0 0.7 %shard_map.54 = (f32[8,32,256]{2,1,0:T(8,128)S(1)}, f32[128,1,128]{2,1,0:T(1,128)S(1)}) custom-call(f32[4,32,256]{2,1,0:T(8,128)S(1)} %get-tuple-element.21.head_ref, f32[4,32,256]{2,1,0:T(8,128)S(1)} %get-tuple-element.22.tail_ref, f32[4,32,256]{2,1,0:T(8,128)S(1)} %collective-permute-done.3.left_ref, ...), custom_call_target="tpu_custom_call" | custom-call | flops 3932160 | bytes 5242880 | tf_op jit(solution)/shard_map/pallas_call | solution.py:339
  33.7 16.7 %all_to_all.5.rows_ref = f32[128,1,128]{2,1,0:T(1,128)S(1)} all-to-all(f32[128,1,128]{2,1,0:T(1,128)S(1)} %get-tuple-element.26), channel_id=1, replica_groups=mesh['cuts_0'=2,'cuts_1'=4,'cuts_2'=4,'event_0'=2,'event_1'=2] {'cuts_0'..., dimensions={0} | all-to-all | bytes 131072 | tf_op jit(solution)/shard_map/all_to_all | solution.py:346
  50.5 1.3 %shard_map.55 = (f32[8,32,256]{2,1,0:T(8,128)}, f32[8,32,256]{2,1,0:T(8,128)}) custom-call(f32[128,1,128]{2,1,0:T(1,128)S(1)} %all_to_all.5.rows_ref, f32[8,32,256]{2,1,0:T(8,128)S(1)} %get-tuple-element.27.gradient_ref, f32[8,8,32,256]{3,2,1,0:T(8,128)S(1)} %copy-done, f32[8,8,32,256]{3,2,1,0:T(8,128)S(1)} %get-tuple-element.24.changes_ref), custom_call_target="tpu_custom_call" | custom-call | flops 2228224 | bytes 4718592 | tf_op jit(solution)/shard_map/pallas_call | solution.py:347
  (3 shorter events, 0.1 us)
Async XLA Ops:
  2.3 2.6 %collective-permute-start.1 = (f32[8,32,256]{2,1,0:T(8,128)S(1)}, f32[8,32,256]{2,1,0:T(8,128)S(1)}, u32[]{:S(2)}, u32[]{:S(2)}) collective-permute-start(f32[8,32,256]{2,1,0:T(8,128)S(1)} %get-tuple-element.18), channel_id=1, source_target_pairs={{0,1},{1,0},{2,3},{3,2},{4,5},{5,4},{6,7},{7,6},{8,9},{9,8},{10,11... | collective-permute-start | bytes 786440 | tf_op jit(solution)/shard_map/ppermute | solution.py:284
  3.8 4.2 %collective-permute-start = (f32[8,32,256]{2,1,0:T(8,128)S(1)}, f32[8,32,256]{2,1,0:T(8,128)S(1)}, u32[]{:S(2)}, u32[]{:S(2)}) collective-permute-start(f32[8,32,256]{2,1,0:T(8,128)S(1)} %get-tuple-element.16), channel_id=1, source_target_pairs={{0,1},{1,0},{2,3},{3,2},{4,5},{5,4},{6,7},{7,6},{8,9},{9,8},{10,11... | collective-permute-start | bytes 786440 | tf_op jit(solution)/shard_map/ppermute | solution.py:284
  5.0 21.0 %copy-start = (f32[8,8,32,256]{3,2,1,0:T(8,128)S(1)}, f32[8,8,32,256]{3,2,1,0:T(8,128)}, u32[]{:S(2)}) copy-start(f32[8,8,32,256]{3,2,1,0:T(8,128)} %steps_ref.5) | copy-start | bytes 6291460
  5.0 14.7 %collective-permute-start.2 = (f32[8,32,256]{2,1,0:T(8,128)S(1)}, f32[8,32,256]{2,1,0:T(8,128)S(1)}, u32[]{:S(2)}, u32[]{:S(2)}) collective-permute-start(f32[8,32,256]{2,1,0:T(8,128)S(1)} %add.6), channel_id=1, source_target_pairs={{0,2},{2,0},{1,3},{3,1},{4,6},{6,4},{5,7},{7,5},{8,10},{10,8},{9,1... | collective-permute-start | bytes 786440 | tf_op jit(solution)/shard_map/ppermute | solution.py:284
  8.0 20.3 %collective-permute-start.6 = (f32[4,32,256]{2,1,0:T(8,128)S(1)}, f32[4,32,256]{2,1,0:T(8,128)S(1)}, u32[]{:S(2)}, u32[]{:S(2)}) collective-permute-start(f32[4,32,256]{2,1,0:T(8,128)S(1)} %slice_add_fusion), channel_id=1, source_target_pairs={{0,124},{1,125},{2,126},{3,127}} | collective-permute-start | bytes 393224 | tf_op jit(solution)/shard_map/ppermute | solution.py:325
  18.3 10.0 %collective-permute-start.7 = (f32[4,32,256]{2,1,0:T(8,128)S(1)}, f32[4,32,256]{2,1,0:T(8,128)S(1)}, u32[]{:S(2)}, u32[]{:S(2)}) collective-permute-start(f32[4,32,256]{2,1,0:T(8,128)S(1)} %slice.13), channel_id=1, source_target_pairs={{0,126},{1,127},{2,124},{3,125}} | collective-permute-start | bytes 393224 | tf_op jit(solution)/shard_map/ppermute | solution.py:322
  20.0 8.4 %collective-permute-start.5 = (f32[4,32,256]{2,1,0:T(8,128)S(1)}, f32[4,32,256]{2,1,0:T(8,128)S(1)}, u32[]{:S(2)}, u32[]{:S(2)}) collective-permute-start(f32[4,32,256]{2,1,0:T(8,128)S(1)} %get-tuple-element.21.head_ref), channel_id=1, source_target_pairs={{4,0},{8,4},{12,8},{16,12},{20,16},{24,20},{28,24},{32,28},{36,32}... | collective-permute-start | bytes 393224 | tf_op jit(solution)/shard_map/ppermute | solution.py:280
  21.3 11.7 %collective-permute-start.4 = (f32[4,32,256]{2,1,0:T(8,128)S(1)}, f32[4,32,256]{2,1,0:T(8,128)S(1)}, u32[]{:S(2)}, u32[]{:S(2)}) collective-permute-start(f32[4,32,256]{2,1,0:T(8,128)S(1)} %get-tuple-element.22.tail_ref), channel_id=1, source_target_pairs={{124,0},{125,1},{126,2},{127,3}} | collective-permute-start | bytes 393224 | tf_op jit(solution)/shard_map/ppermute | solution.py:332
  22.6 10.4 %collective-permute-start.3 = (f32[4,32,256]{2,1,0:T(8,128)S(1)}, f32[4,32,256]{2,1,0:T(8,128)S(1)}, u32[]{:S(2)}, u32[]{:S(2)}) collective-permute-start(f32[4,32,256]{2,1,0:T(8,128)S(1)} %get-tuple-element.22.tail_ref), channel_id=1, source_target_pairs={{0,4},{4,8},{8,12},{12,16},{16,20},{20,24},{24,28},{28,32},{32,36}... | collective-permute-start | bytes 393224 | tf_op jit(solution)/shard_map/ppermute | solution.py:280

commit v6 on v5

--- a/solution.py
+++ b/solution.py
@@ -99,12 +99,30 @@
     copy.wait()
 
 
-def latitude_kernel(keep_ref, near_ref, far_ref, high_ref, low_ref, tail_ref, head_ref):
+def edge_kernel(keep_ref, near_ref, passed_ref, own_ref, other_ref):
+    lons = keep_ref.shape[0]
+    start = jnp.where(cut_number() == lax.axis_size(CUTS) - 1, lons - RIM, 0)
+    for a in range(RIM):
+        own_ref[a] = keep_ref[start + a] + near_ref[start + a]
+        other_ref[a] = passed_ref[start + a]
+
+
+def latitude_kernel(keep_ref, near_ref, far_ref, high_ref, low_ref, plane_ref, first_ref, second_ref):
     lons, rows, lats = keep_ref.shape
     summed = (keep_ref[...] + near_ref[...] + far_ref[...]).reshape(lons * rows, lats)
     plane = smoothed(summed, high_ref[...], low_ref[...]).reshape(lons, rows, lats)
-    head_ref[...] = plane[:RIM]
-    tail_ref[...] = plane[lons - RIM :]
+    plane_ref[...] = plane
+    odd = lax.rem(cut_number(), 2) == 1
+
+    @pl.when(odd)
+    def _():
+        first_ref[...] = plane[:RIM]
+        second_ref[...] = plane[lons - RIM :]
+
+    @pl.when(jnp.logical_not(odd))
+    def _():
+        first_ref[...] = plane[lons - RIM :]
+        second_ref[...] = plane[:RIM]
 
 
 def lane_numbers():
@@ -171,30 +189,28 @@
 
 
 def product_kernel(
-    head_ref, tail_ref, left_ref, wrap_left_ref, right_ref, wrap_own_ref, wrap_other_ref,
-    high_ref, low_ref, steps_ref, changes_ref, gram_ref, gradient_ref, rows_ref, right_scratch,
+    plane_ref, first_ref, second_ref, wrap_own_ref, wrap_other_ref, high_ref, low_ref,
+    steps_ref, changes_ref, gram_ref, gradient_ref, rows_ref, halo,
 ):
     lons, rows, lats = gradient_ref.shape
     weights = cycle_weights()
-    cut = cut_number()
-    last = lax.axis_size(CUTS) - 1
-
-    @pl.when(cut == last)
+    cut, last = cut_number(), lax.axis_size(CUTS) - 1
+    odd = lax.rem(cut, 2)
+    halo[odd ^ 1] = first_ref[...]
+    halo[odd] = second_ref[...]
+
+    @pl.when(jnp.logical_or(cut == 0, cut == last))
     def _():
         summed = (wrap_own_ref[...] + wrap_other_ref[...]).reshape(RIM * rows, lats)
-        plane = smoothed(summed, high_ref[...], low_ref[...])
-        right_scratch[...] = plane.reshape(RIM, rows, lats)
-
-    @pl.when(cut != last)
-    def _():
-        right_scratch[...] = right_ref[...]
+        halo[odd] = smoothed(summed, high_ref[...], low_ref[...]).reshape(RIM, rows, lats)
 
     sums = [jnp.zeros((8, LANES), jnp.float32) for _ in range(2 * PAIRS)]
     for r in range(rows // 8):
         for b in range(lats // LANES):
             at = (slice(8 * r, 8 * r + 8), slice(LANES * b, LANES * (b + 1)))
-            padded = [left_ref[(a, *at)] + wrap_left_ref[(a, *at)] for a in range(RIM)]
-            padded += [ref[(a, *at)] for ref in (head_ref, tail_ref, right_scratch) for a in range(RIM)]
+            padded = [halo[(0, a, *at)] for a in range(RIM)]
+            padded += [plane_ref[(a, *at)] for a in range(lons)]
+            padded += [halo[(1, a, *at)] for a in range(RIM)]
             for a in range(lons):
                 value = weights[RIM] * padded[a + RIM]
                 for k in range(RIM):
@@ -275,11 +291,6 @@
     return pltpu.with_memory_space_constraint(x, pltpu.HBM)
 
 
-def shifted(x, axis, shift):
-    count = lax.axis_size(axis)
-    return lax.ppermute(x, axis, [(i, i + shift) for i in range(count) if 0 <= i + shift < count])
-
-
 def swapped(x, axis):
     return lax.ppermute(x, axis, [(0, 1), (1, 0)])
 
@@ -319,17 +330,23 @@
     )(in_hbm(curvature))
     cuts, last = lax.axis_size(CUTS), lax.axis_size(CUTS) - 1
     events = lax.axis_size(EVENT)
-    wrap_other = lax.ppermute(
-        passed[:RIM], CUTS_EVENT, [(e, last * events + (e ^ 2)) for e in range(events)]
-    )
-    wrap_own = lax.ppermute(keep[:RIM] + near_keep[:RIM], CUTS, [(0, last)])
+    inner = [(c * events + e, c * events + e) for c in range(1, last) for e in range(events)]
     side = ((RIM, rows, lats), jnp.float32)
-    tail, head = call(latitude_kernel, [side, side], 2 * 4 * lats * size, 16 * size)(
-        keep, near_keep, far, high, low
-    )
-    left = shifted(tail, CUTS, 1)
-    right = shifted(head, CUTS, -1)
-    wrap_left = lax.ppermute(tail, CUTS, [(last, 0)])
+    edge_own, edge_other = call(edge_kernel, [side, side], size, 12 * size)(keep, near_keep, passed)
+
+    def wrapped(x, flip):
+        ends = [(e, last * events + (e ^ flip)) for e in range(events)]
+        return lax.ppermute(x, CUTS_EVENT, ends + [two[::-1] for two in ends] + inner)
+
+    wrap_other = wrapped(edge_other, 2)
+    wrap_own = wrapped(edge_own, 0)
+    plane, first, second = call(
+        latitude_kernel, [block, side, side], 2 * 4 * lats * size, 16 * size
+    )(keep, near_keep, far, high, low)
+    first = lax.ppermute(first, CUTS, [(c, c ^ 1) for c in range(cuts)])
+    second = lax.ppermute(
+        second, CUTS, [(0, 0), (last, last)] + [(c, ((c - 1) ^ 1) + 1) for c in range(1, last)]
+    )
     changes, gram = call(
         gram_kernel,
         [(steps.shape, jnp.float32), ((8, LANES), jnp.float32)],
@@ -341,8 +358,8 @@
         [block, ((cuts * events, 1, LANES), jnp.float32)],
         2 * 30 * size,
         4 * 20 * size,
-        scratch_shapes=[pltpu.VMEM((RIM, rows, lats), jnp.float32)],
-    )(head, tail, left, wrap_left, right, wrap_own, wrap_other, high, low, steps, changes, gram)
+        scratch_shapes=[pltpu.VMEM((2, RIM, rows, lats), jnp.float32)],
+    )(plane, first, second, wrap_own, wrap_other, high, low, steps, changes, gram)
     arrived = lax.all_to_all(outgoing, CUTS_EVENT, 0, 0, tiled=True)
     return call(
         direction_kernel,

time: 52 us -> 49.9 us (0.960)
  starting transfers between devices: 20.5 us -> 15.9 us
  waiting for transfers between devices: 5.69 us -> 7.05 us
  blocking collectives: 16.7 us -> 17.6 us
    ppermute x5 -> x4, starting transfers between devices: 17.5 us -> 13 us  [the longest x2 12.2 us: wrapped(): lax.ppermute(x, CUTS_EVENT, ends + [two[::-1] for two in ends] + inner)]
    ppermute x5 -> x4, waiting for transfers between devices: 4.61 us -> 5.98 us  [the longest x2 5.97 us: wrapped(): lax.ppermute(x, CUTS_EVENT, ends + [two[::-1] for two in ends] + inner)]
    all_to_all x1, blocking collectives: 16.7 us -> 17.6 us  [shards(): arrived = lax.all_to_all(outgoing, CUTS_EVENT, 0, 0, tiled=True)]
  transfers between devices with their start and end apart: 8 -> 7, of which waited for: 2 -> 2; matrix products, arithmetic and copies ran while one was open for 0% -> 0% of each run, Pallas kernels for 8% -> 9%
where the time goes in v6:
time: 49.9 us; the launch traced here: 49.6 us
  blocking collectives  17.6 us (35%)
  starting transfers between devices  15.9 us (32%)
  Pallas kernels  8.26 us (17%)
  waiting for transfers between devices  7.05 us (14%)
  between operations  0.75 us (2%)
    all_to_all x1, blocking collectives, shards(): arrived = lax.all_to_all(outgoing, CUTS_EVENT, 0, 0, tiled=True)  17.6 us
    ppermute x2, starting transfers between devices, wrapped(): lax.ppermute(x, CUTS_EVENT, ends + [two[::-1] for two in ends] + inner)  12.2 us
    ppermute x2, waiting for transfers between devices, wrapped(): lax.ppermute(x, CUTS_EVENT, ends + [two[::-1] for two in ends] + inner)  5.97 us
    ppermute x3, starting transfers between devices, swapped(): return lax.ppermute(x, axis, [(0, 1), (1, 0)])  2.96 us
    pallas_call x1, Pallas kernels, shards(): call(gram_kernel, [(steps.shape, jnp.float32), ((8, LANES), jnp.float32)]...  2.41 us
    pallas_call x1, Pallas kernels, shards(): call(radial_kernel, [block] * 4, 2 * 4 * rad_len * kernels.size, 8 * kern...  1.67 us
    pallas_call x1, Pallas kernels, shards(): call(fetch_kernel, [(curvature.shape, jnp.float32), square, square], 10 *...  1.6 us
    pallas_call x1, Pallas kernels, shards(): call(direction_kernel, [block] * 2, 2 * 17 * size, 4 * 18 * size, out_spe...  1.28 us
  transfers between devices with their start and end apart: 7, of which 2 were waited for; matrix products, arithmetic and copies ran while one was open for 0% of the time, Pallas kernels for 9%

profile of v6, /device:TPU:1, one launch (start us, length us, event | category | flops | bytes accessed | tf_op | source)
XLA Modules:
  0.0 49.6 jit_solution(6328309704471527666)
XLA Ops:
  0.6 1.7 %shard_map.50 = (f32[8,32,256]{2,1,0:T(8,128)S(1)}, f32[8,32,256]{2,1,0:T(8,128)S(1)}, f32[8,32,256]{2,1,0:T(8,128)S(1)}, f32[8,32,256]{2,1,0:T(8,128)S(1)}) custom-call(f32[1,8,128,256]{3,2,1,0:T(8,128)} %kernels_ref.1), custom_call_target="tpu_custom_call" | custom-call | flops 268435456 | bytes 2097152 | tf_op jit(solution)/shard_map/pallas_call | solution.py:310
  2.3 1.5 %collective-permute-start.1 = (f32[8,32,256]{2,1,0:T(8,128)S(1)}, f32[8,32,256]{2,1,0:T(8,128)S(1)}, u32[]{:S(2)}, u32[]{:S(2)}) collective-permute-start(f32[8,32,256]{2,1,0:T(8,128)S(1)} %get-tuple-element.21), channel_id=1, source_target_pairs={{0,1},{1,0},{2,3},{3,2},{4,5},{5,4},{6,7},{7,6},{8,9},{9,8},{10,11... | collective-permute-start | bytes 786440 | tf_op jit(solution)/shard_map/ppermute | solution.py:295
  3.8 0.1 collective-permute-start
  3.9 1.1 %collective-permute-done.1 = f32[8,32,256]{2,1,0:T(8,128)S(1)} collective-permute-done((f32[8,32,256]{2,1,0:T(8,128)S(1)}, f32[8,32,256]{2,1,0:T(8,128)S(1)}, u32[]{:S(2)}, u32[]{:S(2)}) %collective-permute-start.1) | collective-permute-done | bytes 262176 | tf_op jit(solution)/shard_map/ppermute | solution.py:295
  5.0 0.0 copy-start
  5.0 1.4 %collective-permute-start.2 = (f32[8,32,256]{2,1,0:T(8,128)S(1)}, f32[8,32,256]{2,1,0:T(8,128)S(1)}, u32[]{:S(2)}, u32[]{:S(2)}) collective-permute-start(f32[8,32,256]{2,1,0:T(8,128)S(1)} %add.3.passed_ref), channel_id=1, source_target_pairs={{0,2},{2,0},{1,3},{3,1},{4,6},{6,4},{5,7},{7,5},{8,10},{10,8},{9,1... | collective-permute-start | bytes 786440 | tf_op jit(solution)/shard_map/ppermute | solution.py:295
  6.4 1.6 %shard_map.51 = (f32[8,8,32,256]{3,2,1,0:T(8,128)S(1)}, bf16[256,256]{1,0:T(8,128)(2,1)S(1)}, bf16[256,256]{1,0:T(8,128)(2,1)S(1)}) custom-call(f32[8,8,32,256]{3,2,1,0:T(8,128)} %curvature_ref.1), custom_call_target="tpu_custom_call" | custom-call | flops 655360 | bytes 4194304 | tf_op jit(solution)/shard_map/pallas_call | solution.py:323
  8.0 0.0 collective-permute-done.near_ref
  8.1 10.3 %collective-permute-start.5 = (f32[4,32,256]{2,1,0:T(8,128)S(1)}, f32[4,32,256]{2,1,0:T(8,128)S(1)}, u32[]{:S(2)}, u32[]{:S(2)}) collective-permute-start(f32[4,32,256]{2,1,0:T(8,128)S(1)} %get-tuple-element.27), channel_id=1, source_target_pairs={{0,124},{1,125},{2,126},{3,127},{124,0},{125,1},{126,2},{127,3},{4... | collective-permute-start | bytes 393224 | tf_op jit(solution)/shard_map/ppermute | solution.py:339
  18.3 1.9 %collective-permute-start.6 = (f32[4,32,256]{2,1,0:T(8,128)S(1)}, f32[4,32,256]{2,1,0:T(8,128)S(1)}, u32[]{:S(2)}, u32[]{:S(2)}) collective-permute-start(f32[4,32,256]{2,1,0:T(8,128)S(1)} %get-tuple-element.28), channel_id=1, source_target_pairs={{0,126},{1,127},{2,124},{3,125},{126,0},{127,1},{124,2},{125,3},{4... | collective-permute-start | bytes 393224 | tf_op jit(solution)/shard_map/ppermute | solution.py:339
  20.3 0.0 collective-permute-done.2.far_ref
  20.3 0.3 shard_map.52
  20.6 0.1 collective-permute-start.3
  20.7 0.7 %collective-permute-start.4 = (f32[4,32,256]{2,1,0:T(8,128)S(1)}, f32[4,32,256]{2,1,0:T(8,128)S(1)}, u32[]{:S(2)}, u32[]{:S(2)}) collective-permute-start(f32[4,32,256]{2,1,0:T(8,128)S(1)} %get-tuple-element.26), channel_id=1, source_target_pairs={{0,0},{124,124},{4,8},{8,4},{12,16},{16,12},{20,24},{24,20},{28,32... | collective-permute-start | bytes 393224 | tf_op jit(solution)/shard_map/ppermute | solution.py:347
  21.4 0.0 copy-done
  21.4 2.4 %shard_map.54 = (f32[8,8,32,256]{3,2,1,0:T(8,128)S(1)}, f32[8,128]{1,0:T(8,128)S(1)}) custom-call(f32[8,8,32,256]{3,2,1,0:T(8,128)S(1)} %copy-done, f32[8,8,32,256]{3,2,1,0:T(8,128)S(1)} %get-tuple-element.29.curvature_ref), custom_call_target="tpu_custom_call" | custom-call | flops 13107200 | bytes 6291456 | tf_op jit(solution)/shard_map/pallas_call | solution.py:350
  23.8 0.0 collective-permute-done.5.wrap_own_ref
  23.8 6.0 %collective-permute-done.6.wrap_other_ref = f32[4,32,256]{2,1,0:T(8,128)S(1)} collective-permute-done((f32[4,32,256]{2,1,0:T(8,128)S(1)}, f32[4,32,256]{2,1,0:T(8,128)S(1)}, u32[]{:S(2)}, u32[]{:S(2)}) %collective-permute-start.6) | collective-permute-done | bytes 131104 | tf_op jit(solution)/shard_map/ppermute | solution.py:339
  29.8 0.0 collective-permute-done.3.first_ref
  29.8 0.0 collective-permute-done.4.second_ref
  29.8 0.9 %shard_map.55 = (f32[8,32,256]{2,1,0:T(8,128)S(1)}, f32[128,1,128]{2,1,0:T(1,128)S(1)}) custom-call(f32[8,32,256]{2,1,0:T(8,128)S(1)} %get-tuple-element.24.plane_ref, f32[4,32,256]{2,1,0:T(8,128)S(1)} %collective-permute-done.3.first_ref, f32[4,32,256]{2,1,0:T(8,128)S(1)} %collective-permute-done.4.second_ref, ...), custom_call_target="tpu_custom_call" | custom-call | flops 3932160 | bytes 5242880 | tf_op jit(solution)/shard_map/pallas_call | solution.py:356
  30.7 17.6 %all_to_all.5.rows_ref = f32[128,1,128]{2,1,0:T(1,128)S(1)} all-to-all(f32[128,1,128]{2,1,0:T(1,128)S(1)} %get-tuple-element.32), channel_id=1, replica_groups=mesh['cuts_0'=2,'cuts_1'=4,'cuts_2'=4,'event_0'=2,'event_1'=2] {'cuts_0'..., dimensions={0} | all-to-all | bytes 131072 | tf_op jit(solution)/shard_map/all_to_all | solution.py:363
  48.4 1.3 %shard_map.56 = (f32[8,32,256]{2,1,0:T(8,128)}, f32[8,32,256]{2,1,0:T(8,128)}) custom-call(f32[128,1,128]{2,1,0:T(1,128)S(1)} %all_to_all.5.rows_ref, f32[8,32,256]{2,1,0:T(8,128)S(1)} %get-tuple-element.33.gradient_ref, f32[8,8,32,256]{3,2,1,0:T(8,128)S(1)} %copy-done, f32[8,8,32,256]{3,2,1,0:T(8,128)S(1)} %get-tuple-element.30.changes_ref), custom_call_target="tpu_custom_call" | custom-call | flops 2228224 | bytes 4718592 | tf_op jit(solution)/shard_map/pallas_call | solution.py:364
  (2 shorter events, 0.1 us)
Async XLA Ops:
  2.3 2.6 %collective-permute-start.1 = (f32[8,32,256]{2,1,0:T(8,128)S(1)}, f32[8,32,256]{2,1,0:T(8,128)S(1)}, u32[]{:S(2)}, u32[]{:S(2)}) collective-permute-start(f32[8,32,256]{2,1,0:T(8,128)S(1)} %get-tuple-element.21), channel_id=1, source_target_pairs={{0,1},{1,0},{2,3},{3,2},{4,5},{5,4},{6,7},{7,6},{8,9},{9,8},{10,11... | collective-permute-start | bytes 786440 | tf_op jit(solution)/shard_map/ppermute | solution.py:295
  3.8 4.2 %collective-permute-start = (f32[8,32,256]{2,1,0:T(8,128)S(1)}, f32[8,32,256]{2,1,0:T(8,128)S(1)}, u32[]{:S(2)}, u32[]{:S(2)}) collective-permute-start(f32[8,32,256]{2,1,0:T(8,128)S(1)} %get-tuple-element.19), channel_id=1, source_target_pairs={{0,1},{1,0},{2,3},{3,2},{4,5},{5,4},{6,7},{7,6},{8,9},{9,8},{10,11... | collective-permute-start | bytes 786440 | tf_op jit(solution)/shard_map/ppermute | solution.py:295
  5.0 16.4 %copy-start = (f32[8,8,32,256]{3,2,1,0:T(8,128)S(1)}, f32[8,8,32,256]{3,2,1,0:T(8,128)}, u32[]{:S(2)}) copy-start(f32[8,8,32,256]{3,2,1,0:T(8,128)} %steps_ref.5) | copy-start | bytes 6291460
  5.0 15.3 %collective-permute-start.2 = (f32[8,32,256]{2,1,0:T(8,128)S(1)}, f32[8,32,256]{2,1,0:T(8,128)S(1)}, u32[]{:S(2)}, u32[]{:S(2)}) collective-permute-start(f32[8,32,256]{2,1,0:T(8,128)S(1)} %add.3.passed_ref), channel_id=1, source_target_pairs={{0,2},{2,0},{1,3},{3,1},{4,6},{6,4},{5,7},{7,5},{8,10},{10,8},{9,1... | collective-permute-start | bytes 786440 | tf_op jit(solution)/shard_map/ppermute | solution.py:295
  8.1 15.8 %collective-permute-start.5 = (f32[4,32,256]{2,1,0:T(8,128)S(1)}, f32[4,32,256]{2,1,0:T(8,128)S(1)}, u32[]{:S(2)}, u32[]{:S(2)}) collective-permute-start(f32[4,32,256]{2,1,0:T(8,128)S(1)} %get-tuple-element.27), channel_id=1, source_target_pairs={{0,124},{1,125},{2,126},{3,127},{124,0},{125,1},{126,2},{127,3},{4... | collective-permute-start | bytes 393224 | tf_op jit(solution)/shard_map/ppermute | solution.py:339
  18.3 11.4 %collective-permute-start.6 = (f32[4,32,256]{2,1,0:T(8,128)S(1)}, f32[4,32,256]{2,1,0:T(8,128)S(1)}, u32[]{:S(2)}, u32[]{:S(2)}) collective-permute-start(f32[4,32,256]{2,1,0:T(8,128)S(1)} %get-tuple-element.28), channel_id=1, source_target_pairs={{0,126},{1,127},{2,124},{3,125},{126,0},{127,1},{124,2},{125,3},{4... | collective-permute-start | bytes 393224 | tf_op jit(solution)/shard_map/ppermute | solution.py:339
  20.6 9.2 %collective-permute-start.3 = (f32[4,32,256]{2,1,0:T(8,128)S(1)}, f32[4,32,256]{2,1,0:T(8,128)S(1)}, u32[]{:S(2)}, u32[]{:S(2)}) collective-permute-start(f32[4,32,256]{2,1,0:T(8,128)S(1)} %get-tuple-element.25), channel_id=1, source_target_pairs={{0,4},{4,0},{8,12},{12,8},{16,20},{20,16},{24,28},{28,24},{32,36},... | collective-permute-start | bytes 393224 | tf_op jit(solution)/shard_map/ppermute | solution.py:346
  20.7 9.1 %collective-permute-start.4 = (f32[4,32,256]{2,1,0:T(8,128)S(1)}, f32[4,32,256]{2,1,0:T(8,128)S(1)}, u32[]{:S(2)}, u32[]{:S(2)}) collective-permute-start(f32[4,32,256]{2,1,0:T(8,128)S(1)} %get-tuple-element.26), channel_id=1, source_target_pairs={{0,0},{124,124},{4,8},{8,4},{12,16},{16,12},{20,24},{24,20},{28,32... | collective-permute-start | bytes 393224 | tf_op jit(solution)/shard_map/ppermute | solution.py:347

commit v7 on v5

--- a/solution.py
+++ b/solution.py
@@ -1,3 +1,4 @@
+import functools
 import math
 
 import jax
@@ -55,14 +56,19 @@
     return matrix / jnp.sum(matrix, axis=axis, keepdims=True)
 
 
-def radial_kernel(kernels_ref, keep_ref, pass_ref, send_keep_ref, send_pass_ref, held_ref, semaphores):
-    _, lons, length, _ = kernels_ref.shape
-    half = lons // 2
+def radial_kernel(
+    kernels_ref, keep_ref, pass_far_ref, pass_near_ref, send_keep_ref, send_pass_ref, held_ref, semaphores
+):
+    _, _, length, _ = kernels_ref.shape
+    odd = lax.rem(cut_number(), 2)
     copies = []
     for piece in range(2):
-        at = slice(piece * half, piece * half + half)
         copies.append(
-            pltpu.make_async_copy(kernels_ref.at[0, at], held_ref.at[at], semaphores.at[piece])
+            pltpu.make_async_copy(
+                kernels_ref.at[0, pl.ds(RIM * (odd ^ piece), RIM)],
+                held_ref.at[pl.ds(RIM * piece, RIM)],
+                semaphores.at[piece],
+            )
         )
         copies[piece].start()
     part = 2 * lax.axis_index("event_0") + lax.axis_index("event_1")
@@ -73,14 +79,16 @@
         [gauss_rows(length, 3.0, local + rows * block, 1) for block in order], axis=0
     )
     weights = jnp.concatenate([jnp.concatenate([m, m], axis=1) for m in split(matrix)], axis=0)
-    outs = (keep_ref, pass_ref, send_keep_ref, send_pass_ref)
     for piece in range(2):
         copies[piece].wait()
-        for a in range(piece * half, piece * half + half):
-            both = dot(weights, jnp.concatenate(split(held_ref[a]), axis=0))
+        for a in range(RIM):
+            at = piece * RIM + a
+            both = dot(weights, jnp.concatenate(split(held_ref[at]), axis=0))
             out = both[:length] + both[length:]
-            for k, ref in enumerate(outs):
-                ref[a] = out[k * rows : (k + 1) * rows]
+            keep_ref[at] = out[:rows]
+            (pass_far_ref, pass_near_ref)[piece][a] = out[rows : 2 * rows]
+            send_keep_ref[at] = out[2 * rows : 3 * rows]
+            send_pass_ref[at] = out[3 * rows :]
 
 
 def smoothed(field, high, low):
@@ -99,12 +107,11 @@
     copy.wait()
 
 
-def latitude_kernel(keep_ref, near_ref, far_ref, high_ref, low_ref, tail_ref, head_ref):
-    lons, rows, lats = keep_ref.shape
-    summed = (keep_ref[...] + near_ref[...] + far_ref[...]).reshape(lons * rows, lats)
-    plane = smoothed(summed, high_ref[...], low_ref[...]).reshape(lons, rows, lats)
-    head_ref[...] = plane[:RIM]
-    tail_ref[...] = plane[lons - RIM :]
+def latitude_kernel(start, keep_ref, near_ref, far_ref, high_ref, low_ref, plane_ref):
+    lons, rows, lats = plane_ref.shape
+    at = slice(start, start + lons)
+    summed = (keep_ref[at] + near_ref[at] + far_ref[...]).reshape(lons * rows, lats)
+    plane_ref[...] = smoothed(summed, high_ref[...], low_ref[...]).reshape(lons, rows, lats)
 
 
 def lane_numbers():
@@ -171,30 +178,19 @@
 
 
 def product_kernel(
-    head_ref, tail_ref, left_ref, wrap_left_ref, right_ref, wrap_own_ref, wrap_other_ref,
-    high_ref, low_ref, steps_ref, changes_ref, gram_ref, gradient_ref, rows_ref, right_scratch,
+    far_halo_ref, far_ref, near_ref, near_halo_ref,
+    steps_ref, changes_ref, gram_ref, gradient_ref, rows_ref, padded_ref,
 ):
     lons, rows, lats = gradient_ref.shape
     weights = cycle_weights()
-    cut = cut_number()
-    last = lax.axis_size(CUTS) - 1
-
-    @pl.when(cut == last)
-    def _():
-        summed = (wrap_own_ref[...] + wrap_other_ref[...]).reshape(RIM * rows, lats)
-        plane = smoothed(summed, high_ref[...], low_ref[...])
-        right_scratch[...] = plane.reshape(RIM, rows, lats)
-
-    @pl.when(cut != last)
-    def _():
-        right_scratch[...] = right_ref[...]
-
+    mirror = 3 * lax.rem(cut_number(), 2)
+    for k, ref in enumerate((far_halo_ref, far_ref, near_ref, near_halo_ref)):
+        padded_ref[k ^ mirror] = ref[...]
     sums = [jnp.zeros((8, LANES), jnp.float32) for _ in range(2 * PAIRS)]
     for r in range(rows // 8):
         for b in range(lats // LANES):
             at = (slice(8 * r, 8 * r + 8), slice(LANES * b, LANES * (b + 1)))
-            padded = [left_ref[(a, *at)] + wrap_left_ref[(a, *at)] for a in range(RIM)]
-            padded += [ref[(a, *at)] for ref in (head_ref, tail_ref, right_scratch) for a in range(RIM)]
+            padded = [padded_ref[(k, a, *at)] for k in range(4) for a in range(RIM)]
             for a in range(lons):
                 value = weights[RIM] * padded[a + RIM]
                 for k in range(RIM):
@@ -275,11 +271,6 @@
     return pltpu.with_memory_space_constraint(x, pltpu.HBM)
 
 
-def shifted(x, axis, shift):
-    count = lax.axis_size(axis)
-    return lax.ppermute(x, axis, [(i, i + shift) for i in range(count) if 0 <= i + shift < count])
-
-
 def swapped(x, axis):
     return lax.ppermute(x, axis, [(0, 1), (1, 0)])
 
@@ -296,18 +287,17 @@
     rows = rad_len // 4
     block = ((lons, rows, lats), jnp.float32)
     size = lons * rows * lats
-    keep, pass_on, send_keep, send_pass = call(
+    half = ((RIM, rows, lats), jnp.float32)
+    cuts, events = lax.axis_size(CUTS), lax.axis_size(EVENT)
+    keep, pass_far, pass_near, send_keep, send_pass = call(
         radial_kernel,
-        [block] * 4,
+        [block, half, half, block, block],
         2 * 4 * rad_len * kernels.size,
         8 * kernels.size,
         in_specs=[pl.BlockSpec(memory_space=pltpu.HBM)],
         scratch_shapes=[pltpu.VMEM(kernels.shape[1:], jnp.float32), pltpu.SemaphoreType.DMA((2,))],
     )(in_hbm(kernels))
     near_pass = swapped(send_pass, "event_1")
-    passed = pass_on + near_pass
-    far = swapped(passed, "event_0")
-    near_keep = swapped(send_keep, "event_1")
     square = ((lats, lats), jnp.bfloat16)
     held_curvature, high, low = call(
         fetch_kernel,
@@ -317,32 +307,34 @@
         in_specs=[pl.BlockSpec(memory_space=pltpu.HBM)],
         scratch_shapes=[pltpu.SemaphoreType.DMA],
     )(in_hbm(curvature))
-    cuts, last = lax.axis_size(CUTS), lax.axis_size(CUTS) - 1
-    events = lax.axis_size(EVENT)
-    wrap_other = lax.ppermute(
-        passed[:RIM], CUTS_EVENT, [(e, last * events + (e ^ 2)) for e in range(events)]
-    )
-    wrap_own = lax.ppermute(keep[:RIM] + near_keep[:RIM], CUTS, [(0, last)])
-    side = ((RIM, rows, lats), jnp.float32)
-    tail, head = call(latitude_kernel, [side, side], 2 * 4 * lats * size, 16 * size)(
-        keep, near_keep, far, high, low
-    )
-    left = shifted(tail, CUTS, 1)
-    right = shifted(head, CUTS, -1)
-    wrap_left = lax.ppermute(tail, CUTS, [(last, 0)])
+    far_chunk = swapped(pass_far + near_pass[:RIM], "event_0")
+    near_chunk = swapped(pass_near + near_pass[RIM:], "event_0")
+    near_keep = swapped(send_keep, "event_1")
     changes, gram = call(
         gram_kernel,
         [(steps.shape, jnp.float32), ((8, LANES), jnp.float32)],
         2 * 100 * size,
         12 * steps.size,
     )(steps, held_curvature)
+
+    def plane_of(start, chunk):
+        return call(
+            functools.partial(latitude_kernel, start), [half], 4 * lats * size, 8 * size
+        )(keep, near_keep, chunk, high, low)[0]
+
+    far_plane = plane_of(0, far_chunk)
+    far_halo = lax.ppermute(
+        far_plane, CUTS, [(c, (((c - 1) ^ 1) + 1) % cuts) for c in range(1, cuts)] + [(0, cuts - 1)]
+    )
+    near_plane = plane_of(RIM, near_chunk)
+    near_halo = lax.ppermute(near_plane, CUTS, [(c, c ^ 1) for c in range(cuts)])
     gradient, outgoing = call(
         product_kernel,
         [block, ((cuts * events, 1, LANES), jnp.float32)],
         2 * 30 * size,
         4 * 20 * size,
-        scratch_shapes=[pltpu.VMEM((RIM, rows, lats), jnp.float32)],
-    )(head, tail, left, wrap_left, right, wrap_own, wrap_other, high, low, steps, changes, gram)
+        scratch_shapes=[pltpu.VMEM((4, RIM, rows, lats), jnp.float32)],
+    )(far_halo, far_plane, near_plane, near_halo, steps, changes, gram)
     arrived = lax.all_to_all(outgoing, CUTS_EVENT, 0, 0, tiled=True)
     return call(
         direction_kernel,

time: 52 us -> 44.3 us (0.85)
  starting transfers between devices: 20.5 us -> 12 us
  blocking collectives: 16.7 us -> 18.5 us
  waiting for transfers between devices: 5.69 us -> 4.56 us
    ppermute x5 -> x2, starting transfers between devices: 17.5 us -> 8.94 us  [the longest x1 8.86 us: shards(): lax.ppermute(far_plane, CUTS, [(c, ((c - 1 ^ 1) + 1) % cuts) for c in ran...]
    ppermute x5 -> x2, waiting for transfers between devices: 4.61 us -> 2.01 us  [the longest x1 2 us: shards(): lax.ppermute(far_plane, CUTS, [(c, ((c - 1 ^ 1) + 1) % cuts) for c in ran...]
    all_to_all x1, blocking collectives: 16.7 us -> 18.5 us  [shards(): arrived = lax.all_to_all(outgoing, CUTS_EVENT, 0, 0, tiled=True)]
    ppermute x3 -> x4, waiting for transfers between devices: 1.07 us -> 2.55 us  [swapped(): return lax.ppermute(x, axis, [(0, 1), (1, 0)])]
    pallas_call x2 -> x3, Pallas kernels: 1.97 us -> 2.15 us  [the longest x1 1.69 us: shards(): call(radial_kernel, [block, half, half, block, block], 2 * 4 * rad_len *...]
    ppermute x3 -> x4, starting transfers between devices: 2.96 us -> 3.1 us  [swapped(): return lax.ppermute(x, axis, [(0, 1), (1, 0)])]
  transfers between devices with their start and end apart: 8 -> 6, of which waited for: 2 -> 3; matrix products, arithmetic and copies ran while one was open for 0% -> 0% of each run, Pallas kernels for 8% -> 10%
where the time goes in v7:
time: 44.3 us; the launch traced here: 44.2 us
  blocking collectives  18.5 us (42%)
  starting transfers between devices  12 us (27%)
  Pallas kernels  8.28 us (19%)
  waiting for transfers between devices  4.56 us (10%)
  between operations  0.7 us (2%)
    all_to_all x1, blocking collectives, shards(): arrived = lax.all_to_all(outgoing, CUTS_EVENT, 0, 0, tiled=True)  18.5 us
    ppermute x1, starting transfers between devices, shards(): lax.ppermute(far_plane, CUTS, [(c, ((c - 1 ^ 1) + 1) % cuts) for c in ran...  8.86 us
    ppermute x4, starting transfers between devices, swapped(): return lax.ppermute(x, axis, [(0, 1), (1, 0)])  3.1 us
    ppermute x4, waiting for transfers between devices, swapped(): return lax.ppermute(x, axis, [(0, 1), (1, 0)])  2.55 us
    pallas_call x1, Pallas kernels, shards(): call(gram_kernel, [(steps.shape, jnp.float32), ((8, LANES), jnp.float32)]...  2.41 us
    ppermute x1, waiting for transfers between devices, shards(): lax.ppermute(far_plane, CUTS, [(c, ((c - 1 ^ 1) + 1) % cuts) for c in ran...  2 us
    pallas_call x1, Pallas kernels, shards(): call(fetch_kernel, [(curvature.shape, jnp.float32), square, square], 10 *...  1.72 us
    pallas_call x1, Pallas kernels, shards(): call(radial_kernel, [block, half, half, block, block], 2 * 4 * rad_len *...  1.69 us
  transfers between devices with their start and end apart: 6, of which 3 were waited for; matrix products, arithmetic and copies ran while one was open for 0% of the time, Pallas kernels for 10%

profile of v7, /device:TPU:1, one launch (start us, length us, event | category | flops | bytes accessed | tf_op | source)
XLA Modules:
  0.0 44.2 jit_solution(12195700824910963570)
XLA Ops:
  0.6 1.7 %shard_map.50 = (f32[8,32,256]{2,1,0:T(8,128)S(1)}, f32[4,32,256]{2,1,0:T(8,128)S(1)}, f32[4,32,256]{2,1,0:T(8,128)S(1)}, f32[8,32,256]{2,1,0:T(8,128)S(1)}, f32[8,32,256]{2,1,0:T(8,128)S(1)}) custom-call(f32[1,8,128,256]{3,2,1,0:T(8,128)} %kernels_ref.1), custom_call_target="tpu_custom_call" | custom-call | flops 268435456 | bytes 2097152 | tf_op jit(solution)/shard_map/pallas_call | solution.py:292
  2.3 1.5 %collective-permute-start.1 = (f32[8,32,256]{2,1,0:T(8,128)S(1)}, f32[8,32,256]{2,1,0:T(8,128)S(1)}, u32[]{:S(2)}, u32[]{:S(2)}) collective-permute-start(f32[8,32,256]{2,1,0:T(8,128)S(1)} %get-tuple-element.17), channel_id=1, source_target_pairs={{0,1},{1,0},{2,3},{3,2},{4,5},{5,4},{6,7},{7,6},{8,9},{9,8},{10,11... | collective-permute-start | bytes 786440 | tf_op jit(solution)/shard_map/ppermute | solution.py:275
  3.8 0.1 collective-permute-start
  3.9 1.1 %collective-permute-done.1 = f32[8,32,256]{2,1,0:T(8,128)S(1)} collective-permute-done((f32[8,32,256]{2,1,0:T(8,128)S(1)}, f32[8,32,256]{2,1,0:T(8,128)S(1)}, u32[]{:S(2)}, u32[]{:S(2)}) %collective-permute-start.1) | collective-permute-done | bytes 262176 | tf_op jit(solution)/shard_map/ppermute | solution.py:275
  5.0 1.4 %collective-permute-start.2 = (f32[4,32,256]{2,1,0:T(8,128)S(1)}, f32[4,32,256]{2,1,0:T(8,128)S(1)}, u32[]{:S(2)}, u32[]{:S(2)}) collective-permute-start(f32[4,32,256]{2,1,0:T(8,128)S(1)} %get-tuple-element.27), channel_id=1, source_target_pairs={{0,2},{2,0},{1,3},{3,1},{4,6},{6,4},{5,7},{7,5},{8,10},{10,8},{9,1... | collective-permute-start | bytes 393224 | tf_op jit(solution)/shard_map/ppermute | solution.py:275
  6.4 0.0 copy-start
  6.4 0.1 collective-permute-start.4
  6.5 1.7 %shard_map.51 = (f32[8,8,32,256]{3,2,1,0:T(8,128)S(1)}, bf16[256,256]{1,0:T(8,128)(2,1)S(1)}, bf16[256,256]{1,0:T(8,128)(2,1)S(1)}) custom-call(f32[8,8,32,256]{3,2,1,0:T(8,128)} %curvature_ref.1), custom_call_target="tpu_custom_call" | custom-call | flops 655360 | bytes 4194304 | tf_op jit(solution)/shard_map/pallas_call | solution.py:302
  8.3 0.0 collective-permute-done.near_ref
  8.3 1.5 %collective-permute-done.2.far_ref = f32[4,32,256]{2,1,0:T(8,128)S(1)} collective-permute-done((f32[4,32,256]{2,1,0:T(8,128)S(1)}, f32[4,32,256]{2,1,0:T(8,128)S(1)}, u32[]{:S(2)}, u32[]{:S(2)}) %collective-permute-start.2) | collective-permute-done | bytes 131104 | tf_op jit(solution)/shard_map/ppermute | solution.py:275
  9.8 0.2 shard_map.52.far_ref
  10.0 8.9 %collective-permute-start.3 = (f32[4,32,256]{2,1,0:T(8,128)S(1)}, f32[4,32,256]{2,1,0:T(8,128)S(1)}, u32[]{:S(2)}, u32[]{:S(2)}) collective-permute-start(f32[4,32,256]{2,1,0:T(8,128)S(1)} %shard_map.52.far_ref), channel_id=1, source_target_pairs={{4,8},{8,4},{12,16},{16,12},{20,24},{24,20},{28,32},{32,28},{36,40... | collective-permute-start | bytes 393224 | tf_op jit(solution)/shard_map/ppermute | solution.py:326
  18.9 0.0 collective-permute-done.4.far_ref
  18.9 0.2 shard_map.53.near_ref
  19.1 0.1 collective-permute-start.5
  19.2 0.0 copy-done
  19.2 2.4 %shard_map.54 = (f32[8,8,32,256]{3,2,1,0:T(8,128)S(1)}, f32[8,128]{1,0:T(8,128)S(1)}) custom-call(f32[8,8,32,256]{3,2,1,0:T(8,128)S(1)} %copy-done, f32[8,8,32,256]{3,2,1,0:T(8,128)S(1)} %get-tuple-element.21.curvature_ref), custom_call_target="tpu_custom_call" | custom-call | flops 13107200 | bytes 6291456 | tf_op jit(solution)/shard_map/pallas_call | solution.py:313
  21.6 2.0 %collective-permute-done.3.far_halo_ref = f32[4,32,256]{2,1,0:T(8,128)S(1)} collective-permute-done((f32[4,32,256]{2,1,0:T(8,128)S(1)}, f32[4,32,256]{2,1,0:T(8,128)S(1)}, u32[]{:S(2)}, u32[]{:S(2)}) %collective-permute-start.3) | collective-permute-done | bytes 131104 | tf_op jit(solution)/shard_map/ppermute | solution.py:326
  23.6 0.0 collective-permute-done.5.near_halo_ref
  23.6 0.8 %shard_map.55 = (f32[8,32,256]{2,1,0:T(8,128)S(1)}, f32[128,1,128]{2,1,0:T(1,128)S(1)}) custom-call(f32[4,32,256]{2,1,0:T(8,128)S(1)} %collective-permute-done.3.far_halo_ref, f32[4,32,256]{2,1,0:T(8,128)S(1)} %shard_map.52.far_ref, f32[4,32,256]{2,1,0:T(8,128)S(1)} %shard_map.53.near_ref, f32[4,32,256]{2,1,0:T(8,128)S(1)} %collective-permute-done.5.near_halo_ref, ...), custom_call_target="tpu_custom_call" | custom-call | flops 3932160 | bytes 5242880 | tf_op jit(solution)/shard_map/pallas_call | solution.py:331
  24.4 18.5 %all_to_all.5.rows_ref = f32[128,1,128]{2,1,0:T(1,128)S(1)} all-to-all(f32[128,1,128]{2,1,0:T(1,128)S(1)} %get-tuple-element.24), channel_id=1, replica_groups=mesh['cuts_0'=2,'cuts_1'=4,'cuts_2'=4,'event_0'=2,'event_1'=2] {'cuts_0'..., dimensions={0} | all-to-all | bytes 131072 | tf_op jit(solution)/shard_map/all_to_all | solution.py:338
  42.9 1.2 %shard_map.56 = (f32[8,32,256]{2,1,0:T(8,128)}, f32[8,32,256]{2,1,0:T(8,128)}) custom-call(f32[128,1,128]{2,1,0:T(1,128)S(1)} %all_to_all.5.rows_ref, f32[8,32,256]{2,1,0:T(8,128)S(1)} %get-tuple-element.25.gradient_ref, f32[8,8,32,256]{3,2,1,0:T(8,128)S(1)} %copy-done, f32[8,8,32,256]{3,2,1,0:T(8,128)S(1)} %get-tuple-element.22.changes_ref), custom_call_target="tpu_custom_call" | custom-call | flops 2228224 | bytes 4718592 | tf_op jit(solution)/shard_map/pallas_call | solution.py:339
  (1 shorter events, 0.0 us)
Async XLA Ops:
  2.3 2.6 %collective-permute-start.1 = (f32[8,32,256]{2,1,0:T(8,128)S(1)}, f32[8,32,256]{2,1,0:T(8,128)S(1)}, u32[]{:S(2)}, u32[]{:S(2)}) collective-permute-start(f32[8,32,256]{2,1,0:T(8,128)S(1)} %get-tuple-element.17), channel_id=1, source_target_pairs={{0,1},{1,0},{2,3},{3,2},{4,5},{5,4},{6,7},{7,6},{8,9},{9,8},{10,11... | collective-permute-start | bytes 786440 | tf_op jit(solution)/shard_map/ppermute | solution.py:275
  3.8 4.5 %collective-permute-start = (f32[8,32,256]{2,1,0:T(8,128)S(1)}, f32[8,32,256]{2,1,0:T(8,128)S(1)}, u32[]{:S(2)}, u32[]{:S(2)}) collective-permute-start(f32[8,32,256]{2,1,0:T(8,128)S(1)} %get-tuple-element.15), channel_id=1, source_target_pairs={{0,1},{1,0},{2,3},{3,2},{4,5},{5,4},{6,7},{7,6},{8,9},{9,8},{10,11... | collective-permute-start | bytes 786440 | tf_op jit(solution)/shard_map/ppermute | solution.py:275
  5.0 4.8 %collective-permute-start.2 = (f32[4,32,256]{2,1,0:T(8,128)S(1)}, f32[4,32,256]{2,1,0:T(8,128)S(1)}, u32[]{:S(2)}, u32[]{:S(2)}) collective-permute-start(f32[4,32,256]{2,1,0:T(8,128)S(1)} %get-tuple-element.27), channel_id=1, source_target_pairs={{0,2},{2,0},{1,3},{3,1},{4,6},{6,4},{5,7},{7,5},{8,10},{10,8},{9,1... | collective-permute-start | bytes 393224 | tf_op jit(solution)/shard_map/ppermute | solution.py:275
  6.4 12.8 %copy-start = (f32[8,8,32,256]{3,2,1,0:T(8,128)S(1)}, f32[8,8,32,256]{3,2,1,0:T(8,128)}, u32[]{:S(2)}) copy-start(f32[8,8,32,256]{3,2,1,0:T(8,128)} %steps_ref.5) | copy-start | bytes 6291460
  6.4 12.5 %collective-permute-start.4 = (f32[4,32,256]{2,1,0:T(8,128)S(1)}, f32[4,32,256]{2,1,0:T(8,128)S(1)}, u32[]{:S(2)}, u32[]{:S(2)}) collective-permute-start(f32[4,32,256]{2,1,0:T(8,128)S(1)} %get-tuple-element.26), channel_id=1, source_target_pairs={{0,2},{2,0},{1,3},{3,1},{4,6},{6,4},{5,7},{7,5},{8,10},{10,8},{9,1... | collective-permute-start | bytes 393224 | tf_op jit(solution)/shard_map/ppermute | solution.py:275
  10.0 13.6 %collective-permute-start.3 = (f32[4,32,256]{2,1,0:T(8,128)S(1)}, f32[4,32,256]{2,1,0:T(8,128)S(1)}, u32[]{:S(2)}, u32[]{:S(2)}) collective-permute-start(f32[4,32,256]{2,1,0:T(8,128)S(1)} %shard_map.52.far_ref), channel_id=1, source_target_pairs={{4,8},{8,4},{12,16},{16,12},{20,24},{24,20},{28,32},{32,28},{36,40... | collective-permute-start | bytes 393224 | tf_op jit(solution)/shard_map/ppermute | solution.py:326
  19.1 4.5 %collective-permute-start.5 = (f32[4,32,256]{2,1,0:T(8,128)S(1)}, f32[4,32,256]{2,1,0:T(8,128)S(1)}, u32[]{:S(2)}, u32[]{:S(2)}) collective-permute-start(f32[4,32,256]{2,1,0:T(8,128)S(1)} %shard_map.53.near_ref), channel_id=1, source_target_pairs={{0,4},{4,0},{8,12},{12,8},{16,20},{20,16},{24,28},{28,24},{32,36},... | collective-permute-start | bytes 393224 | tf_op jit(solution)/shard_map/ppermute | solution.py:330

commit v8 on v7

--- a/solution.py
+++ b/solution.py
@@ -1,4 +1,3 @@
-import functools
 import math
 
 import jax
@@ -56,20 +55,25 @@
     return matrix / jnp.sum(matrix, axis=axis, keepdims=True)
 
 
-def radial_kernel(
-    kernels_ref, keep_ref, pass_far_ref, pass_near_ref, send_keep_ref, send_pass_ref, held_ref, semaphores
+def radial_products(field_ref, weights, keep_ref, pass_ref, send_keep_ref, send_pass_ref):
+    for a in range(field_ref.shape[0]):
+        both = dot(weights, jnp.concatenate(split(field_ref[a]), axis=0))
+        length = both.shape[0] // 2
+        rows = length // 4
+        out = both[:length] + both[length:]
+        for k, ref in enumerate((keep_ref, pass_ref, send_keep_ref, send_pass_ref)):
+            ref[a] = out[k * rows : (k + 1) * rows]
+
+
+def far_radial_kernel(
+    kernels_ref, keep_ref, pass_ref, send_keep_ref, send_pass_ref, near_ref, weights_ref, far_ref, semaphores
 ):
-    _, _, length, _ = kernels_ref.shape
+    length = kernels_ref.shape[2]
     odd = lax.rem(cut_number(), 2)
     copies = []
-    for piece in range(2):
-        copies.append(
-            pltpu.make_async_copy(
-                kernels_ref.at[0, pl.ds(RIM * (odd ^ piece), RIM)],
-                held_ref.at[pl.ds(RIM * piece, RIM)],
-                semaphores.at[piece],
-            )
-        )
+    for piece, ref in enumerate((far_ref, near_ref)):
+        source = kernels_ref.at[0, pl.ds(RIM * (odd ^ piece), RIM)]
+        copies.append(pltpu.make_async_copy(source, ref, semaphores.at[piece]))
         copies[piece].start()
     part = 2 * lax.axis_index("event_0") + lax.axis_index("event_1")
     rows = length // 4
@@ -79,16 +83,14 @@
         [gauss_rows(length, 3.0, local + rows * block, 1) for block in order], axis=0
     )
     weights = jnp.concatenate([jnp.concatenate([m, m], axis=1) for m in split(matrix)], axis=0)
-    for piece in range(2):
-        copies[piece].wait()
-        for a in range(RIM):
-            at = piece * RIM + a
-            both = dot(weights, jnp.concatenate(split(held_ref[at]), axis=0))
-            out = both[:length] + both[length:]
-            keep_ref[at] = out[:rows]
-            (pass_far_ref, pass_near_ref)[piece][a] = out[rows : 2 * rows]
-            send_keep_ref[at] = out[2 * rows : 3 * rows]
-            send_pass_ref[at] = out[3 * rows :]
+    weights_ref[...] = weights
+    copies[0].wait()
+    radial_products(far_ref, weights, keep_ref, pass_ref, send_keep_ref, send_pass_ref)
+    copies[1].wait()
+
+
+def near_radial_kernel(near_ref, weights_ref, keep_ref, pass_ref, send_keep_ref, send_pass_ref):
+    radial_products(near_ref, weights_ref[...], keep_ref, pass_ref, send_keep_ref, send_pass_ref)
 
 
 def smoothed(field, high, low):
@@ -107,10 +109,9 @@
     copy.wait()
 
 
-def latitude_kernel(start, keep_ref, near_ref, far_ref, high_ref, low_ref, plane_ref):
+def latitude_kernel(keep_ref, core_ref, chip_ref, high_ref, low_ref, plane_ref):
     lons, rows, lats = plane_ref.shape
-    at = slice(start, start + lons)
-    summed = (keep_ref[at] + near_ref[at] + far_ref[...]).reshape(lons * rows, lats)
+    summed = (keep_ref[...] + core_ref[...] + chip_ref[...]).reshape(lons * rows, lats)
     plane_ref[...] = smoothed(summed, high_ref[...], low_ref[...]).reshape(lons, rows, lats)
 
 
@@ -289,15 +290,25 @@
     size = lons * rows * lats
     half = ((RIM, rows, lats), jnp.float32)
     cuts, events = lax.axis_size(CUTS), lax.axis_size(EVENT)
-    keep, pass_far, pass_near, send_keep, send_pass = call(
-        radial_kernel,
-        [block, half, half, block, block],
-        2 * 4 * rad_len * kernels.size,
+    table = ((2 * rad_len, 2 * rad_len), jnp.bfloat16)
+    flops = 4 * rad_len * kernels.size
+    far_keep, far_pass, far_send_keep, far_send_pass, near_field, weights = call(
+        far_radial_kernel,
+        [half] * 4 + [((RIM, rad_len, lats), jnp.float32), table],
+        flops,
         8 * kernels.size,
         in_specs=[pl.BlockSpec(memory_space=pltpu.HBM)],
-        scratch_shapes=[pltpu.VMEM(kernels.shape[1:], jnp.float32), pltpu.SemaphoreType.DMA((2,))],
+        scratch_shapes=[
+            pltpu.VMEM((RIM, rad_len, lats), jnp.float32),
+            pltpu.SemaphoreType.DMA((2,)),
+        ],
     )(in_hbm(kernels))
-    near_pass = swapped(send_pass, "event_1")
+    far_core_pass = swapped(far_send_pass, "event_1")
+    near_keep, near_pass, near_send_keep, near_send_pass = call(
+        near_radial_kernel, [half] * 4, flops, 4 * kernels.size
+    )(near_field, weights)
+    far_chip = swapped(far_pass + far_core_pass, "event_0")
+    near_core_pass = swapped(near_send_pass, "event_1")
     square = ((lats, lats), jnp.bfloat16)
     held_curvature, high, low = call(
         fetch_kernel,
@@ -307,9 +318,9 @@
         in_specs=[pl.BlockSpec(memory_space=pltpu.HBM)],
         scratch_shapes=[pltpu.SemaphoreType.DMA],
     )(in_hbm(curvature))
-    far_chunk = swapped(pass_far + near_pass[:RIM], "event_0")
-    near_chunk = swapped(pass_near + near_pass[RIM:], "event_0")
-    near_keep = swapped(send_keep, "event_1")
+    near_chip = swapped(near_pass + near_core_pass, "event_0")
+    far_core = swapped(far_send_keep, "event_1")
+    near_core = swapped(near_send_keep, "event_1")
     changes, gram = call(
         gram_kernel,
         [(steps.shape, jnp.float32), ((8, LANES), jnp.float32)],
@@ -317,16 +328,14 @@
         12 * steps.size,
     )(steps, held_curvature)
 
-    def plane_of(start, chunk):
-        return call(
-            functools.partial(latitude_kernel, start), [half], 4 * lats * size, 8 * size
-        )(keep, near_keep, chunk, high, low)[0]
-
-    far_plane = plane_of(0, far_chunk)
+    def plane_of(*parts):
+        return call(latitude_kernel, [half], 4 * lats * size, 8 * size)(*parts, high, low)[0]
+
+    far_plane = plane_of(far_keep, far_core, far_chip)
     far_halo = lax.ppermute(
         far_plane, CUTS, [(c, (((c - 1) ^ 1) + 1) % cuts) for c in range(1, cuts)] + [(0, cuts - 1)]
     )
-    near_plane = plane_of(RIM, near_chunk)
+    near_plane = plane_of(near_keep, near_core, near_chip)
     near_halo = lax.ppermute(near_plane, CUTS, [(c, c ^ 1) for c in range(cuts)])
     gradient, outgoing = call(
         product_kernel,

time: 44.3 us -> 43.9 us (level)
  waiting for transfers between devices: 4.56 us -> 2.97 us
  starting transfers between devices: 12 us -> 13.3 us
    ppermute x4 -> x6, waiting for transfers between devices: 2.55 us -> 0.97 us  [swapped(): return lax.ppermute(x, axis, [(0, 1), (1, 0)])]
    ppermute x4 -> x6, starting transfers between devices: 3.1 us -> 4.32 us  [swapped(): return lax.ppermute(x, axis, [(0, 1), (1, 0)])]
    pallas_call x3 -> x4, Pallas kernels: 2.15 us -> 2.14 us  [the longest x1 1.39 us: shards(): call(far_radial_kernel, [half] * 4 + [((RIM, rad_len, lats), jnp.float32)...]
  transfers between devices with their start and end apart: 6 -> 8, of which waited for: 3 -> 3; matrix products, arithmetic and copies ran while one was open for 0% -> 0% of each run, Pallas kernels for 10% -> 11%
where the time goes in v8:
time: 43.9 us; the launch traced here: 43.7 us
  blocking collectives  18.5 us (42%)
  starting transfers between devices  13.3 us (30%)
  Pallas kernels  8.15 us (19%)
  waiting for transfers between devices  2.97 us (7%)
  between operations  0.73 us (2%)
    all_to_all x1, blocking collectives, shards(): arrived = lax.all_to_all(outgoing, CUTS_EVENT, 0, 0, tiled=True)  18.5 us
    ppermute x1, starting transfers between devices, shards(): lax.ppermute(far_plane, CUTS, [(c, ((c - 1 ^ 1) + 1) % cuts) for c in ran...  8.86 us
    ppermute x6, starting transfers between devices, swapped(): return lax.ppermute(x, axis, [(0, 1), (1, 0)])  4.32 us
    pallas_call x1, Pallas kernels, shards(): call(gram_kernel, [(steps.shape, jnp.float32), ((8, LANES), jnp.float32)]...  2.41 us
    ppermute x1, waiting for transfers between devices, shards(): lax.ppermute(far_plane, CUTS, [(c, ((c - 1 ^ 1) + 1) % cuts) for c in ran...  2 us
    pallas_call x1, Pallas kernels, shards(): call(fetch_kernel, [(curvature.shape, jnp.float32), square, square], 10 *...  1.6 us
    pallas_call x1, Pallas kernels, shards(): call(far_radial_kernel, [half] * 4 + [((RIM, rad_len, lats), jnp.float32)...  1.39 us
    pallas_call x1, Pallas kernels, shards(): call(direction_kernel, [block] * 2, 2 * 17 * size, 4 * 18 * size, out_spe...  1.25 us
  transfers between devices with their start and end apart: 8, of which 3 were waited for; matrix products, arithmetic and copies ran while one was open for 0% of the time, Pallas kernels for 11%

profile of v8, /device:TPU:1, one launch (start us, length us, event | category | flops | bytes accessed | tf_op | source)
XLA Modules:
  0.0 43.7 jit_solution(15205429043494794407)
XLA Ops:
  0.6 1.4 %shard_map.50 = (f32[4,32,256]{2,1,0:T(8,128)S(1)}, f32[4,32,256]{2,1,0:T(8,128)S(1)}, f32[4,32,256]{2,1,0:T(8,128)S(1)}, f32[4,32,256]{2,1,0:T(8,128)S(1)}, f32...) custom-call(f32[1,8,128,256]{3,2,1,0:T(8,128)} %kernels_ref.1), custom_call_target="tpu_custom_call" | custom-call | flops 134217728 | bytes 2097152 | tf_op jit(solution)/shard_map/pallas_call | solution.py:295
  2.0 1.5 %collective-permute-start.1 = (f32[4,32,256]{2,1,0:T(8,128)S(1)}, f32[4,32,256]{2,1,0:T(8,128)S(1)}, u32[]{:S(2)}, u32[]{:S(2)}) collective-permute-start(f32[4,32,256]{2,1,0:T(8,128)S(1)} %get-tuple-element.22), channel_id=1, source_target_pairs={{0,1},{1,0},{2,3},{3,2},{4,5},{5,4},{6,7},{7,6},{8,9},{9,8},{10,11... | collective-permute-start | bytes 393224 | tf_op jit(solution)/shard_map/ppermute | solution.py:276
  3.5 0.3 shard_map.53
  3.8 0.1 collective-permute-start.5
  3.9 0.5 %collective-permute-start = (f32[4,32,256]{2,1,0:T(8,128)S(1)}, f32[4,32,256]{2,1,0:T(8,128)S(1)}, u32[]{:S(2)}, u32[]{:S(2)}) collective-permute-start(f32[4,32,256]{2,1,0:T(8,128)S(1)} %get-tuple-element.20), channel_id=1, source_target_pairs={{0,1},{1,0},{2,3},{3,2},{4,5},{5,4},{6,7},{7,6},{8,9},{9,8},{10,11... | collective-permute-start | bytes 393224 | tf_op jit(solution)/shard_map/ppermute | solution.py:276
  4.4 0.1 collective-permute-done.1
  4.5 0.0 copy-start
  4.5 1.4 %collective-permute-start.2 = (f32[4,32,256]{2,1,0:T(8,128)S(1)}, f32[4,32,256]{2,1,0:T(8,128)S(1)}, u32[]{:S(2)}, u32[]{:S(2)}) collective-permute-start(f32[4,32,256]{2,1,0:T(8,128)S(1)} %add.6), channel_id=1, source_target_pairs={{0,2},{2,0},{1,3},{3,1},{4,6},{6,4},{5,7},{7,5},{8,10},{10,8},{9,1... | collective-permute-start | bytes 393224 | tf_op jit(solution)/shard_map/ppermute | solution.py:276
  5.9 0.6 %collective-permute-start.4 = (f32[4,32,256]{2,1,0:T(8,128)S(1)}, f32[4,32,256]{2,1,0:T(8,128)S(1)}, u32[]{:S(2)}, u32[]{:S(2)}) collective-permute-start(f32[4,32,256]{2,1,0:T(8,128)S(1)} %get-tuple-element.28), channel_id=1, source_target_pairs={{0,1},{1,0},{2,3},{3,2},{4,5},{5,4},{6,7},{7,6},{8,9},{9,8},{10,11... | collective-permute-start | bytes 393224 | tf_op jit(solution)/shard_map/ppermute | solution.py:276
  6.6 0.0 collective-permute-done.5
  6.6 0.2 collective-permute-start.6
  6.8 1.6 %shard_map.51 = (f32[8,8,32,256]{3,2,1,0:T(8,128)S(1)}, bf16[256,256]{1,0:T(8,128)(2,1)S(1)}, bf16[256,256]{1,0:T(8,128)(2,1)S(1)}) custom-call(f32[8,8,32,256]{3,2,1,0:T(8,128)} %curvature_ref.1), custom_call_target="tpu_custom_call" | custom-call | flops 655360 | bytes 4194304 | tf_op jit(solution)/shard_map/pallas_call | solution.py:313
  8.4 0.0 collective-permute-done.core_ref
  8.4 0.9 %collective-permute-done.2.chip_ref = f32[4,32,256]{2,1,0:T(8,128)S(1)} collective-permute-done((f32[4,32,256]{2,1,0:T(8,128)S(1)}, f32[4,32,256]{2,1,0:T(8,128)S(1)}, u32[]{:S(2)}, u32[]{:S(2)}) %collective-permute-start.2) | collective-permute-done | bytes 131104 | tf_op jit(solution)/shard_map/ppermute | solution.py:276
  9.3 0.2 shard_map.52.far_ref
  9.5 8.9 %collective-permute-start.3 = (f32[4,32,256]{2,1,0:T(8,128)S(1)}, f32[4,32,256]{2,1,0:T(8,128)S(1)}, u32[]{:S(2)}, u32[]{:S(2)}) collective-permute-start(f32[4,32,256]{2,1,0:T(8,128)S(1)} %shard_map.52.far_ref), channel_id=1, source_target_pairs={{4,8},{8,4},{12,16},{16,12},{20,24},{24,20},{28,32},{32,28},{36,40... | collective-permute-start | bytes 393224 | tf_op jit(solution)/shard_map/ppermute | solution.py:335
  18.4 0.0 collective-permute-done.4.core_ref
  18.4 0.0 collective-permute-done.6.chip_ref
  18.4 0.2 shard_map.54.near_ref
  18.6 0.1 collective-permute-start.7
  18.7 0.0 copy-done
  18.7 2.4 %shard_map.55 = (f32[8,8,32,256]{3,2,1,0:T(8,128)S(1)}, f32[8,128]{1,0:T(8,128)S(1)}) custom-call(f32[8,8,32,256]{3,2,1,0:T(8,128)S(1)} %copy-done, f32[8,8,32,256]{3,2,1,0:T(8,128)S(1)} %get-tuple-element.31.curvature_ref), custom_call_target="tpu_custom_call" | custom-call | flops 13107200 | bytes 6291456 | tf_op jit(solution)/shard_map/pallas_call | solution.py:324
  21.1 2.0 %collective-permute-done.3.far_halo_ref = f32[4,32,256]{2,1,0:T(8,128)S(1)} collective-permute-done((f32[4,32,256]{2,1,0:T(8,128)S(1)}, f32[4,32,256]{2,1,0:T(8,128)S(1)}, u32[]{:S(2)}, u32[]{:S(2)}) %collective-permute-start.3) | collective-permute-done | bytes 131104 | tf_op jit(solution)/shard_map/ppermute | solution.py:335
  23.1 0.0 collective-permute-done.7.near_halo_ref
  23.1 0.8 %shard_map.56 = (f32[8,32,256]{2,1,0:T(8,128)S(1)}, f32[128,1,128]{2,1,0:T(1,128)S(1)}) custom-call(f32[4,32,256]{2,1,0:T(8,128)S(1)} %collective-permute-done.3.far_halo_ref, f32[4,32,256]{2,1,0:T(8,128)S(1)} %shard_map.52.far_ref, f32[4,32,256]{2,1,0:T(8,128)S(1)} %shard_map.54.near_ref, f32[4,32,256]{2,1,0:T(8,128)S(1)} %collective-permute-done.7.near_halo_ref, ...), custom_call_target="tpu_custom_call" | custom-call | flops 3932160 | bytes 5242880 | tf_op jit(solution)/shard_map/pallas_call | solution.py:340
  23.9 18.5 %all_to_all.5.rows_ref = f32[128,1,128]{2,1,0:T(1,128)S(1)} all-to-all(f32[128,1,128]{2,1,0:T(1,128)S(1)} %get-tuple-element.34), channel_id=1, replica_groups=mesh['cuts_0'=2,'cuts_1'=4,'cuts_2'=4,'event_0'=2,'event_1'=2] {'cuts_0'..., dimensions={0} | all-to-all | bytes 131072 | tf_op jit(solution)/shard_map/all_to_all | solution.py:347
  42.4 1.2 %shard_map.57 = (f32[8,32,256]{2,1,0:T(8,128)}, f32[8,32,256]{2,1,0:T(8,128)}) custom-call(f32[128,1,128]{2,1,0:T(1,128)S(1)} %all_to_all.5.rows_ref, f32[8,32,256]{2,1,0:T(8,128)S(1)} %get-tuple-element.35.gradient_ref, f32[8,8,32,256]{3,2,1,0:T(8,128)S(1)} %copy-done, f32[8,8,32,256]{3,2,1,0:T(8,128)S(1)} %get-tuple-element.32.changes_ref), custom_call_target="tpu_custom_call" | custom-call | flops 2228224 | bytes 4718592 | tf_op jit(solution)/shard_map/pallas_call | solution.py:348
  (2 shorter events, 0.0 us)
Async XLA Ops:
  2.0 2.4 %collective-permute-start.1 = (f32[4,32,256]{2,1,0:T(8,128)S(1)}, f32[4,32,256]{2,1,0:T(8,128)S(1)}, u32[]{:S(2)}, u32[]{:S(2)}) collective-permute-start(f32[4,32,256]{2,1,0:T(8,128)S(1)} %get-tuple-element.22), channel_id=1, source_target_pairs={{0,1},{1,0},{2,3},{3,2},{4,5},{5,4},{6,7},{7,6},{8,9},{9,8},{10,11... | collective-permute-start | bytes 393224 | tf_op jit(solution)/shard_map/ppermute | solution.py:276
  3.8 2.8 %collective-permute-start.5 = (f32[4,32,256]{2,1,0:T(8,128)S(1)}, f32[4,32,256]{2,1,0:T(8,128)S(1)}, u32[]{:S(2)}, u32[]{:S(2)}) collective-permute-start(f32[4,32,256]{2,1,0:T(8,128)S(1)} %get-tuple-element.30), channel_id=1, source_target_pairs={{0,1},{1,0},{2,3},{3,2},{4,5},{5,4},{6,7},{7,6},{8,9},{9,8},{10,11... | collective-permute-start | bytes 393224 | tf_op jit(solution)/shard_map/ppermute | solution.py:276
  3.9 4.5 %collective-permute-start = (f32[4,32,256]{2,1,0:T(8,128)S(1)}, f32[4,32,256]{2,1,0:T(8,128)S(1)}, u32[]{:S(2)}, u32[]{:S(2)}) collective-permute-start(f32[4,32,256]{2,1,0:T(8,128)S(1)} %get-tuple-element.20), channel_id=1, source_target_pairs={{0,1},{1,0},{2,3},{3,2},{4,5},{5,4},{6,7},{7,6},{8,9},{9,8},{10,11... | collective-permute-start | bytes 393224 | tf_op jit(solution)/shard_map/ppermute | solution.py:276
  4.5 14.2 %copy-start = (f32[8,8,32,256]{3,2,1,0:T(8,128)S(1)}, f32[8,8,32,256]{3,2,1,0:T(8,128)}, u32[]{:S(2)}) copy-start(f32[8,8,32,256]{3,2,1,0:T(8,128)} %steps_ref.5) | copy-start | bytes 6291460
  4.5 4.8 %collective-permute-start.2 = (f32[4,32,256]{2,1,0:T(8,128)S(1)}, f32[4,32,256]{2,1,0:T(8,128)S(1)}, u32[]{:S(2)}, u32[]{:S(2)}) collective-permute-start(f32[4,32,256]{2,1,0:T(8,128)S(1)} %add.6), channel_id=1, source_target_pairs={{0,2},{2,0},{1,3},{3,1},{4,6},{6,4},{5,7},{7,5},{8,10},{10,8},{9,1... | collective-permute-start | bytes 393224 | tf_op jit(solution)/shard_map/ppermute | solution.py:276
  5.9 12.5 %collective-permute-start.4 = (f32[4,32,256]{2,1,0:T(8,128)S(1)}, f32[4,32,256]{2,1,0:T(8,128)S(1)}, u32[]{:S(2)}, u32[]{:S(2)}) collective-permute-start(f32[4,32,256]{2,1,0:T(8,128)S(1)} %get-tuple-element.28), channel_id=1, source_target_pairs={{0,1},{1,0},{2,3},{3,2},{4,5},{5,4},{6,7},{7,6},{8,9},{9,8},{10,11... | collective-permute-start | bytes 393224 | tf_op jit(solution)/shard_map/ppermute | solution.py:276
  6.6 11.8 %collective-permute-start.6 = (f32[4,32,256]{2,1,0:T(8,128)S(1)}, f32[4,32,256]{2,1,0:T(8,128)S(1)}, u32[]{:S(2)}, u32[]{:S(2)}) collective-permute-start(f32[4,32,256]{2,1,0:T(8,128)S(1)} %add.7), channel_id=1, source_target_pairs={{0,2},{2,0},{1,3},{3,1},{4,6},{6,4},{5,7},{7,5},{8,10},{10,8},{9,1... | collective-permute-start | bytes 393224 | tf_op jit(solution)/shard_map/ppermute | solution.py:276
  9.5 13.6 %collective-permute-start.3 = (f32[4,32,256]{2,1,0:T(8,128)S(1)}, f32[4,32,256]{2,1,0:T(8,128)S(1)}, u32[]{:S(2)}, u32[]{:S(2)}) collective-permute-start(f32[4,32,256]{2,1,0:T(8,128)S(1)} %shard_map.52.far_ref), channel_id=1, source_target_pairs={{4,8},{8,4},{12,16},{16,12},{20,24},{24,20},{28,32},{32,28},{36,40... | collective-permute-start | bytes 393224 | tf_op jit(solution)/shard_map/ppermute | solution.py:335
  18.6 4.5 %collective-permute-start.7 = (f32[4,32,256]{2,1,0:T(8,128)S(1)}, f32[4,32,256]{2,1,0:T(8,128)S(1)}, u32[]{:S(2)}, u32[]{:S(2)}) collective-permute-start(f32[4,32,256]{2,1,0:T(8,128)S(1)} %shard_map.54.near_ref), channel_id=1, source_target_pairs={{0,4},{4,0},{8,12},{12,8},{16,20},{20,16},{24,28},{28,24},{32,36},... | collective-permute-start | bytes 393224 | tf_op jit(solution)/shard_map/ppermute | solution.py:339

commit v9 on v8

--- a/solution.py
+++ b/solution.py
@@ -89,8 +89,13 @@
     copies[1].wait()
 
 
-def near_radial_kernel(near_ref, weights_ref, keep_ref, pass_ref, send_keep_ref, send_pass_ref):
+def near_radial_kernel(
+    near_ref, weights_ref, keep_ref, pass_ref, send_keep_ref, send_pass_ref, high_ref, low_ref
+):
     radial_products(near_ref, weights_ref[...], keep_ref, pass_ref, send_keep_ref, send_pass_ref)
+    lats = high_ref.shape[0]
+    column = lax.broadcasted_iota(jnp.int32, (lats, lats), 1)
+    high_ref[...], low_ref[...] = split(gauss_rows(lats, 4.0, column, 0))
 
 
 def smoothed(field, high, low):
@@ -100,19 +105,37 @@
     return out[:count] + out[count:]
 
 
-def fetch_kernel(curvature_ref, held_ref, high_ref, low_ref, semaphore):
+def fetch_kernel(curvature_ref, held_ref, semaphore):
     copy = pltpu.make_async_copy(curvature_ref, held_ref, semaphore)
     copy.start()
-    lats = high_ref.shape[0]
-    column = lax.broadcasted_iota(jnp.int32, (lats, lats), 1)
-    high_ref[...], low_ref[...] = split(gauss_rows(lats, 4.0, column, 0))
     copy.wait()
 
 
-def latitude_kernel(keep_ref, core_ref, chip_ref, high_ref, low_ref, plane_ref):
-    lons, rows, lats = plane_ref.shape
-    summed = (keep_ref[...] + core_ref[...] + chip_ref[...]).reshape(lons * rows, lats)
-    plane_ref[...] = smoothed(summed, high_ref[...], low_ref[...]).reshape(lons, rows, lats)
+def plane_of(parts, high_ref, low_ref):
+    summed = sum(ref[...] for ref in parts)
+    lons, rows, lats = summed.shape
+    plane = smoothed(summed.reshape(lons * rows, lats), high_ref[...], low_ref[...])
+    return plane.reshape(lons, rows, lats)
+
+
+def far_latitude_kernel(
+    keep_ref, core_ref, chip_ref, passed_ref, cross_ref, high_ref, low_ref, plane_ref, out_ref
+):
+    plane = plane_of((keep_ref, core_ref, chip_ref), high_ref, low_ref)
+    plane_ref[...] = plane
+    first = cut_number() == 0
+
+    @pl.when(first)
+    def _():
+        out_ref[...] = plane_of((passed_ref, cross_ref), high_ref, low_ref)
+
+    @pl.when(jnp.logical_not(first))
+    def _():
+        out_ref[...] = plane
+
+
+def near_latitude_kernel(keep_ref, core_ref, chip_ref, high_ref, low_ref, plane_ref):
+    plane_ref[...] = plane_of((keep_ref, core_ref, chip_ref), high_ref, low_ref)
 
 
 def lane_numbers():
@@ -304,23 +327,29 @@
         ],
     )(in_hbm(kernels))
     far_core_pass = swapped(far_send_pass, "event_1")
-    near_keep, near_pass, near_send_keep, near_send_pass = call(
-        near_radial_kernel, [half] * 4, flops, 4 * kernels.size
+    square = ((lats, lats), jnp.bfloat16)
+    near_keep, near_pass, near_send_keep, near_send_pass, high, low = call(
+        near_radial_kernel, [half] * 4 + [square] * 2, flops, 4 * kernels.size
     )(near_field, weights)
-    far_chip = swapped(far_pass + far_core_pass, "event_0")
+    far_passed = far_pass + far_core_pass
+    far_chip = swapped(far_passed, "event_0")
     near_core_pass = swapped(near_send_pass, "event_1")
-    square = ((lats, lats), jnp.bfloat16)
-    held_curvature, high, low = call(
+    near_chip = swapped(near_pass + near_core_pass, "event_0")
+    far_core = swapped(far_send_keep, "event_1")
+    near_core = swapped(near_send_keep, "event_1")
+    (held_curvature,) = call(
         fetch_kernel,
-        [(curvature.shape, jnp.float32), square, square],
-        10 * lats * lats,
+        [(curvature.shape, jnp.float32)],
+        0,
         8 * curvature.size,
         in_specs=[pl.BlockSpec(memory_space=pltpu.HBM)],
         scratch_shapes=[pltpu.SemaphoreType.DMA],
     )(in_hbm(curvature))
-    near_chip = swapped(near_pass + near_core_pass, "event_0")
-    far_core = swapped(far_send_keep, "event_1")
-    near_core = swapped(near_send_keep, "event_1")
+    cross = lax.ppermute(
+        far_keep + far_core,
+        CUTS_EVENT,
+        [(e, e ^ 2) for e in range(events)] + [(d, d) for d in range(events, cuts * events)],
+    )
     changes, gram = call(
         gram_kernel,
         [(steps.shape, jnp.float32), ((8, LANES), jnp.float32)],
@@ -328,14 +357,17 @@
         12 * steps.size,
     )(steps, held_curvature)
 
-    def plane_of(*parts):
-        return call(latitude_kernel, [half], 4 * lats * size, 8 * size)(*parts, high, low)[0]
-
-    far_plane = plane_of(far_keep, far_core, far_chip)
-    far_halo = lax.ppermute(
-        far_plane, CUTS, [(c, (((c - 1) ^ 1) + 1) % cuts) for c in range(1, cuts)] + [(0, cuts - 1)]
-    )
-    near_plane = plane_of(near_keep, near_core, near_chip)
+    far_plane, far_out = call(far_latitude_kernel, [half] * 2, 4 * lats * size, 8 * size)(
+        far_keep, far_core, far_chip, far_passed, cross, high, low
+    )
+    pairs = []
+    for c in range(cuts):
+        other, flip = (((c - 1) ^ 1) + 1) % cuts if c else cuts - 1, 2 if c == 0 else 0
+        pairs += [(c * events + e, other * events + (e ^ flip)) for e in range(events)]
+    far_halo = lax.ppermute(far_out, CUTS_EVENT, pairs)
+    (near_plane,) = call(near_latitude_kernel, [half], 4 * lats * size, 8 * size)(
+        near_keep, near_core, near_chip, high, low
+    )
     near_halo = lax.ppermute(near_plane, CUTS, [(c, c ^ 1) for c in range(cuts)])
     gradient, outgoing = call(
         product_kernel,

time: 43.9 us -> 45.7 us (1.041)
  waiting for transfers between devices: 2.97 us -> 4.27 us
  starting transfers between devices: 13.3 us -> 14 us
  blocking collectives: 18.5 us -> 18 us
    ppermute x6, waiting for transfers between devices: 0.97 us -> 3.2 us  [swapped(): return lax.ppermute(x, axis, [(0, 1), (1, 0)])]
    ppermute x1, starting transfers between devices: 0.09 us -> 1.67 us  [shards(): lax.ppermute(near_plane, CUTS, [(c, c ^ 1) for c in range(cuts)])]
    ppermute x1 -> x2, starting transfers between devices: 8.86 us -> 7.59 us  [the longest x1 5.42 us: shards(): far_halo = lax.ppermute(far_out, CUTS_EVENT, pairs)]
    ppermute x1 -> x2, waiting for transfers between devices: 2 us -> 1.07 us  [the longest x1 0.9 us: shards(): lax.ppermute(far_keep + far_core, CUTS_EVENT, [(e, e ^ 2) for e in range(...]
    all_to_all x1, blocking collectives: 18.5 us -> 18 us  [shards(): arrived = lax.all_to_all(outgoing, CUTS_EVENT, 0, 0, tiled=True)]
  transfers between devices with their start and end apart: 8 -> 9, of which waited for: 3 -> 4; matrix products, arithmetic and copies ran while one was open for 0% -> 0% of each run, Pallas kernels for 11% -> 10%
where the time goes in v9:
time: 45.7 us; the launch traced here: 45.5 us
  blocking collectives  18 us (39%)
  starting transfers between devices  14 us (31%)
  Pallas kernels  8.43 us (18%)
  waiting for transfers between devices  4.27 us (9%)
  between operations  0.74 us (2%)
    all_to_all x1, blocking collectives, shards(): arrived = lax.all_to_all(outgoing, CUTS_EVENT, 0, 0, tiled=True)  18 us
    ppermute x1, starting transfers between devices, shards(): far_halo = lax.ppermute(far_out, CUTS_EVENT, pairs)  5.42 us
    ppermute x6, starting transfers between devices, swapped(): return lax.ppermute(x, axis, [(0, 1), (1, 0)])  4.75 us
    ppermute x6, waiting for transfers between devices, swapped(): return lax.ppermute(x, axis, [(0, 1), (1, 0)])  3.2 us
    pallas_call x1, Pallas kernels, shards(): call(gram_kernel, [(steps.shape, jnp.float32), ((8, LANES), jnp.float32)]...  2.41 us
    ppermute x1, starting transfers between devices, shards(): lax.ppermute(far_keep + far_core, CUTS_EVENT, [(e, e ^ 2) for e in range(...  2.17 us
    ppermute x1, starting transfers between devices, shards(): lax.ppermute(near_plane, CUTS, [(c, c ^ 1) for c in range(cuts)])  1.67 us
    pallas_call x1, Pallas kernels, shards(): call(fetch_kernel, [(curvature.shape, jnp.float32)], 0, 8 * curvature.siz...  1.6 us
  transfers between devices with their start and end apart: 9, of which 4 were waited for; matrix products, arithmetic and copies ran while one was open for 0% of the time, Pallas kernels for 10%

profile of v9, /device:TPU:1, one launch (start us, length us, event | category | flops | bytes accessed | tf_op | source)
XLA Modules:
  0.0 45.5 jit_solution(5245436474015228668)
XLA Ops:
  0.6 1.4 %shard_map.50 = (f32[4,32,256]{2,1,0:T(8,128)S(1)}, f32[4,32,256]{2,1,0:T(8,128)S(1)}, f32[4,32,256]{2,1,0:T(8,128)S(1)}, f32[4,32,256]{2,1,0:T(8,128)S(1)}, f32...) custom-call(f32[1,8,128,256]{3,2,1,0:T(8,128)} %kernels_ref.1), custom_call_target="tpu_custom_call" | custom-call | flops 134217728 | bytes 2097152 | tf_op jit(solution)/shard_map/pallas_call | solution.py:318
  2.0 0.4 shard_map.51
  2.4 1.5 %collective-permute-start.6 = (f32[4,32,256]{2,1,0:T(8,128)S(1)}, f32[4,32,256]{2,1,0:T(8,128)S(1)}, u32[]{:S(2)}, u32[]{:S(2)}) collective-permute-start(f32[4,32,256]{2,1,0:T(8,128)S(1)} %get-tuple-element.33), channel_id=1, source_target_pairs={{0,1},{1,0},{2,3},{3,2},{4,5},{5,4},{6,7},{7,6},{8,9},{9,8},{10,11... | collective-permute-start | bytes 393224 | tf_op jit(solution)/shard_map/ppermute | solution.py:299
  3.8 0.1 collective-permute-start
  3.9 0.4 collective-permute-start.1
  4.4 0.1 collective-permute-start.5
  4.5 0.4 collective-permute-done.6
  4.9 1.4 %collective-permute-start.7 = (f32[4,32,256]{2,1,0:T(8,128)S(1)}, f32[4,32,256]{2,1,0:T(8,128)S(1)}, u32[]{:S(2)}, u32[]{:S(2)}) collective-permute-start(f32[4,32,256]{2,1,0:T(8,128)S(1)} %add.11), channel_id=1, source_target_pairs={{0,2},{2,0},{1,3},{3,1},{4,6},{6,4},{5,7},{7,5},{8,10},{10,8},{9,1... | collective-permute-start | bytes 393224 | tf_op jit(solution)/shard_map/ppermute | solution.py:299
  6.3 0.0 collective-permute-done.core_ref
  6.3 2.2 %collective-permute-start.3 = (f32[4,32,256]{2,1,0:T(8,128)S(1)}, f32[4,32,256]{2,1,0:T(8,128)S(1)}, u32[]{:S(2)}, u32[]{:S(2)}) collective-permute-start(f32[4,32,256]{2,1,0:T(8,128)S(1)} %add.10), channel_id=1, source_target_pairs={{0,2},{1,3},{2,0},{3,1},{4,4},{5,5},{6,6},{7,7},{8,8},{9,9},{10,10... | collective-permute-start | bytes 393224 | tf_op jit(solution)/shard_map/ppermute | solution.py:348
  8.5 0.0 collective-permute-done.1
  8.5 1.3 %collective-permute-start.2 = (f32[4,32,256]{2,1,0:T(8,128)S(1)}, f32[4,32,256]{2,1,0:T(8,128)S(1)}, u32[]{:S(2)}, u32[]{:S(2)}) collective-permute-start(f32[4,32,256]{2,1,0:T(8,128)S(1)} %add.9.passed_ref), channel_id=1, source_target_pairs={{0,2},{2,0},{1,3},{3,1},{4,6},{6,4},{5,7},{7,5},{8,10},{10,8},{9,1... | collective-permute-start | bytes 393224 | tf_op jit(solution)/shard_map/ppermute | solution.py:299
  9.8 0.0 collective-permute-done.5.core_ref
  9.8 0.0 collective-permute-done.7.chip_ref
  9.8 0.2 shard_map.53.near_ref
  10.0 1.7 %collective-permute-start.8 = (f32[4,32,256]{2,1,0:T(8,128)S(1)}, f32[4,32,256]{2,1,0:T(8,128)S(1)}, u32[]{:S(2)}, u32[]{:S(2)}) collective-permute-start(f32[4,32,256]{2,1,0:T(8,128)S(1)} %shard_map.53.near_ref), channel_id=1, source_target_pairs={{0,4},{4,0},{8,12},{12,8},{16,20},{20,16},{24,28},{28,24},{32,36},... | collective-permute-start | bytes 393224 | tf_op jit(solution)/shard_map/ppermute | solution.py:371
  11.7 0.9 %collective-permute-done.3.cross_ref = f32[4,32,256]{2,1,0:T(8,128)S(1)} collective-permute-done((f32[4,32,256]{2,1,0:T(8,128)S(1)}, f32[4,32,256]{2,1,0:T(8,128)S(1)}, u32[]{:S(2)}, u32[]{:S(2)}) %collective-permute-start.3) | collective-permute-done | bytes 131104 | tf_op jit(solution)/shard_map/ppermute | solution.py:348
  12.6 2.8 %collective-permute-done.2.chip_ref = f32[4,32,256]{2,1,0:T(8,128)S(1)} collective-permute-done((f32[4,32,256]{2,1,0:T(8,128)S(1)}, f32[4,32,256]{2,1,0:T(8,128)S(1)}, u32[]{:S(2)}, u32[]{:S(2)}) %collective-permute-start.2) | collective-permute-done | bytes 131104 | tf_op jit(solution)/shard_map/ppermute | solution.py:299
  15.4 0.5 shard_map.52
  15.9 0.0 copy-start
  15.9 5.4 %collective-permute-start.4 = (f32[4,32,256]{2,1,0:T(8,128)S(1)}, f32[4,32,256]{2,1,0:T(8,128)S(1)}, u32[]{:S(2)}, u32[]{:S(2)}) collective-permute-start(f32[4,32,256]{2,1,0:T(8,128)S(1)} %get-tuple-element.28), channel_id=1, source_target_pairs={{0,126},{1,127},{2,124},{3,125},{4,8},{5,9},{6,10},{7,11},{8,4},{9... | collective-permute-start | bytes 393224 | tf_op jit(solution)/shard_map/ppermute | solution.py:367
  21.3 1.6 %shard_map.54.curvature_ref = f32[8,8,32,256]{3,2,1,0:T(8,128)S(1)} custom-call(f32[8,8,32,256]{3,2,1,0:T(8,128)} %curvature_ref.1), custom_call_target="tpu_custom_call" | custom-call | bytes 4194304 | tf_op jit(solution)/shard_map/pallas_call | solution.py:340
  22.9 0.0 copy-done
  22.9 2.4 %shard_map.55 = (f32[8,8,32,256]{3,2,1,0:T(8,128)S(1)}, f32[8,128]{1,0:T(8,128)S(1)}) custom-call(f32[8,8,32,256]{3,2,1,0:T(8,128)S(1)} %copy-done, f32[8,8,32,256]{3,2,1,0:T(8,128)S(1)} %shard_map.54.curvature_ref), custom_call_target="tpu_custom_call" | custom-call | flops 13107200 | bytes 6291456 | tf_op jit(solution)/shard_map/pallas_call | solution.py:353
  25.3 0.0 collective-permute-done.8.near_halo_ref
  25.3 0.2 collective-permute-done.4.far_halo_ref
  25.5 0.8 %shard_map.56 = (f32[8,32,256]{2,1,0:T(8,128)S(1)}, f32[128,1,128]{2,1,0:T(1,128)S(1)}) custom-call(f32[4,32,256]{2,1,0:T(8,128)S(1)} %collective-permute-done.4.far_halo_ref, f32[4,32,256]{2,1,0:T(8,128)S(1)} %get-tuple-element.29.far_ref, f32[4,32,256]{2,1,0:T(8,128)S(1)} %shard_map.53.near_ref, f32[4,32,256]{2,1,0:T(8,128)S(1)} %collective-permute-done.8.near_halo_ref, ...), custom_call_target="tpu_custom_call" | custom-call | flops 3932160 | bytes 5242880 | tf_op jit(solution)/shard_map/pallas_call | solution.py:372
  26.3 18.0 %all_to_all.5.rows_ref = f32[128,1,128]{2,1,0:T(1,128)S(1)} all-to-all(f32[128,1,128]{2,1,0:T(1,128)S(1)} %get-tuple-element.36), channel_id=1, replica_groups=mesh['cuts_0'=2,'cuts_1'=4,'cuts_2'=4,'event_0'=2,'event_1'=2] {'cuts_0'..., dimensions={0} | all-to-all | bytes 131072 | tf_op jit(solution)/shard_map/all_to_all | solution.py:379
  44.2 1.2 %shard_map.57 = (f32[8,32,256]{2,1,0:T(8,128)}, f32[8,32,256]{2,1,0:T(8,128)}) custom-call(f32[128,1,128]{2,1,0:T(1,128)S(1)} %all_to_all.5.rows_ref, f32[8,32,256]{2,1,0:T(8,128)S(1)} %get-tuple-element.37.gradient_ref, f32[8,8,32,256]{3,2,1,0:T(8,128)S(1)} %copy-done, f32[8,8,32,256]{3,2,1,0:T(8,128)S(1)} %get-tuple-element.34.changes_ref), custom_call_target="tpu_custom_call" | custom-call | flops 2228224 | bytes 4718592 | tf_op jit(solution)/shard_map/pallas_call | solution.py:380
  (3 shorter events, 0.1 us)
Async XLA Ops:
  2.4 2.4 %collective-permute-start.6 = (f32[4,32,256]{2,1,0:T(8,128)S(1)}, f32[4,32,256]{2,1,0:T(8,128)S(1)}, u32[]{:S(2)}, u32[]{:S(2)}) collective-permute-start(f32[4,32,256]{2,1,0:T(8,128)S(1)} %get-tuple-element.33), channel_id=1, source_target_pairs={{0,1},{1,0},{2,3},{3,2},{4,5},{5,4},{6,7},{7,6},{8,9},{9,8},{10,11... | collective-permute-start | bytes 393224 | tf_op jit(solution)/shard_map/ppermute | solution.py:299
  3.8 2.4 %collective-permute-start = (f32[4,32,256]{2,1,0:T(8,128)S(1)}, f32[4,32,256]{2,1,0:T(8,128)S(1)}, u32[]{:S(2)}, u32[]{:S(2)}) collective-permute-start(f32[4,32,256]{2,1,0:T(8,128)S(1)} %get-tuple-element.21), channel_id=1, source_target_pairs={{0,1},{1,0},{2,3},{3,2},{4,5},{5,4},{6,7},{7,6},{8,9},{9,8},{10,11... | collective-permute-start | bytes 393224 | tf_op jit(solution)/shard_map/ppermute | solution.py:299
  3.9 4.5 %collective-permute-start.1 = (f32[4,32,256]{2,1,0:T(8,128)S(1)}, f32[4,32,256]{2,1,0:T(8,128)S(1)}, u32[]{:S(2)}, u32[]{:S(2)}) collective-permute-start(f32[4,32,256]{2,1,0:T(8,128)S(1)} %get-tuple-element.23), channel_id=1, source_target_pairs={{0,1},{1,0},{2,3},{3,2},{4,5},{5,4},{6,7},{7,6},{8,9},{9,8},{10,11... | collective-permute-start | bytes 393224 | tf_op jit(solution)/shard_map/ppermute | solution.py:299
  4.4 5.4 %collective-permute-start.5 = (f32[4,32,256]{2,1,0:T(8,128)S(1)}, f32[4,32,256]{2,1,0:T(8,128)S(1)}, u32[]{:S(2)}, u32[]{:S(2)}) collective-permute-start(f32[4,32,256]{2,1,0:T(8,128)S(1)} %get-tuple-element.31), channel_id=1, source_target_pairs={{0,1},{1,0},{2,3},{3,2},{4,5},{5,4},{6,7},{7,6},{8,9},{9,8},{10,11... | collective-permute-start | bytes 393224 | tf_op jit(solution)/shard_map/ppermute | solution.py:299
  4.9 4.9 %collective-permute-start.7 = (f32[4,32,256]{2,1,0:T(8,128)S(1)}, f32[4,32,256]{2,1,0:T(8,128)S(1)}, u32[]{:S(2)}, u32[]{:S(2)}) collective-permute-start(f32[4,32,256]{2,1,0:T(8,128)S(1)} %add.11), channel_id=1, source_target_pairs={{0,2},{2,0},{1,3},{3,1},{4,6},{6,4},{5,7},{7,5},{8,10},{10,8},{9,1... | collective-permute-start | bytes 393224 | tf_op jit(solution)/shard_map/ppermute | solution.py:299
  6.3 6.3 %collective-permute-start.3 = (f32[4,32,256]{2,1,0:T(8,128)S(1)}, f32[4,32,256]{2,1,0:T(8,128)S(1)}, u32[]{:S(2)}, u32[]{:S(2)}) collective-permute-start(f32[4,32,256]{2,1,0:T(8,128)S(1)} %add.10), channel_id=1, source_target_pairs={{0,2},{1,3},{2,0},{3,1},{4,4},{5,5},{6,6},{7,7},{8,8},{9,9},{10,10... | collective-permute-start | bytes 393224 | tf_op jit(solution)/shard_map/ppermute | solution.py:348
  8.5 6.9 %collective-permute-start.2 = (f32[4,32,256]{2,1,0:T(8,128)S(1)}, f32[4,32,256]{2,1,0:T(8,128)S(1)}, u32[]{:S(2)}, u32[]{:S(2)}) collective-permute-start(f32[4,32,256]{2,1,0:T(8,128)S(1)} %add.9.passed_ref), channel_id=1, source_target_pairs={{0,2},{2,0},{1,3},{3,1},{4,6},{6,4},{5,7},{7,5},{8,10},{10,8},{9,1... | collective-permute-start | bytes 393224 | tf_op jit(solution)/shard_map/ppermute | solution.py:299
  10.0 15.3 %collective-permute-start.8 = (f32[4,32,256]{2,1,0:T(8,128)S(1)}, f32[4,32,256]{2,1,0:T(8,128)S(1)}, u32[]{:S(2)}, u32[]{:S(2)}) collective-permute-start(f32[4,32,256]{2,1,0:T(8,128)S(1)} %shard_map.53.near_ref), channel_id=1, source_target_pairs={{0,4},{4,0},{8,12},{12,8},{16,20},{20,16},{24,28},{28,24},{32,36},... | collective-permute-start | bytes 393224 | tf_op jit(solution)/shard_map/ppermute | solution.py:371
  15.9 7.0 %copy-start = (f32[8,8,32,256]{3,2,1,0:T(8,128)S(1)}, f32[8,8,32,256]{3,2,1,0:T(8,128)}, u32[]{:S(2)}) copy-start(f32[8,8,32,256]{3,2,1,0:T(8,128)} %steps_ref.5) | copy-start | bytes 6291460
  15.9 9.6 %collective-permute-start.4 = (f32[4,32,256]{2,1,0:T(8,128)S(1)}, f32[4,32,256]{2,1,0:T(8,128)S(1)}, u32[]{:S(2)}, u32[]{:S(2)}) collective-permute-start(f32[4,32,256]{2,1,0:T(8,128)S(1)} %get-tuple-element.28), channel_id=1, source_target_pairs={{0,126},{1,127},{2,124},{3,125},{4,8},{5,9},{6,10},{7,11},{8,4},{9... | collective-permute-start | bytes 393224 | tf_op jit(solution)/shard_map/ppermute | solution.py:367

commit v10 on v8

--- a/solution.py
+++ b/solution.py
@@ -78,12 +78,16 @@
     part = 2 * lax.axis_index("event_0") + lax.axis_index("event_1")
     rows = length // 4
     local = lax.broadcasted_iota(jnp.int32, (rows, length), 0)
-    order = [part, part ^ 2, part ^ 1, part ^ 3]
-    matrix = jnp.concatenate(
-        [gauss_rows(length, 3.0, local + rows * block, 1) for block in order], axis=0
-    )
-    weights = jnp.concatenate([jnp.concatenate([m, m], axis=1) for m in split(matrix)], axis=0)
-    weights_ref[...] = weights
+
+    def weights_of(first):
+        order = [first, first ^ 2, first ^ 1, first ^ 3]
+        matrix = jnp.concatenate(
+            [gauss_rows(length, 3.0, local + rows * block, 1) for block in order], axis=0
+        )
+        return jnp.concatenate([jnp.concatenate([m, m], axis=1) for m in split(matrix)], axis=0)
+
+    weights = weights_of(jnp.where(cut_number() == 0, part ^ 2, part))
+    weights_ref[...] = weights_of(part)
     copies[0].wait()
     radial_products(far_ref, weights, keep_ref, pass_ref, send_keep_ref, send_pass_ref)
     copies[1].wait()
@@ -332,8 +336,15 @@
         return call(latitude_kernel, [half], 4 * lats * size, 8 * size)(*parts, high, low)[0]
 
     far_plane = plane_of(far_keep, far_core, far_chip)
-    far_halo = lax.ppermute(
-        far_plane, CUTS, [(c, (((c - 1) ^ 1) + 1) % cuts) for c in range(1, cuts)] + [(0, cuts - 1)]
+    pairs = []
+    for c in range(cuts):
+        other, flip = (((c - 1) ^ 1) + 1) % cuts if c else cuts - 1, 2 if c == 0 else 0
+        pairs += [(c * events + e, other * events + (e ^ flip)) for e in range(events)]
+    far_halo = lax.ppermute(far_plane, CUTS_EVENT, pairs)
+    far_plane = lax.ppermute(
+        far_plane,
+        CUTS_EVENT,
+        [(e, e ^ 2) for e in range(events)] + [(d, d) for d in range(events, cuts * events)],
     )
     near_plane = plane_of(near_keep, near_core, near_chip)
     near_halo = lax.ppermute(near_plane, CUTS, [(c, c ^ 1) for c in range(cuts)])

time: 43.9 us -> 44 us (level)
    ppermute x1 -> x2, waiting for transfers between devices: 2 us -> 0.83 us  [the longest x1 0.83 us: shards(): far_halo = lax.ppermute(far_plane, CUTS_EVENT, pairs)]
    ppermute x1, waiting for transfers between devices: 0.01 us -> 0.83 us  [shards(): lax.ppermute(near_plane, CUTS, [(c, c ^ 1) for c in range(cuts)])]
    ppermute x1 -> x2, starting transfers between devices: 8.86 us -> 9.27 us  [the longest x1 6.03 us: shards(): far_halo = lax.ppermute(far_plane, CUTS_EVENT, pairs)]
  transfers between devices with their start and end apart: 8 -> 9, of which waited for: 3 -> 4; matrix products, arithmetic and copies ran while one was open for 0% -> 0% of each run, Pallas kernels for 11% -> 11%
where the time goes in v10:
time: 44 us; the launch traced here: 43.8 us
  blocking collectives  18.6 us (42%)
  starting transfers between devices  13.7 us (31%)
  Pallas kernels  8.15 us (19%)
  waiting for transfers between devices  2.64 us (6%)
  between operations  0.74 us (2%)
    all_to_all x1, blocking collectives, shards(): arrived = lax.all_to_all(outgoing, CUTS_EVENT, 0, 0, tiled=True)  18.6 us
    ppermute x1, starting transfers between devices, shards(): far_halo = lax.ppermute(far_plane, CUTS_EVENT, pairs)  6.03 us
    ppermute x6, starting transfers between devices, swapped(): return lax.ppermute(x, axis, [(0, 1), (1, 0)])  4.32 us
    ppermute x1, starting transfers between devices, shards(): lax.ppermute(far_plane, CUTS_EVENT, [(e, e ^ 2) for e in range(events)] +...  3.24 us
    pallas_call x1, Pallas kernels, shards(): call(gram_kernel, [(steps.shape, jnp.float32), ((8, LANES), jnp.float32)]...  2.41 us
    pallas_call x1, Pallas kernels, shards(): call(fetch_kernel, [(curvature.shape, jnp.float32), square, square], 10 *...  1.6 us
    pallas_call x1, Pallas kernels, shards(): call(far_radial_kernel, [half] * 4 + [((RIM, rad_len, lats), jnp.float32)...  1.39 us
    pallas_call x1, Pallas kernels, shards(): call(direction_kernel, [block] * 2, 2 * 17 * size, 4 * 18 * size, out_spe...  1.25 us
  transfers between devices with their start and end apart: 9, of which 4 were waited for; matrix products, arithmetic and copies ran while one was open for 0% of the time, Pallas kernels for 11%

profile of v10, /device:TPU:1, one launch (start us, length us, event | category | flops | bytes accessed | tf_op | source)
XLA Modules:
  0.0 43.8 jit_solution(17952644051668156918)
XLA Ops:
  0.6 1.4 %shard_map.50 = (f32[4,32,256]{2,1,0:T(8,128)S(1)}, f32[4,32,256]{2,1,0:T(8,128)S(1)}, f32[4,32,256]{2,1,0:T(8,128)S(1)}, f32[4,32,256]{2,1,0:T(8,128)S(1)}, f32...) custom-call(f32[1,8,128,256]{3,2,1,0:T(8,128)} %kernels_ref.1), custom_call_target="tpu_custom_call" | custom-call | flops 134217728 | bytes 2097152 | tf_op jit(solution)/shard_map/pallas_call | solution.py:299
  2.0 1.5 %collective-permute-start.1 = (f32[4,32,256]{2,1,0:T(8,128)S(1)}, f32[4,32,256]{2,1,0:T(8,128)S(1)}, u32[]{:S(2)}, u32[]{:S(2)}) collective-permute-start(f32[4,32,256]{2,1,0:T(8,128)S(1)} %get-tuple-element.22), channel_id=1, source_target_pairs={{0,1},{1,0},{2,3},{3,2},{4,5},{5,4},{6,7},{7,6},{8,9},{9,8},{10,11... | collective-permute-start | bytes 393224 | tf_op jit(solution)/shard_map/ppermute | solution.py:280
  3.5 0.3 shard_map.53
  3.8 0.1 collective-permute-start.6
  3.9 0.5 %collective-permute-start = (f32[4,32,256]{2,1,0:T(8,128)S(1)}, f32[4,32,256]{2,1,0:T(8,128)S(1)}, u32[]{:S(2)}, u32[]{:S(2)}) collective-permute-start(f32[4,32,256]{2,1,0:T(8,128)S(1)} %get-tuple-element.20), channel_id=1, source_target_pairs={{0,1},{1,0},{2,3},{3,2},{4,5},{5,4},{6,7},{7,6},{8,9},{9,8},{10,11... | collective-permute-start | bytes 393224 | tf_op jit(solution)/shard_map/ppermute | solution.py:280
  4.4 0.1 collective-permute-done.1
  4.5 0.0 copy-start
  4.5 1.4 %collective-permute-start.2 = (f32[4,32,256]{2,1,0:T(8,128)S(1)}, f32[4,32,256]{2,1,0:T(8,128)S(1)}, u32[]{:S(2)}, u32[]{:S(2)}) collective-permute-start(f32[4,32,256]{2,1,0:T(8,128)S(1)} %add.6), channel_id=1, source_target_pairs={{0,2},{2,0},{1,3},{3,1},{4,6},{6,4},{5,7},{7,5},{8,10},{10,8},{9,1... | collective-permute-start | bytes 393224 | tf_op jit(solution)/shard_map/ppermute | solution.py:280
  5.9 0.6 %collective-permute-start.5 = (f32[4,32,256]{2,1,0:T(8,128)S(1)}, f32[4,32,256]{2,1,0:T(8,128)S(1)}, u32[]{:S(2)}, u32[]{:S(2)}) collective-permute-start(f32[4,32,256]{2,1,0:T(8,128)S(1)} %get-tuple-element.28), channel_id=1, source_target_pairs={{0,1},{1,0},{2,3},{3,2},{4,5},{5,4},{6,7},{7,6},{8,9},{9,8},{10,11... | collective-permute-start | bytes 393224 | tf_op jit(solution)/shard_map/ppermute | solution.py:280
  6.6 0.0 collective-permute-done.6
  6.6 0.2 collective-permute-start.7
  6.8 1.6 %shard_map.51 = (f32[8,8,32,256]{3,2,1,0:T(8,128)S(1)}, bf16[256,256]{1,0:T(8,128)(2,1)S(1)}, bf16[256,256]{1,0:T(8,128)(2,1)S(1)}) custom-call(f32[8,8,32,256]{3,2,1,0:T(8,128)} %curvature_ref.1), custom_call_target="tpu_custom_call" | custom-call | flops 655360 | bytes 4194304 | tf_op jit(solution)/shard_map/pallas_call | solution.py:317
  8.4 0.0 collective-permute-done.core_ref
  8.4 0.9 %collective-permute-done.2.chip_ref = f32[4,32,256]{2,1,0:T(8,128)S(1)} collective-permute-done((f32[4,32,256]{2,1,0:T(8,128)S(1)}, f32[4,32,256]{2,1,0:T(8,128)S(1)}, u32[]{:S(2)}, u32[]{:S(2)}) %collective-permute-start.2) | collective-permute-done | bytes 131104 | tf_op jit(solution)/shard_map/ppermute | solution.py:280
  9.3 0.2 shard_map.52
  9.5 3.2 %collective-permute-start.4 = (f32[4,32,256]{2,1,0:T(8,128)S(1)}, f32[4,32,256]{2,1,0:T(8,128)S(1)}, u32[]{:S(2)}, u32[]{:S(2)}) collective-permute-start(f32[4,32,256]{2,1,0:T(8,128)S(1)} %shard_map.52), channel_id=1, source_target_pairs={{0,2},{1,3},{2,0},{3,1},{4,4},{5,5},{6,6},{7,7},{8,8},{9,9},{10,10... | collective-permute-start | bytes 393224 | tf_op jit(solution)/shard_map/ppermute | solution.py:344
  12.8 6.0 %collective-permute-start.3 = (f32[4,32,256]{2,1,0:T(8,128)S(1)}, f32[4,32,256]{2,1,0:T(8,128)S(1)}, u32[]{:S(2)}, u32[]{:S(2)}) collective-permute-start(f32[4,32,256]{2,1,0:T(8,128)S(1)} %shard_map.52), channel_id=1, source_target_pairs={{0,126},{1,127},{2,124},{3,125},{4,8},{5,9},{6,10},{7,11},{8,4},{9... | collective-permute-start | bytes 393224 | tf_op jit(solution)/shard_map/ppermute | solution.py:343
  18.8 0.0 collective-permute-done.5.core_ref
  18.8 0.0 collective-permute-done.7.chip_ref
  18.8 0.2 shard_map.54.near_ref
  19.0 0.1 collective-permute-start.8
  19.1 0.0 copy-done
  19.1 2.4 %shard_map.55 = (f32[8,8,32,256]{3,2,1,0:T(8,128)S(1)}, f32[8,128]{1,0:T(8,128)S(1)}) custom-call(f32[8,8,32,256]{3,2,1,0:T(8,128)S(1)} %copy-done, f32[8,8,32,256]{3,2,1,0:T(8,128)S(1)} %get-tuple-element.31.curvature_ref), custom_call_target="tpu_custom_call" | custom-call | flops 13107200 | bytes 6291456 | tf_op jit(solution)/shard_map/pallas_call | solution.py:328
  21.5 0.0 collective-permute-done.4.far_ref
  21.6 0.8 %collective-permute-done.3.far_halo_ref = f32[4,32,256]{2,1,0:T(8,128)S(1)} collective-permute-done((f32[4,32,256]{2,1,0:T(8,128)S(1)}, f32[4,32,256]{2,1,0:T(8,128)S(1)}, u32[]{:S(2)}, u32[]{:S(2)}) %collective-permute-start.3) | collective-permute-done | bytes 131104 | tf_op jit(solution)/shard_map/ppermute | solution.py:343
  22.4 0.8 %collective-permute-done.8.near_halo_ref = f32[4,32,256]{2,1,0:T(8,128)S(1)} collective-permute-done((f32[4,32,256]{2,1,0:T(8,128)S(1)}, f32[4,32,256]{2,1,0:T(8,128)S(1)}, u32[]{:S(2)}, u32[]{:S(2)}) %collective-permute-start.8) | collective-permute-done | bytes 131104 | tf_op jit(solution)/shard_map/ppermute | solution.py:350
  23.2 0.8 %shard_map.56 = (f32[8,32,256]{2,1,0:T(8,128)S(1)}, f32[128,1,128]{2,1,0:T(1,128)S(1)}) custom-call(f32[4,32,256]{2,1,0:T(8,128)S(1)} %collective-permute-done.3.far_halo_ref, f32[4,32,256]{2,1,0:T(8,128)S(1)} %collective-permute-done.4.far_ref, f32[4,32,256]{2,1,0:T(8,128)S(1)} %shard_map.54.near_ref, ...), custom_call_target="tpu_custom_call" | custom-call | flops 3932160 | bytes 5242880 | tf_op jit(solution)/shard_map/pallas_call | solution.py:351
  24.0 18.6 %all_to_all.5.rows_ref = f32[128,1,128]{2,1,0:T(1,128)S(1)} all-to-all(f32[128,1,128]{2,1,0:T(1,128)S(1)} %get-tuple-element.34), channel_id=1, replica_groups=mesh['cuts_0'=2,'cuts_1'=4,'cuts_2'=4,'event_0'=2,'event_1'=2] {'cuts_0'..., dimensions={0} | all-to-all | bytes 131072 | tf_op jit(solution)/shard_map/all_to_all | solution.py:358
  42.6 1.2 %shard_map.57 = (f32[8,32,256]{2,1,0:T(8,128)}, f32[8,32,256]{2,1,0:T(8,128)}) custom-call(f32[128,1,128]{2,1,0:T(1,128)S(1)} %all_to_all.5.rows_ref, f32[8,32,256]{2,1,0:T(8,128)S(1)} %get-tuple-element.35.gradient_ref, f32[8,8,32,256]{3,2,1,0:T(8,128)S(1)} %copy-done, f32[8,8,32,256]{3,2,1,0:T(8,128)S(1)} %get-tuple-element.32.changes_ref), custom_call_target="tpu_custom_call" | custom-call | flops 2228224 | bytes 4718592 | tf_op jit(solution)/shard_map/pallas_call | solution.py:359
  (2 shorter events, 0.0 us)
Async XLA Ops:
  2.0 2.4 %collective-permute-start.1 = (f32[4,32,256]{2,1,0:T(8,128)S(1)}, f32[4,32,256]{2,1,0:T(8,128)S(1)}, u32[]{:S(2)}, u32[]{:S(2)}) collective-permute-start(f32[4,32,256]{2,1,0:T(8,128)S(1)} %get-tuple-element.22), channel_id=1, source_target_pairs={{0,1},{1,0},{2,3},{3,2},{4,5},{5,4},{6,7},{7,6},{8,9},{9,8},{10,11... | collective-permute-start | bytes 393224 | tf_op jit(solution)/shard_map/ppermute | solution.py:280
  3.8 2.8 %collective-permute-start.6 = (f32[4,32,256]{2,1,0:T(8,128)S(1)}, f32[4,32,256]{2,1,0:T(8,128)S(1)}, u32[]{:S(2)}, u32[]{:S(2)}) collective-permute-start(f32[4,32,256]{2,1,0:T(8,128)S(1)} %get-tuple-element.30), channel_id=1, source_target_pairs={{0,1},{1,0},{2,3},{3,2},{4,5},{5,4},{6,7},{7,6},{8,9},{9,8},{10,11... | collective-permute-start | bytes 393224 | tf_op jit(solution)/shard_map/ppermute | solution.py:280
  3.9 4.5 %collective-permute-start = (f32[4,32,256]{2,1,0:T(8,128)S(1)}, f32[4,32,256]{2,1,0:T(8,128)S(1)}, u32[]{:S(2)}, u32[]{:S(2)}) collective-permute-start(f32[4,32,256]{2,1,0:T(8,128)S(1)} %get-tuple-element.20), channel_id=1, source_target_pairs={{0,1},{1,0},{2,3},{3,2},{4,5},{5,4},{6,7},{7,6},{8,9},{9,8},{10,11... | collective-permute-start | bytes 393224 | tf_op jit(solution)/shard_map/ppermute | solution.py:280
  4.5 14.6 %copy-start = (f32[8,8,32,256]{3,2,1,0:T(8,128)S(1)}, f32[8,8,32,256]{3,2,1,0:T(8,128)}, u32[]{:S(2)}) copy-start(f32[8,8,32,256]{3,2,1,0:T(8,128)} %steps_ref.5) | copy-start | bytes 6291460
  4.5 4.8 %collective-permute-start.2 = (f32[4,32,256]{2,1,0:T(8,128)S(1)}, f32[4,32,256]{2,1,0:T(8,128)S(1)}, u32[]{:S(2)}, u32[]{:S(2)}) collective-permute-start(f32[4,32,256]{2,1,0:T(8,128)S(1)} %add.6), channel_id=1, source_target_pairs={{0,2},{2,0},{1,3},{3,1},{4,6},{6,4},{5,7},{7,5},{8,10},{10,8},{9,1... | collective-permute-start | bytes 393224 | tf_op jit(solution)/shard_map/ppermute | solution.py:280
  5.9 12.9 %collective-permute-start.5 = (f32[4,32,256]{2,1,0:T(8,128)S(1)}, f32[4,32,256]{2,1,0:T(8,128)S(1)}, u32[]{:S(2)}, u32[]{:S(2)}) collective-permute-start(f32[4,32,256]{2,1,0:T(8,128)S(1)} %get-tuple-element.28), channel_id=1, source_target_pairs={{0,1},{1,0},{2,3},{3,2},{4,5},{5,4},{6,7},{7,6},{8,9},{9,8},{10,11... | collective-permute-start | bytes 393224 | tf_op jit(solution)/shard_map/ppermute | solution.py:280
  6.6 12.2 %collective-permute-start.7 = (f32[4,32,256]{2,1,0:T(8,128)S(1)}, f32[4,32,256]{2,1,0:T(8,128)S(1)}, u32[]{:S(2)}, u32[]{:S(2)}) collective-permute-start(f32[4,32,256]{2,1,0:T(8,128)S(1)} %add.7), channel_id=1, source_target_pairs={{0,2},{2,0},{1,3},{3,1},{4,6},{6,4},{5,7},{7,5},{8,10},{10,8},{9,1... | collective-permute-start | bytes 393224 | tf_op jit(solution)/shard_map/ppermute | solution.py:280
  9.5 12.0 %collective-permute-start.4 = (f32[4,32,256]{2,1,0:T(8,128)S(1)}, f32[4,32,256]{2,1,0:T(8,128)S(1)}, u32[]{:S(2)}, u32[]{:S(2)}) collective-permute-start(f32[4,32,256]{2,1,0:T(8,128)S(1)} %shard_map.52), channel_id=1, source_target_pairs={{0,2},{1,3},{2,0},{3,1},{4,4},{5,5},{6,6},{7,7},{8,8},{9,9},{10,10... | collective-permute-start | bytes 393224 | tf_op jit(solution)/shard_map/ppermute | solution.py:344
  12.8 9.6 %collective-permute-start.3 = (f32[4,32,256]{2,1,0:T(8,128)S(1)}, f32[4,32,256]{2,1,0:T(8,128)S(1)}, u32[]{:S(2)}, u32[]{:S(2)}) collective-permute-start(f32[4,32,256]{2,1,0:T(8,128)S(1)} %shard_map.52), channel_id=1, source_target_pairs={{0,126},{1,127},{2,124},{3,125},{4,8},{5,9},{6,10},{7,11},{8,4},{9... | collective-permute-start | bytes 393224 | tf_op jit(solution)/shard_map/ppermute | solution.py:343
  19.0 4.2 %collective-permute-start.8 = (f32[4,32,256]{2,1,0:T(8,128)S(1)}, f32[4,32,256]{2,1,0:T(8,128)S(1)}, u32[]{:S(2)}, u32[]{:S(2)}) collective-permute-start(f32[4,32,256]{2,1,0:T(8,128)S(1)} %shard_map.54.near_ref), channel_id=1, source_target_pairs={{0,4},{4,0},{8,12},{12,8},{16,20},{20,16},{24,28},{28,24},{32,36},... | collective-permute-start | bytes 393224 | tf_op jit(solution)/shard_map/ppermute | solution.py:350

commit v11 on v10

--- a/solution.py
+++ b/solution.py
@@ -1,3 +1,4 @@
+import functools
 import math
 
 import jax
@@ -93,8 +94,15 @@
     copies[1].wait()
 
 
-def near_radial_kernel(near_ref, weights_ref, keep_ref, pass_ref, send_keep_ref, send_pass_ref):
-    radial_products(near_ref, weights_ref[...], keep_ref, pass_ref, send_keep_ref, send_pass_ref)
+def near_radial_kernel(
+    near_ref, weights_ref, far_send_keep_ref, keep_ref, pass_ref, rest_ref, high_ref, low_ref
+):
+    rest_ref[2] = far_send_keep_ref[...]
+    parts = (keep_ref, pass_ref, rest_ref.at[1], rest_ref.at[0])
+    radial_products(near_ref, weights_ref[...], *parts)
+    lats = high_ref.shape[0]
+    column = lax.broadcasted_iota(jnp.int32, (lats, lats), 1)
+    high_ref[...], low_ref[...] = split(gauss_rows(lats, 4.0, column, 0))
 
 
 def smoothed(field, high, low):
@@ -104,18 +112,9 @@
     return out[:count] + out[count:]
 
 
-def fetch_kernel(curvature_ref, held_ref, high_ref, low_ref, semaphore):
-    copy = pltpu.make_async_copy(curvature_ref, held_ref, semaphore)
-    copy.start()
-    lats = high_ref.shape[0]
-    column = lax.broadcasted_iota(jnp.int32, (lats, lats), 1)
-    high_ref[...], low_ref[...] = split(gauss_rows(lats, 4.0, column, 0))
-    copy.wait()
-
-
-def latitude_kernel(keep_ref, core_ref, chip_ref, high_ref, low_ref, plane_ref):
+def latitude_kernel(slot, keep_ref, rest_ref, chip_ref, high_ref, low_ref, plane_ref):
     lons, rows, lats = plane_ref.shape
-    summed = (keep_ref[...] + core_ref[...] + chip_ref[...]).reshape(lons * rows, lats)
+    summed = (keep_ref[...] + rest_ref[slot] + chip_ref[...]).reshape(lons * rows, lats)
     plane_ref[...] = smoothed(summed, high_ref[...], low_ref[...]).reshape(lons, rows, lats)
 
 
@@ -140,8 +139,16 @@
     return row
 
 
-def gram_kernel(steps_ref, curvature_ref, changes_ref, row_ref):
+def gram_kernel(steps_ref, curvature_hbm, changes_ref, row_ref, curvature_ref, semaphores):
     lons, rows, lats = steps_ref.shape[1:]
+
+    def fetch(a):
+        return pltpu.make_async_copy(
+            curvature_hbm.at[:, a], curvature_ref.at[:, a], semaphores.at[a]
+        )
+
+    for a in range(lons):
+        fetch(a).start()
     spots = [
         (slice(8 * r, 8 * r + 8), slice(LANES * b, LANES * (b + 1)))
         for r in range(rows // 8)
@@ -151,6 +158,7 @@
     upper = [(i, j) for i in range(PAIRS) for j in range(i, PAIRS)]
 
     def first(a, sums):
+        fetch(a).wait()
         for at in spots:
             steps = [steps_ref[(i, a, *at)] for i in range(half)]
             changes = [None] * PAIRS
@@ -308,34 +316,30 @@
         ],
     )(in_hbm(kernels))
     far_core_pass = swapped(far_send_pass, "event_1")
-    near_keep, near_pass, near_send_keep, near_send_pass = call(
-        near_radial_kernel, [half] * 4, flops, 4 * kernels.size
-    )(near_field, weights)
+    square = ((lats, lats), jnp.bfloat16)
+    near_keep, near_pass, rest, high, low = call(
+        near_radial_kernel,
+        [half, half, ((3, RIM, rows, lats), jnp.float32), square, square],
+        flops,
+        4 * kernels.size,
+    )(near_field, weights, far_send_keep)
     far_chip = swapped(far_pass + far_core_pass, "event_0")
-    near_core_pass = swapped(near_send_pass, "event_1")
-    square = ((lats, lats), jnp.bfloat16)
-    held_curvature, high, low = call(
-        fetch_kernel,
-        [(curvature.shape, jnp.float32), square, square],
-        10 * lats * lats,
-        8 * curvature.size,
-        in_specs=[pl.BlockSpec(memory_space=pltpu.HBM)],
-        scratch_shapes=[pltpu.SemaphoreType.DMA],
-    )(in_hbm(curvature))
-    near_chip = swapped(near_pass + near_core_pass, "event_0")
-    far_core = swapped(far_send_keep, "event_1")
-    near_core = swapped(near_send_keep, "event_1")
+    rest = swapped(rest, "event_1")
+    near_chip = swapped(near_pass + rest[0], "event_0")
     changes, gram = call(
         gram_kernel,
         [(steps.shape, jnp.float32), ((8, LANES), jnp.float32)],
         2 * 100 * size,
         12 * steps.size,
-    )(steps, held_curvature)
-
-    def plane_of(*parts):
-        return call(latitude_kernel, [half], 4 * lats * size, 8 * size)(*parts, high, low)[0]
-
-    far_plane = plane_of(far_keep, far_core, far_chip)
+        in_specs=[pl.BlockSpec(memory_space=pltpu.VMEM), pl.BlockSpec(memory_space=pltpu.HBM)],
+        scratch_shapes=[pltpu.VMEM(curvature.shape, jnp.float32), pltpu.SemaphoreType.DMA((lons,))],
+    )(steps, in_hbm(curvature))
+
+    def plane_of(slot, *parts):
+        kernel = functools.partial(latitude_kernel, slot)
+        return call(kernel, [half], 4 * lats * size, 8 * size)(*parts, high, low)[0]
+
+    far_plane = plane_of(2, far_keep, rest, far_chip)
     pairs = []
     for c in range(cuts):
         other, flip = (((c - 1) ^ 1) + 1) % cuts if c else cuts - 1, 2 if c == 0 else 0
@@ -346,7 +350,7 @@
         CUTS_EVENT,
         [(e, e ^ 2) for e in range(events)] + [(d, d) for d in range(events, cuts * events)],
     )
-    near_plane = plane_of(near_keep, near_core, near_chip)
+    near_plane = plane_of(1, near_keep, rest, near_chip)
     near_halo = lax.ppermute(near_plane, CUTS, [(c, c ^ 1) for c in range(cuts)])
     gradient, outgoing = call(
         product_kernel,

time: 44 us -> 44.9 us (1.020)
  waiting for transfers between devices: 2.64 us -> 5.2 us
  starting transfers between devices: 13.7 us -> 12.5 us
  Pallas kernels: 8.15 us -> 7.64 us
    ppermute x6 -> x4, waiting for transfers between devices: 0.97 us -> 4.56 us  [swapped(): return lax.ppermute(x, axis, [(0, 1), (1, 0)])]
    pallas_call x4 -> x3, Pallas kernels: 2.34 us -> 0.81 us  [the longest x2 0.45 us: plane_of(): return call(kernel, [half], 4 * lats * size, 8 * size)(*parts, high, low)[0]]
    ppermute x6 -> x4, starting transfers between devices: 4.32 us -> 3.18 us  [swapped(): return lax.ppermute(x, axis, [(0, 1), (1, 0)])]
    pallas_call x1, Pallas kernels: 2.41 us -> 3.43 us  [shards(): call(gram_kernel, [(steps.shape, jnp.float32), ((8, LANES), jnp.float32)]...]
    ppermute x1, waiting for transfers between devices: 0.83 us -> 0.01 us  [shards(): far_halo = lax.ppermute(far_plane, CUTS_EVENT, pairs)]
  transfers between devices with their start and end apart: 9 -> 7, of which waited for: 4 -> 3; matrix products, arithmetic and copies ran while one was open for 0% -> 0% of each run, Pallas kernels for 11% -> 9%
where the time goes in v11:
time: 44.9 us; the launch traced here: 44.7 us
  blocking collectives  18.6 us (41%)
  starting transfers between devices  12.5 us (28%)
  Pallas kernels  7.64 us (17%)
  waiting for transfers between devices  5.2 us (12%)
  between operations  0.73 us (2%)
    all_to_all x1, blocking collectives, shards(): arrived = lax.all_to_all(outgoing, CUTS_EVENT, 0, 0, tiled=True)  18.6 us
    ppermute x1, starting transfers between devices, shards(): far_halo = lax.ppermute(far_plane, CUTS_EVENT, pairs)  6.03 us
    ppermute x4, waiting for transfers between devices, swapped(): return lax.ppermute(x, axis, [(0, 1), (1, 0)])  4.56 us
    pallas_call x1, Pallas kernels, shards(): call(gram_kernel, [(steps.shape, jnp.float32), ((8, LANES), jnp.float32)]...  3.43 us
    ppermute x1, starting transfers between devices, shards(): lax.ppermute(far_plane, CUTS_EVENT, [(e, e ^ 2) for e in range(events)] +...  3.23 us
    ppermute x4, starting transfers between devices, swapped(): return lax.ppermute(x, axis, [(0, 1), (1, 0)])  3.18 us
    pallas_call x1, Pallas kernels, shards(): call(far_radial_kernel, [half] * 4 + [((RIM, rad_len, lats), jnp.float32)...  1.39 us
    pallas_call x1, Pallas kernels, shards(): call(direction_kernel, [block] * 2, 2 * 17 * size, 4 * 18 * size, out_spe...  1.25 us
  transfers between devices with their start and end apart: 7, of which 3 were waited for; matrix products, arithmetic and copies ran while one was open for 0% of the time, Pallas kernels for 9%

profile of v11, /device:TPU:1, one launch (start us, length us, event | category | flops | bytes accessed | tf_op | source)
XLA Modules:
  0.0 44.7 jit_solution(17992513985156870259)
XLA Ops:
  0.6 1.4 %shard_map.50 = (f32[4,32,256]{2,1,0:T(8,128)S(1)}, f32[4,32,256]{2,1,0:T(8,128)S(1)}, f32[4,32,256]{2,1,0:T(8,128)S(1)}, f32[4,32,256]{2,1,0:T(8,128)S(1)}, f32...) custom-call(f32[1,8,128,256]{3,2,1,0:T(8,128)} %kernels_ref.1), custom_call_target="tpu_custom_call" | custom-call | flops 134217728 | bytes 2097152 | tf_op jit(solution)/shard_map/pallas_call | solution.py:307
  2.0 0.0 copy-start
  2.0 0.4 shard_map.51
  2.4 1.5 %collective-permute-start = (f32[3,4,32,256]{3,2,1,0:T(8,128)S(1)}, f32[3,4,32,256]{3,2,1,0:T(8,128)S(1)}, u32[]{:S(2)}, u32[]{:S(2)}) collective-permute-start(f32[3,4,32,256]{3,2,1,0:T(8,128)S(1)} %get-tuple-element.21), channel_id=1, source_target_pairs={{0,1},{1,0},{2,3},{3,2},{4,5},{5,4},{6,7},{7,6},{8,9},{9,8},{10,11... | collective-permute-start | bytes 1179656 | tf_op jit(solution)/shard_map/ppermute | solution.py:288
  3.9 0.1 collective-permute-start.1
  4.0 1.4 %collective-permute-done.1 = f32[4,32,256]{2,1,0:T(8,128)S(1)} collective-permute-done((f32[4,32,256]{2,1,0:T(8,128)S(1)}, f32[4,32,256]{2,1,0:T(8,128)S(1)}, u32[]{:S(2)}, u32[]{:S(2)}) %collective-permute-start.1) | collective-permute-done | bytes 131104 | tf_op jit(solution)/shard_map/ppermute | solution.py:288
  5.4 1.4 %collective-permute-start.2 = (f32[4,32,256]{2,1,0:T(8,128)S(1)}, f32[4,32,256]{2,1,0:T(8,128)S(1)}, u32[]{:S(2)}, u32[]{:S(2)}) collective-permute-start(f32[4,32,256]{2,1,0:T(8,128)S(1)} %add.6), channel_id=1, source_target_pairs={{0,2},{2,0},{1,3},{3,1},{4,6},{6,4},{5,7},{7,5},{8,10},{10,8},{9,1... | collective-permute-start | bytes 393224 | tf_op jit(solution)/shard_map/ppermute | solution.py:288
  6.8 0.0 collective-permute-done.rest_ref
  6.8 0.2 collective-permute-start.5
  7.1 3.1 %collective-permute-done.2.chip_ref = f32[4,32,256]{2,1,0:T(8,128)S(1)} collective-permute-done((f32[4,32,256]{2,1,0:T(8,128)S(1)}, f32[4,32,256]{2,1,0:T(8,128)S(1)}, u32[]{:S(2)}, u32[]{:S(2)}) %collective-permute-start.2) | collective-permute-done | bytes 131104 | tf_op jit(solution)/shard_map/ppermute | solution.py:288
  10.2 0.2 shard_map.52
  10.4 3.2 %collective-permute-start.4 = (f32[4,32,256]{2,1,0:T(8,128)S(1)}, f32[4,32,256]{2,1,0:T(8,128)S(1)}, u32[]{:S(2)}, u32[]{:S(2)}) collective-permute-start(f32[4,32,256]{2,1,0:T(8,128)S(1)} %shard_map.52), channel_id=1, source_target_pairs={{0,2},{1,3},{2,0},{3,1},{4,4},{5,5},{6,6},{7,7},{8,8},{9,9},{10,10... | collective-permute-start | bytes 393224 | tf_op jit(solution)/shard_map/ppermute | solution.py:348
  13.7 6.0 %collective-permute-start.3 = (f32[4,32,256]{2,1,0:T(8,128)S(1)}, f32[4,32,256]{2,1,0:T(8,128)S(1)}, u32[]{:S(2)}, u32[]{:S(2)}) collective-permute-start(f32[4,32,256]{2,1,0:T(8,128)S(1)} %shard_map.52), channel_id=1, source_target_pairs={{0,126},{1,127},{2,124},{3,125},{4,8},{5,9},{6,10},{7,11},{8,4},{9... | collective-permute-start | bytes 393224 | tf_op jit(solution)/shard_map/ppermute | solution.py:347
  19.7 0.0 collective-permute-done.5.chip_ref
  19.7 0.2 shard_map.53.near_ref
  19.9 0.1 collective-permute-start.6
  20.0 0.0 copy-done
  20.0 3.4 %shard_map.54 = (f32[8,8,32,256]{3,2,1,0:T(8,128)S(1)}, f32[8,128]{1,0:T(8,128)S(1)}) custom-call(f32[8,8,32,256]{3,2,1,0:T(8,128)S(1)} %copy-done, f32[8,8,32,256]{3,2,1,0:T(8,128)} %curvature_hbm.1), custom_call_target="tpu_custom_call" | custom-call | flops 13107200 | bytes 6291456 | tf_op jit(solution)/shard_map/pallas_call | solution.py:329
  23.5 0.0 collective-permute-done.4.far_ref
  23.5 0.0 collective-permute-done.3.far_halo_ref
  23.5 0.6 %collective-permute-done.6.near_halo_ref = f32[4,32,256]{2,1,0:T(8,128)S(1)} collective-permute-done((f32[4,32,256]{2,1,0:T(8,128)S(1)}, f32[4,32,256]{2,1,0:T(8,128)S(1)}, u32[]{:S(2)}, u32[]{:S(2)}) %collective-permute-start.6) | collective-permute-done | bytes 131104 | tf_op jit(solution)/shard_map/ppermute | solution.py:354
  24.1 0.8 %shard_map.55 = (f32[8,32,256]{2,1,0:T(8,128)S(1)}, f32[128,1,128]{2,1,0:T(1,128)S(1)}) custom-call(f32[4,32,256]{2,1,0:T(8,128)S(1)} %collective-permute-done.3.far_halo_ref, f32[4,32,256]{2,1,0:T(8,128)S(1)} %collective-permute-done.4.far_ref, f32[4,32,256]{2,1,0:T(8,128)S(1)} %shard_map.53.near_ref, ...), custom_call_target="tpu_custom_call" | custom-call | flops 3932160 | bytes 5242880 | tf_op jit(solution)/shard_map/pallas_call | solution.py:355
  24.9 18.6 %all_to_all.5.rows_ref = f32[128,1,128]{2,1,0:T(1,128)S(1)} all-to-all(f32[128,1,128]{2,1,0:T(1,128)S(1)} %get-tuple-element.30), channel_id=1, replica_groups=mesh['cuts_0'=2,'cuts_1'=4,'cuts_2'=4,'event_0'=2,'event_1'=2] {'cuts_0'..., dimensions={0} | all-to-all | bytes 131072 | tf_op jit(solution)/shard_map/all_to_all | solution.py:362
  43.5 1.2 %shard_map.56 = (f32[8,32,256]{2,1,0:T(8,128)}, f32[8,32,256]{2,1,0:T(8,128)}) custom-call(f32[128,1,128]{2,1,0:T(1,128)S(1)} %all_to_all.5.rows_ref, f32[8,32,256]{2,1,0:T(8,128)S(1)} %get-tuple-element.31.gradient_ref, f32[8,8,32,256]{3,2,1,0:T(8,128)S(1)} %copy-done, f32[8,8,32,256]{3,2,1,0:T(8,128)S(1)} %get-tuple-element.28.changes_ref), custom_call_target="tpu_custom_call" | custom-call | flops 2228224 | bytes 4718592 | tf_op jit(solution)/shard_map/pallas_call | solution.py:363
  (2 shorter events, 0.0 us)
Async XLA Ops:
  2.0 18.0 %copy-start = (f32[8,8,32,256]{3,2,1,0:T(8,128)S(1)}, f32[8,8,32,256]{3,2,1,0:T(8,128)}, u32[]{:S(2)}) copy-start(f32[8,8,32,256]{3,2,1,0:T(8,128)} %steps_ref.5) | copy-start | bytes 6291460
  2.4 4.4 %collective-permute-start = (f32[3,4,32,256]{3,2,1,0:T(8,128)S(1)}, f32[3,4,32,256]{3,2,1,0:T(8,128)S(1)}, u32[]{:S(2)}, u32[]{:S(2)}) collective-permute-start(f32[3,4,32,256]{3,2,1,0:T(8,128)S(1)} %get-tuple-element.21), channel_id=1, source_target_pairs={{0,1},{1,0},{2,3},{3,2},{4,5},{5,4},{6,7},{7,6},{8,9},{9,8},{10,11... | collective-permute-start | bytes 1179656 | tf_op jit(solution)/shard_map/ppermute | solution.py:288
  3.9 1.5 %collective-permute-start.1 = (f32[4,32,256]{2,1,0:T(8,128)S(1)}, f32[4,32,256]{2,1,0:T(8,128)S(1)}, u32[]{:S(2)}, u32[]{:S(2)}) collective-permute-start(f32[4,32,256]{2,1,0:T(8,128)S(1)} %get-tuple-element.23), channel_id=1, source_target_pairs={{0,1},{1,0},{2,3},{3,2},{4,5},{5,4},{6,7},{7,6},{8,9},{9,8},{10,11... | collective-permute-start | bytes 393224 | tf_op jit(solution)/shard_map/ppermute | solution.py:288
  5.4 4.8 %collective-permute-start.2 = (f32[4,32,256]{2,1,0:T(8,128)S(1)}, f32[4,32,256]{2,1,0:T(8,128)S(1)}, u32[]{:S(2)}, u32[]{:S(2)}) collective-permute-start(f32[4,32,256]{2,1,0:T(8,128)S(1)} %add.6), channel_id=1, source_target_pairs={{0,2},{2,0},{1,3},{3,1},{4,6},{6,4},{5,7},{7,5},{8,10},{10,8},{9,1... | collective-permute-start | bytes 393224 | tf_op jit(solution)/shard_map/ppermute | solution.py:288
  6.8 12.8 %collective-permute-start.5 = (f32[4,32,256]{2,1,0:T(8,128)S(1)}, f32[4,32,256]{2,1,0:T(8,128)S(1)}, u32[]{:S(2)}, u32[]{:S(2)}) collective-permute-start(f32[4,32,256]{2,1,0:T(8,128)S(1)} %fusion), channel_id=1, source_target_pairs={{0,2},{2,0},{1,3},{3,1},{4,6},{6,4},{5,7},{7,5},{8,10},{10,8},{9,1... | collective-permute-start | bytes 393224 | tf_op jit(solution)/shard_map/ppermute | solution.py:288
  10.4 13.1 %collective-permute-start.4 = (f32[4,32,256]{2,1,0:T(8,128)S(1)}, f32[4,32,256]{2,1,0:T(8,128)S(1)}, u32[]{:S(2)}, u32[]{:S(2)}) collective-permute-start(f32[4,32,256]{2,1,0:T(8,128)S(1)} %shard_map.52), channel_id=1, source_target_pairs={{0,2},{1,3},{2,0},{3,1},{4,4},{5,5},{6,6},{7,7},{8,8},{9,9},{10,10... | collective-permute-start | bytes 393224 | tf_op jit(solution)/shard_map/ppermute | solution.py:348
  13.7 9.8 %collective-permute-start.3 = (f32[4,32,256]{2,1,0:T(8,128)S(1)}, f32[4,32,256]{2,1,0:T(8,128)S(1)}, u32[]{:S(2)}, u32[]{:S(2)}) collective-permute-start(f32[4,32,256]{2,1,0:T(8,128)S(1)} %shard_map.52), channel_id=1, source_target_pairs={{0,126},{1,127},{2,124},{3,125},{4,8},{5,9},{6,10},{7,11},{8,4},{9... | collective-permute-start | bytes 393224 | tf_op jit(solution)/shard_map/ppermute | solution.py:347
  19.9 4.2 %collective-permute-start.6 = (f32[4,32,256]{2,1,0:T(8,128)S(1)}, f32[4,32,256]{2,1,0:T(8,128)S(1)}, u32[]{:S(2)}, u32[]{:S(2)}) collective-permute-start(f32[4,32,256]{2,1,0:T(8,128)S(1)} %shard_map.53.near_ref), channel_id=1, source_target_pairs={{0,4},{4,0},{8,12},{12,8},{16,20},{20,16},{24,28},{28,24},{32,36},... | collective-permute-start | bytes 393224 | tf_op jit(solution)/shard_map/ppermute | solution.py:354

commit v12 on v11

--- a/solution.py
+++ b/solution.py
@@ -139,8 +139,20 @@
     return row
 
 
-def gram_kernel(steps_ref, curvature_hbm, changes_ref, row_ref, curvature_ref, semaphores):
-    lons, rows, lats = steps_ref.shape[1:]
+def spots(shape):
+    return [
+        (slice(8 * r, 8 * r + 8), slice(LANES * b, LANES * (b + 1)))
+        for r in range(shape[0] // 8)
+        for b in range(shape[1] // LANES)
+    ]
+
+
+def summed_over(lons, step, size):
+    return lax.fori_loop(0, lons, step, [jnp.zeros((8, LANES), jnp.float32)] * size)
+
+
+def first_gram_kernel(steps_ref, curvature_hbm, changes_ref, row_ref, curvature_ref, semaphores):
+    lons, *plane = steps_ref.shape[1:]
 
     def fetch(a):
         return pltpu.make_async_copy(
@@ -149,45 +161,43 @@
 
     for a in range(lons):
         fetch(a).start()
-    spots = [
-        (slice(8 * r, 8 * r + 8), slice(LANES * b, LANES * (b + 1)))
-        for r in range(rows // 8)
-        for b in range(lats // LANES)
-    ]
     half = PAIRS // 2
-    upper = [(i, j) for i in range(PAIRS) for j in range(i, PAIRS)]
-
-    def first(a, sums):
+
+    def step(a, sums):
         fetch(a).wait()
-        for at in spots:
+        for at in spots(plane):
             steps = [steps_ref[(i, a, *at)] for i in range(half)]
             changes = [None] * PAIRS
             for i in range(PAIRS):
-                step = steps[i] if i < half else steps_ref[(i, a, *at)]
-                changes[i] = curvature_ref[(i, a, *at)] * step
+                value = steps[i] if i < half else steps_ref[(i, a, *at)]
+                changes[i] = curvature_ref[(i, a, *at)] * value
                 changes_ref[(i, a, *at)] = changes[i]
             sums = [sums[k] + steps[k // PAIRS] * changes[k % PAIRS] for k in range(half * PAIRS)]
         return sums
 
-    def second(a, sums):
-        for at in spots:
+    row_ref[...] = placed(enumerate(summed_over(lons, step, half * PAIRS)))
+
+
+def second_gram_kernel(steps_ref, changes_ref, first_ref, row_ref):
+    lons, *plane = steps_ref.shape[1:]
+    half = PAIRS // 2
+    upper = [(i, j) for i in range(PAIRS) for j in range(i, PAIRS)]
+
+    def mixed(a, sums):
+        for at in spots(plane):
             steps = [steps_ref[(i, a, *at)] for i in range(half, PAIRS)]
             changes = [changes_ref[(i, a, *at)] for i in range(PAIRS)]
             sums = [sums[k] + steps[k // PAIRS] * changes[k % PAIRS] for k in range(half * PAIRS)]
         return sums
 
-    def third(a, sums):
-        for at in spots:
+    def squares(a, sums):
+        for at in spots(plane):
             changes = [changes_ref[(i, a, *at)] for i in range(PAIRS)]
             sums = [value + changes[i] * changes[j] for value, (i, j) in zip(sums, upper)]
         return sums
 
-    zero = jnp.zeros((8, LANES), jnp.float32)
-    row = zero
-    for start, step, size in ((0, first, 32), (32, second, 32), (SQUARES, third, len(upper))):
-        sums = lax.fori_loop(0, lons, step, [zero] * size)
-        row = row + placed([(start + k, value) for k, value in enumerate(sums)])
-    row_ref[...] = row
+    row = first_ref[...] + placed(enumerate(summed_over(lons, mixed, half * PAIRS), half * PAIRS))
+    row_ref[...] = row + placed(enumerate(summed_over(lons, squares, len(upper)), SQUARES))
 
 
 def product_kernel(
@@ -326,14 +336,18 @@
     far_chip = swapped(far_pass + far_core_pass, "event_0")
     rest = swapped(rest, "event_1")
     near_chip = swapped(near_pass + rest[0], "event_0")
-    changes, gram = call(
-        gram_kernel,
-        [(steps.shape, jnp.float32), ((8, LANES), jnp.float32)],
-        2 * 100 * size,
+    row = ((8, LANES), jnp.float32)
+    changes, first_row = call(
+        first_gram_kernel,
+        [(steps.shape, jnp.float32), row],
+        2 * 40 * size,
         12 * steps.size,
         in_specs=[pl.BlockSpec(memory_space=pltpu.VMEM), pl.BlockSpec(memory_space=pltpu.HBM)],
         scratch_shapes=[pltpu.VMEM(curvature.shape, jnp.float32), pltpu.SemaphoreType.DMA((lons,))],
     )(steps, in_hbm(curvature))
+    (gram,) = call(second_gram_kernel, [row], 2 * 68 * size, 8 * steps.size)(
+        steps, changes, first_row
+    )
 
     def plane_of(slot, *parts):
         kernel = functools.partial(latitude_kernel, slot)

time: 44.9 us -> 44.9 us (level)
    pallas_call x1 -> x2, Pallas kernels: 3.43 us -> 3.43 us  [the longest x1 1.88 us: shards(): call(first_gram_kernel, [(steps.shape, jnp.float32), row], 2 * 40 * size,...]
where the time goes in v12:
time: 44.9 us; the launch traced here: 44.7 us
  blocking collectives  18.6 us (41%)
  starting transfers between devices  12.5 us (28%)
  Pallas kernels  7.64 us (17%)
  waiting for transfers between devices  5.19 us (12%)
  between operations  0.74 us (2%)
    all_to_all x1, blocking collectives, shards(): arrived = lax.all_to_all(outgoing, CUTS_EVENT, 0, 0, tiled=True)  18.6 us
    ppermute x1, starting transfers between devices, shards(): far_halo = lax.ppermute(far_plane, CUTS_EVENT, pairs)  6.03 us
    ppermute x4, waiting for transfers between devices, swapped(): return lax.ppermute(x, axis, [(0, 1), (1, 0)])  4.56 us
    ppermute x1, starting transfers between devices, shards(): lax.ppermute(far_plane, CUTS_EVENT, [(e, e ^ 2) for e in range(events)] +...  3.23 us
    ppermute x4, starting transfers between devices, swapped(): return lax.ppermute(x, axis, [(0, 1), (1, 0)])  3.18 us
    pallas_call x1, Pallas kernels, shards(): call(first_gram_kernel, [(steps.shape, jnp.float32), row], 2 * 40 * size,...  1.88 us
    pallas_call x1, Pallas kernels, shards(): call(second_gram_kernel, [row], 2 * 68 * size, 8 * steps.size)  1.55 us
    pallas_call x1, Pallas kernels, shards(): call(far_radial_kernel, [half] * 4 + [((RIM, rad_len, lats), jnp.float32)...  1.39 us
  transfers between devices with their start and end apart: 7, of which 3 were waited for; matrix products, arithmetic and copies ran while one was open for 0% of the time, Pallas kernels for 9%

profile of v12, /device:TPU:1, one launch (start us, length us, event | category | flops | bytes accessed | tf_op | source)
XLA Modules:
  0.0 44.7 jit_solution(2912401685269938971)
XLA Ops:
  0.6 1.4 %shard_map.50 = (f32[4,32,256]{2,1,0:T(8,128)S(1)}, f32[4,32,256]{2,1,0:T(8,128)S(1)}, f32[4,32,256]{2,1,0:T(8,128)S(1)}, f32[4,32,256]{2,1,0:T(8,128)S(1)}, f32...) custom-call(f32[1,8,128,256]{3,2,1,0:T(8,128)} %kernels_ref.1), custom_call_target="tpu_custom_call" | custom-call | flops 134217728 | bytes 2097152 | tf_op jit(solution)/shard_map/pallas_call | solution.py:317
  2.0 0.0 copy-start
  2.0 0.4 shard_map.51
  2.4 1.5 %collective-permute-start = (f32[3,4,32,256]{3,2,1,0:T(8,128)S(1)}, f32[3,4,32,256]{3,2,1,0:T(8,128)S(1)}, u32[]{:S(2)}, u32[]{:S(2)}) collective-permute-start(f32[3,4,32,256]{3,2,1,0:T(8,128)S(1)} %get-tuple-element.21), channel_id=1, source_target_pairs={{0,1},{1,0},{2,3},{3,2},{4,5},{5,4},{6,7},{7,6},{8,9},{9,8},{10,11... | collective-permute-start | bytes 1179656 | tf_op jit(solution)/shard_map/ppermute | solution.py:298
  3.9 0.1 collective-permute-start.1
  4.0 1.4 %collective-permute-done.1 = f32[4,32,256]{2,1,0:T(8,128)S(1)} collective-permute-done((f32[4,32,256]{2,1,0:T(8,128)S(1)}, f32[4,32,256]{2,1,0:T(8,128)S(1)}, u32[]{:S(2)}, u32[]{:S(2)}) %collective-permute-start.1) | collective-permute-done | bytes 131104 | tf_op jit(solution)/shard_map/ppermute | solution.py:298
  5.4 1.4 %collective-permute-start.2 = (f32[4,32,256]{2,1,0:T(8,128)S(1)}, f32[4,32,256]{2,1,0:T(8,128)S(1)}, u32[]{:S(2)}, u32[]{:S(2)}) collective-permute-start(f32[4,32,256]{2,1,0:T(8,128)S(1)} %add.6), channel_id=1, source_target_pairs={{0,2},{2,0},{1,3},{3,1},{4,6},{6,4},{5,7},{7,5},{8,10},{10,8},{9,1... | collective-permute-start | bytes 393224 | tf_op jit(solution)/shard_map/ppermute | solution.py:298
  6.8 0.0 collective-permute-done.rest_ref
  6.8 0.2 collective-permute-start.5
  7.1 3.1 %collective-permute-done.2.chip_ref = f32[4,32,256]{2,1,0:T(8,128)S(1)} collective-permute-done((f32[4,32,256]{2,1,0:T(8,128)S(1)}, f32[4,32,256]{2,1,0:T(8,128)S(1)}, u32[]{:S(2)}, u32[]{:S(2)}) %collective-permute-start.2) | collective-permute-done | bytes 131104 | tf_op jit(solution)/shard_map/ppermute | solution.py:298
  10.2 0.2 shard_map.52
  10.4 3.2 %collective-permute-start.4 = (f32[4,32,256]{2,1,0:T(8,128)S(1)}, f32[4,32,256]{2,1,0:T(8,128)S(1)}, u32[]{:S(2)}, u32[]{:S(2)}) collective-permute-start(f32[4,32,256]{2,1,0:T(8,128)S(1)} %shard_map.52), channel_id=1, source_target_pairs={{0,2},{1,3},{2,0},{3,1},{4,4},{5,5},{6,6},{7,7},{8,8},{9,9},{10,10... | collective-permute-start | bytes 393224 | tf_op jit(solution)/shard_map/ppermute | solution.py:362
  13.7 6.0 %collective-permute-start.3 = (f32[4,32,256]{2,1,0:T(8,128)S(1)}, f32[4,32,256]{2,1,0:T(8,128)S(1)}, u32[]{:S(2)}, u32[]{:S(2)}) collective-permute-start(f32[4,32,256]{2,1,0:T(8,128)S(1)} %shard_map.52), channel_id=1, source_target_pairs={{0,126},{1,127},{2,124},{3,125},{4,8},{5,9},{6,10},{7,11},{8,4},{9... | collective-permute-start | bytes 393224 | tf_op jit(solution)/shard_map/ppermute | solution.py:361
  19.7 0.0 collective-permute-done.5.chip_ref
  19.7 0.2 shard_map.53.near_ref
  19.9 0.1 collective-permute-start.6
  20.0 0.0 copy-done
  20.0 1.9 %shard_map.54 = (f32[8,8,32,256]{3,2,1,0:T(8,128)S(1)}, f32[8,128]{1,0:T(8,128)S(1)}) custom-call(f32[8,8,32,256]{3,2,1,0:T(8,128)S(1)} %copy-done, f32[8,8,32,256]{3,2,1,0:T(8,128)} %curvature_hbm.1), custom_call_target="tpu_custom_call" | custom-call | flops 5242880 | bytes 6291456 | tf_op jit(solution)/shard_map/pallas_call | solution.py:340
  21.9 1.6 %shard_map.55.gram_ref = f32[8,128]{1,0:T(8,128)S(1)} custom-call(f32[8,8,32,256]{3,2,1,0:T(8,128)S(1)} %copy-done, f32[8,8,32,256]{3,2,1,0:T(8,128)S(1)} %get-tuple-element.28.changes_ref, f32[8,128]{1,0:T(8,128)S(1)} %get-tuple-element.29.first_ref), custom_call_target="tpu_custom_call" | custom-call | flops 8912896 | bytes 4194304 | tf_op jit(solution)/shard_map/pallas_call | solution.py:348
  23.5 0.0 collective-permute-done.4.far_ref
  23.5 0.0 collective-permute-done.3.far_halo_ref
  23.5 0.6 %collective-permute-done.6.near_halo_ref = f32[4,32,256]{2,1,0:T(8,128)S(1)} collective-permute-done((f32[4,32,256]{2,1,0:T(8,128)S(1)}, f32[4,32,256]{2,1,0:T(8,128)S(1)}, u32[]{:S(2)}, u32[]{:S(2)}) %collective-permute-start.6) | collective-permute-done | bytes 131104 | tf_op jit(solution)/shard_map/ppermute | solution.py:368
  24.1 0.8 %shard_map.56 = (f32[8,32,256]{2,1,0:T(8,128)S(1)}, f32[128,1,128]{2,1,0:T(1,128)S(1)}) custom-call(f32[4,32,256]{2,1,0:T(8,128)S(1)} %collective-permute-done.3.far_halo_ref, f32[4,32,256]{2,1,0:T(8,128)S(1)} %collective-permute-done.4.far_ref, f32[4,32,256]{2,1,0:T(8,128)S(1)} %shard_map.53.near_ref, ...), custom_call_target="tpu_custom_call" | custom-call | flops 3932160 | bytes 5242880 | tf_op jit(solution)/shard_map/pallas_call | solution.py:369
  24.9 18.6 %all_to_all.5.rows_ref = f32[128,1,128]{2,1,0:T(1,128)S(1)} all-to-all(f32[128,1,128]{2,1,0:T(1,128)S(1)} %get-tuple-element.30), channel_id=1, replica_groups=mesh['cuts_0'=2,'cuts_1'=4,'cuts_2'=4,'event_0'=2,'event_1'=2] {'cuts_0'..., dimensions={0} | all-to-all | bytes 131072 | tf_op jit(solution)/shard_map/all_to_all | solution.py:376
  43.5 1.2 %shard_map.57 = (f32[8,32,256]{2,1,0:T(8,128)}, f32[8,32,256]{2,1,0:T(8,128)}) custom-call(f32[128,1,128]{2,1,0:T(1,128)S(1)} %all_to_all.5.rows_ref, f32[8,32,256]{2,1,0:T(8,128)S(1)} %get-tuple-element.31.gradient_ref, f32[8,8,32,256]{3,2,1,0:T(8,128)S(1)} %copy-done, f32[8,8,32,256]{3,2,1,0:T(8,128)S(1)} %get-tuple-element.28.changes_ref), custom_call_target="tpu_custom_call" | custom-call | flops 2228224 | bytes 4718592 | tf_op jit(solution)/shard_map/pallas_call | solution.py:377
  (2 shorter events, 0.0 us)
Async XLA Ops:
  2.0 18.0 %copy-start = (f32[8,8,32,256]{3,2,1,0:T(8,128)S(1)}, f32[8,8,32,256]{3,2,1,0:T(8,128)}, u32[]{:S(2)}) copy-start(f32[8,8,32,256]{3,2,1,0:T(8,128)} %steps_ref.7) | copy-start | bytes 6291460
  2.4 4.4 %collective-permute-start = (f32[3,4,32,256]{3,2,1,0:T(8,128)S(1)}, f32[3,4,32,256]{3,2,1,0:T(8,128)S(1)}, u32[]{:S(2)}, u32[]{:S(2)}) collective-permute-start(f32[3,4,32,256]{3,2,1,0:T(8,128)S(1)} %get-tuple-element.21), channel_id=1, source_target_pairs={{0,1},{1,0},{2,3},{3,2},{4,5},{5,4},{6,7},{7,6},{8,9},{9,8},{10,11... | collective-permute-start | bytes 1179656 | tf_op jit(solution)/shard_map/ppermute | solution.py:298
  3.9 1.5 %collective-permute-start.1 = (f32[4,32,256]{2,1,0:T(8,128)S(1)}, f32[4,32,256]{2,1,0:T(8,128)S(1)}, u32[]{:S(2)}, u32[]{:S(2)}) collective-permute-start(f32[4,32,256]{2,1,0:T(8,128)S(1)} %get-tuple-element.23), channel_id=1, source_target_pairs={{0,1},{1,0},{2,3},{3,2},{4,5},{5,4},{6,7},{7,6},{8,9},{9,8},{10,11... | collective-permute-start | bytes 393224 | tf_op jit(solution)/shard_map/ppermute | solution.py:298
  5.4 4.8 %collective-permute-start.2 = (f32[4,32,256]{2,1,0:T(8,128)S(1)}, f32[4,32,256]{2,1,0:T(8,128)S(1)}, u32[]{:S(2)}, u32[]{:S(2)}) collective-permute-start(f32[4,32,256]{2,1,0:T(8,128)S(1)} %add.6), channel_id=1, source_target_pairs={{0,2},{2,0},{1,3},{3,1},{4,6},{6,4},{5,7},{7,5},{8,10},{10,8},{9,1... | collective-permute-start | bytes 393224 | tf_op jit(solution)/shard_map/ppermute | solution.py:298
  6.8 12.8 %collective-permute-start.5 = (f32[4,32,256]{2,1,0:T(8,128)S(1)}, f32[4,32,256]{2,1,0:T(8,128)S(1)}, u32[]{:S(2)}, u32[]{:S(2)}) collective-permute-start(f32[4,32,256]{2,1,0:T(8,128)S(1)} %fusion), channel_id=1, source_target_pairs={{0,2},{2,0},{1,3},{3,1},{4,6},{6,4},{5,7},{7,5},{8,10},{10,8},{9,1... | collective-permute-start | bytes 393224 | tf_op jit(solution)/shard_map/ppermute | solution.py:298
  10.4 13.1 %collective-permute-start.4 = (f32[4,32,256]{2,1,0:T(8,128)S(1)}, f32[4,32,256]{2,1,0:T(8,128)S(1)}, u32[]{:S(2)}, u32[]{:S(2)}) collective-permute-start(f32[4,32,256]{2,1,0:T(8,128)S(1)} %shard_map.52), channel_id=1, source_target_pairs={{0,2},{1,3},{2,0},{3,1},{4,4},{5,5},{6,6},{7,7},{8,8},{9,9},{10,10... | collective-permute-start | bytes 393224 | tf_op jit(solution)/shard_map/ppermute | solution.py:362
  13.7 9.8 %collective-permute-start.3 = (f32[4,32,256]{2,1,0:T(8,128)S(1)}, f32[4,32,256]{2,1,0:T(8,128)S(1)}, u32[]{:S(2)}, u32[]{:S(2)}) collective-permute-start(f32[4,32,256]{2,1,0:T(8,128)S(1)} %shard_map.52), channel_id=1, source_target_pairs={{0,126},{1,127},{2,124},{3,125},{4,8},{5,9},{6,10},{7,11},{8,4},{9... | collective-permute-start | bytes 393224 | tf_op jit(solution)/shard_map/ppermute | solution.py:361
  19.9 4.2 %collective-permute-start.6 = (f32[4,32,256]{2,1,0:T(8,128)S(1)}, f32[4,32,256]{2,1,0:T(8,128)S(1)}, u32[]{:S(2)}, u32[]{:S(2)}) collective-permute-start(f32[4,32,256]{2,1,0:T(8,128)S(1)} %shard_map.53.near_ref), channel_id=1, source_target_pairs={{0,4},{4,0},{8,12},{12,8},{16,20},{20,16},{24,28},{28,24},{32,36},... | collective-permute-start | bytes 393224 | tf_op jit(solution)/shard_map/ppermute | solution.py:368

commit v13 on v12

--- a/solution.py
+++ b/solution.py
@@ -151,20 +151,26 @@
     return lax.fori_loop(0, lons, step, [jnp.zeros((8, LANES), jnp.float32)] * size)
 
 
-def first_gram_kernel(steps_ref, curvature_hbm, changes_ref, row_ref, curvature_ref, semaphores):
+def first_gram_kernel(
+    steps_hbm, curvature_hbm, steps_ref, changes_ref, row_ref, curvature_ref, semaphores
+):
     lons, *plane = steps_ref.shape[1:]
 
-    def fetch(a):
-        return pltpu.make_async_copy(
-            curvature_hbm.at[:, a], curvature_ref.at[:, a], semaphores.at[a]
-        )
+    def fetches(a):
+        pairs = ((steps_hbm, steps_ref), (curvature_hbm, curvature_ref))
+        return [
+            pltpu.make_async_copy(source.at[:, a], target.at[:, a], semaphores.at[k, a])
+            for k, (source, target) in enumerate(pairs)
+        ]
 
     for a in range(lons):
-        fetch(a).start()
+        for fetch in fetches(a):
+            fetch.start()
     half = PAIRS // 2
 
     def step(a, sums):
-        fetch(a).wait()
+        for fetch in fetches(a):
+            fetch.wait()
         for at in spots(plane):
             steps = [steps_ref[(i, a, *at)] for i in range(half)]
             changes = [None] * PAIRS
@@ -337,16 +343,19 @@
     rest = swapped(rest, "event_1")
     near_chip = swapped(near_pass + rest[0], "event_0")
     row = ((8, LANES), jnp.float32)
-    changes, first_row = call(
+    held_steps, changes, first_row = call(
         first_gram_kernel,
-        [(steps.shape, jnp.float32), row],
+        [(steps.shape, jnp.float32)] * 2 + [row],
         2 * 40 * size,
-        12 * steps.size,
-        in_specs=[pl.BlockSpec(memory_space=pltpu.VMEM), pl.BlockSpec(memory_space=pltpu.HBM)],
-        scratch_shapes=[pltpu.VMEM(curvature.shape, jnp.float32), pltpu.SemaphoreType.DMA((lons,))],
-    )(steps, in_hbm(curvature))
+        16 * steps.size,
+        in_specs=[pl.BlockSpec(memory_space=pltpu.HBM)] * 2,
+        scratch_shapes=[
+            pltpu.VMEM(curvature.shape, jnp.float32),
+            pltpu.SemaphoreType.DMA((2, lons)),
+        ],
+    )(in_hbm(steps), in_hbm(curvature))
     (gram,) = call(second_gram_kernel, [row], 2 * 68 * size, 8 * steps.size)(
-        steps, changes, first_row
+        held_steps, changes, first_row
     )
 
     def plane_of(slot, *parts):
@@ -372,7 +381,7 @@
         2 * 30 * size,
         4 * 20 * size,
         scratch_shapes=[pltpu.VMEM((4, RIM, rows, lats), jnp.float32)],
-    )(far_halo, far_plane, near_plane, near_halo, steps, changes, gram)
+    )(far_halo, far_plane, near_plane, near_halo, held_steps, changes, gram)
     arrived = lax.all_to_all(outgoing, CUTS_EVENT, 0, 0, tiled=True)
     return call(
         direction_kernel,
@@ -381,7 +390,7 @@
         4 * 18 * size,
         out_specs=[pl.BlockSpec(memory_space=pltpu.HBM)] * 2,
         scratch_shapes=[pltpu.VMEM((lons, rows, lats), jnp.float32), pltpu.SemaphoreType.DMA((5,))],
-    )(arrived, gradient, steps, changes)
+    )(arrived, gradient, held_steps, changes)
 
 
 def solution(mesh):

time: 44.9 us -> 44.9 us (level)
  Pallas kernels: 7.64 us -> 8.24 us
  waiting for transfers between devices: 5.19 us -> 4.59 us
    pallas_call x1, Pallas kernels: 1.88 us -> 2.49 us  [shards(): call(first_gram_kernel, [(steps.shape, jnp.float32)] * 2 + [row], 2 * 40...]
    ppermute x1, waiting for transfers between devices: 0.62 us -> 0.03 us  [shards(): lax.ppermute(near_plane, CUTS, [(c, c ^ 1) for c in range(cuts)])]
  transfers between devices with their start and end apart: 7 -> 7, of which waited for: 3 -> 2; matrix products, arithmetic and copies ran while one was open for 0% -> 0% of each run, Pallas kernels for 9% -> 10%
where the time goes in v13:
time: 44.9 us; the launch traced here: 44.7 us
  blocking collectives  18.6 us (41%)
  starting transfers between devices  12.5 us (28%)
  Pallas kernels  8.24 us (18%)
  waiting for transfers between devices  4.59 us (10%)
  between operations  0.72 us (2%)
    all_to_all x1, blocking collectives, shards(): arrived = lax.all_to_all(outgoing, CUTS_EVENT, 0, 0, tiled=True)  18.6 us
    ppermute x1, starting transfers between devices, shards(): far_halo = lax.ppermute(far_plane, CUTS_EVENT, pairs)  6.04 us
    ppermute x4, waiting for transfers between devices, swapped(): return lax.ppermute(x, axis, [(0, 1), (1, 0)])  4.56 us
    ppermute x1, starting transfers between devices, shards(): lax.ppermute(far_plane, CUTS_EVENT, [(e, e ^ 2) for e in range(events)] +...  3.23 us
    ppermute x4, starting transfers between devices, swapped(): return lax.ppermute(x, axis, [(0, 1), (1, 0)])  3.18 us
    pallas_call x1, Pallas kernels, shards(): call(first_gram_kernel, [(steps.shape, jnp.float32)] * 2 + [row], 2 * 40...  2.49 us
    pallas_call x1, Pallas kernels, shards(): call(second_gram_kernel, [row], 2 * 68 * size, 8 * steps.size)  1.55 us
    pallas_call x1, Pallas kernels, shards(): call(far_radial_kernel, [half] * 4 + [((RIM, rad_len, lats), jnp.float32)...  1.39 us
  transfers between devices with their start and end apart: 7, of which 2 were waited for; matrix products, arithmetic and copies ran while one was open for 0% of the time, Pallas kernels for 10%

profile of v13, /device:TPU:1, one launch (start us, length us, event | category | flops | bytes accessed | tf_op | source)
XLA Modules:
  0.0 44.7 jit_solution(1595207244583418575)
XLA Ops:
  0.6 1.4 %shard_map.50 = (f32[4,32,256]{2,1,0:T(8,128)S(1)}, f32[4,32,256]{2,1,0:T(8,128)S(1)}, f32[4,32,256]{2,1,0:T(8,128)S(1)}, f32[4,32,256]{2,1,0:T(8,128)S(1)}, f32...) custom-call(f32[1,8,128,256]{3,2,1,0:T(8,128)} %kernels_ref.1), custom_call_target="tpu_custom_call" | custom-call | flops 134217728 | bytes 2097152 | tf_op jit(solution)/shard_map/pallas_call | solution.py:323
  2.0 0.4 shard_map.51
  2.4 1.5 %collective-permute-start = (f32[3,4,32,256]{3,2,1,0:T(8,128)S(1)}, f32[3,4,32,256]{3,2,1,0:T(8,128)S(1)}, u32[]{:S(2)}, u32[]{:S(2)}) collective-permute-start(f32[3,4,32,256]{3,2,1,0:T(8,128)S(1)} %get-tuple-element.22), channel_id=1, source_target_pairs={{0,1},{1,0},{2,3},{3,2},{4,5},{5,4},{6,7},{7,6},{8,9},{9,8},{10,11... | collective-permute-start | bytes 1179656 | tf_op jit(solution)/shard_map/ppermute | solution.py:304
  3.8 0.1 collective-permute-start.1
  3.9 1.4 %collective-permute-done.1 = f32[4,32,256]{2,1,0:T(8,128)S(1)} collective-permute-done((f32[4,32,256]{2,1,0:T(8,128)S(1)}, f32[4,32,256]{2,1,0:T(8,128)S(1)}, u32[]{:S(2)}, u32[]{:S(2)}) %collective-permute-start.1) | collective-permute-done | bytes 131104 | tf_op jit(solution)/shard_map/ppermute | solution.py:304
  5.4 1.4 %collective-permute-start.2 = (f32[4,32,256]{2,1,0:T(8,128)S(1)}, f32[4,32,256]{2,1,0:T(8,128)S(1)}, u32[]{:S(2)}, u32[]{:S(2)}) collective-permute-start(f32[4,32,256]{2,1,0:T(8,128)S(1)} %add.6), channel_id=1, source_target_pairs={{0,2},{2,0},{1,3},{3,1},{4,6},{6,4},{5,7},{7,5},{8,10},{10,8},{9,1... | collective-permute-start | bytes 393224 | tf_op jit(solution)/shard_map/ppermute | solution.py:304
  6.8 0.0 collective-permute-done.rest_ref
  6.8 0.2 collective-permute-start.5
  7.1 3.1 %collective-permute-done.2.chip_ref = f32[4,32,256]{2,1,0:T(8,128)S(1)} collective-permute-done((f32[4,32,256]{2,1,0:T(8,128)S(1)}, f32[4,32,256]{2,1,0:T(8,128)S(1)}, u32[]{:S(2)}, u32[]{:S(2)}) %collective-permute-start.2) | collective-permute-done | bytes 131104 | tf_op jit(solution)/shard_map/ppermute | solution.py:304
  10.2 0.2 shard_map.52
  10.4 3.2 %collective-permute-start.4 = (f32[4,32,256]{2,1,0:T(8,128)S(1)}, f32[4,32,256]{2,1,0:T(8,128)S(1)}, u32[]{:S(2)}, u32[]{:S(2)}) collective-permute-start(f32[4,32,256]{2,1,0:T(8,128)S(1)} %shard_map.52), channel_id=1, source_target_pairs={{0,2},{1,3},{2,0},{3,1},{4,4},{5,5},{6,6},{7,7},{8,8},{9,9},{10,10... | collective-permute-start | bytes 393224 | tf_op jit(solution)/shard_map/ppermute | solution.py:371
  13.6 6.0 %collective-permute-start.3 = (f32[4,32,256]{2,1,0:T(8,128)S(1)}, f32[4,32,256]{2,1,0:T(8,128)S(1)}, u32[]{:S(2)}, u32[]{:S(2)}) collective-permute-start(f32[4,32,256]{2,1,0:T(8,128)S(1)} %shard_map.52), channel_id=1, source_target_pairs={{0,126},{1,127},{2,124},{3,125},{4,8},{5,9},{6,10},{7,11},{8,4},{9... | collective-permute-start | bytes 393224 | tf_op jit(solution)/shard_map/ppermute | solution.py:370
  19.7 0.0 collective-permute-done.5.chip_ref
  19.7 0.2 shard_map.53.near_ref
  19.9 0.1 collective-permute-start.6
  20.0 2.5 %shard_map.54 = (f32[8,8,32,256]{3,2,1,0:T(8,128)S(1)}, f32[8,8,32,256]{3,2,1,0:T(8,128)S(1)}, f32[8,128]{1,0:T(8,128)S(1)}) custom-call(f32[8,8,32,256]{3,2,1,0:T(8,128)} %steps_hbm.1, f32[8,8,32,256]{3,2,1,0:T(8,128)} %curvature_hbm.1), custom_call_target="tpu_custom_call" | custom-call | flops 5242880 | bytes 8388608 | tf_op jit(solution)/shard_map/pallas_call | solution.py:346
  22.5 1.6 %shard_map.55.gram_ref = f32[8,128]{1,0:T(8,128)S(1)} custom-call(f32[8,8,32,256]{3,2,1,0:T(8,128)S(1)} %get-tuple-element.29.steps_ref, f32[8,8,32,256]{3,2,1,0:T(8,128)S(1)} %get-tuple-element.30.changes_ref, f32[8,128]{1,0:T(8,128)S(1)} %get-tuple-element.31.first_ref), custom_call_target="tpu_custom_call" | custom-call | flops 8912896 | bytes 4194304 | tf_op jit(solution)/shard_map/pallas_call | solution.py:357
  24.1 0.0 collective-permute-done.4.far_ref
  24.1 0.0 collective-permute-done.3.far_halo_ref
  24.1 0.0 collective-permute-done.6.near_halo_ref
  24.1 0.8 %shard_map.56 = (f32[8,32,256]{2,1,0:T(8,128)S(1)}, f32[128,1,128]{2,1,0:T(1,128)S(1)}) custom-call(f32[4,32,256]{2,1,0:T(8,128)S(1)} %collective-permute-done.3.far_halo_ref, f32[4,32,256]{2,1,0:T(8,128)S(1)} %collective-permute-done.4.far_ref, f32[4,32,256]{2,1,0:T(8,128)S(1)} %shard_map.53.near_ref, ...), custom_call_target="tpu_custom_call" | custom-call | flops 3932160 | bytes 5242880 | tf_op jit(solution)/shard_map/pallas_call | solution.py:378
  24.9 18.6 %all_to_all.5.rows_ref = f32[128,1,128]{2,1,0:T(1,128)S(1)} all-to-all(f32[128,1,128]{2,1,0:T(1,128)S(1)} %get-tuple-element.32), channel_id=1, replica_groups=mesh['cuts_0'=2,'cuts_1'=4,'cuts_2'=4,'event_0'=2,'event_1'=2] {'cuts_0'..., dimensions={0} | all-to-all | bytes 131072 | tf_op jit(solution)/shard_map/all_to_all | solution.py:385
  43.5 1.2 %shard_map.57 = (f32[8,32,256]{2,1,0:T(8,128)}, f32[8,32,256]{2,1,0:T(8,128)}) custom-call(f32[128,1,128]{2,1,0:T(1,128)S(1)} %all_to_all.5.rows_ref, f32[8,32,256]{2,1,0:T(8,128)S(1)} %get-tuple-element.33.gradient_ref, f32[8,8,32,256]{3,2,1,0:T(8,128)S(1)} %get-tuple-element.29.steps_ref, f32[8,8,32,256]{3,2,1,0:T(8,128)S(1)} %get-tuple-element.30.changes_ref), custom_call_target="tpu_custom_call" | custom-call | flops 2228224 | bytes 4718592 | tf_op jit(solution)/shard_map/pallas_call | solution.py:386
  (2 shorter events, 0.0 us)
Async XLA Ops:
  2.4 4.4 %collective-permute-start = (f32[3,4,32,256]{3,2,1,0:T(8,128)S(1)}, f32[3,4,32,256]{3,2,1,0:T(8,128)S(1)}, u32[]{:S(2)}, u32[]{:S(2)}) collective-permute-start(f32[3,4,32,256]{3,2,1,0:T(8,128)S(1)} %get-tuple-element.22), channel_id=1, source_target_pairs={{0,1},{1,0},{2,3},{3,2},{4,5},{5,4},{6,7},{7,6},{8,9},{9,8},{10,11... | collective-permute-start | bytes 1179656 | tf_op jit(solution)/shard_map/ppermute | solution.py:304
  3.8 1.5 %collective-permute-start.1 = (f32[4,32,256]{2,1,0:T(8,128)S(1)}, f32[4,32,256]{2,1,0:T(8,128)S(1)}, u32[]{:S(2)}, u32[]{:S(2)}) collective-permute-start(f32[4,32,256]{2,1,0:T(8,128)S(1)} %get-tuple-element.24), channel_id=1, source_target_pairs={{0,1},{1,0},{2,3},{3,2},{4,5},{5,4},{6,7},{7,6},{8,9},{9,8},{10,11... | collective-permute-start | bytes 393224 | tf_op jit(solution)/shard_map/ppermute | solution.py:304
  5.4 4.8 %collective-permute-start.2 = (f32[4,32,256]{2,1,0:T(8,128)S(1)}, f32[4,32,256]{2,1,0:T(8,128)S(1)}, u32[]{:S(2)}, u32[]{:S(2)}) collective-permute-start(f32[4,32,256]{2,1,0:T(8,128)S(1)} %add.6), channel_id=1, source_target_pairs={{0,2},{2,0},{1,3},{3,1},{4,6},{6,4},{5,7},{7,5},{8,10},{10,8},{9,1... | collective-permute-start | bytes 393224 | tf_op jit(solution)/shard_map/ppermute | solution.py:304
  6.8 12.8 %collective-permute-start.5 = (f32[4,32,256]{2,1,0:T(8,128)S(1)}, f32[4,32,256]{2,1,0:T(8,128)S(1)}, u32[]{:S(2)}, u32[]{:S(2)}) collective-permute-start(f32[4,32,256]{2,1,0:T(8,128)S(1)} %fusion), channel_id=1, source_target_pairs={{0,2},{2,0},{1,3},{3,1},{4,6},{6,4},{5,7},{7,5},{8,10},{10,8},{9,1... | collective-permute-start | bytes 393224 | tf_op jit(solution)/shard_map/ppermute | solution.py:304
  10.4 13.7 %collective-permute-start.4 = (f32[4,32,256]{2,1,0:T(8,128)S(1)}, f32[4,32,256]{2,1,0:T(8,128)S(1)}, u32[]{:S(2)}, u32[]{:S(2)}) collective-permute-start(f32[4,32,256]{2,1,0:T(8,128)S(1)} %shard_map.52), channel_id=1, source_target_pairs={{0,2},{1,3},{2,0},{3,1},{4,4},{5,5},{6,6},{7,7},{8,8},{9,9},{10,10... | collective-permute-start | bytes 393224 | tf_op jit(solution)/shard_map/ppermute | solution.py:371
  13.6 10.4 %collective-permute-start.3 = (f32[4,32,256]{2,1,0:T(8,128)S(1)}, f32[4,32,256]{2,1,0:T(8,128)S(1)}, u32[]{:S(2)}, u32[]{:S(2)}) collective-permute-start(f32[4,32,256]{2,1,0:T(8,128)S(1)} %shard_map.52), channel_id=1, source_target_pairs={{0,126},{1,127},{2,124},{3,125},{4,8},{5,9},{6,10},{7,11},{8,4},{9... | collective-permute-start | bytes 393224 | tf_op jit(solution)/shard_map/ppermute | solution.py:370
  19.9 4.2 %collective-permute-start.6 = (f32[4,32,256]{2,1,0:T(8,128)S(1)}, f32[4,32,256]{2,1,0:T(8,128)S(1)}, u32[]{:S(2)}, u32[]{:S(2)}) collective-permute-start(f32[4,32,256]{2,1,0:T(8,128)S(1)} %shard_map.53.near_ref), channel_id=1, source_target_pairs={{0,4},{4,0},{8,12},{12,8},{16,20},{20,16},{24,28},{28,24},{32,36},... | collective-permute-start | bytes 393224 | tf_op jit(solution)/shard_map/ppermute | solution.py:377
